TPU v7x, 32 devices: a 4x2x2 block of a 4x4x8 slice. The times are simulated.
32 devices in a mesh: pod: 4 (over y, z), mp: 8 (over x, core).
Axes of the slice: x: 4, y: 2, z: 2, core: 2. Of those that a mesh axis runs over, the one named last changes fastest.
The devices are a block of a 4x4x8 slice.
Arguments:
- d_pool: bfloat16 [65536, 26, 128], P(('pod', 'mp')), parts along dimension 0
- row_ids: int32 [128, 16384, 1], P(('pod', 'mp')), parts along dimension 0
- lengths: int32 [128, 16384], P(('pod', 'mp')), parts along dimension 0
- tables: bfloat16 [128, 16384, 128], P(('pod', 'mp')), parts along dimension 0
- row_accum: float32 [128, 16384], P(('pod', 'mp')), parts along dimension 0
- learn_rate: float32 [], replicated
Outputs:
- output 1: bfloat16 [128, 16384, 128], P(('pod', 'mp')), parts along dimension 0
- output 2: float32 [128, 16384], P(('pod', 'mp')), parts along dimension 0
There are 4 independent parts. A program takes and returns all parts, laid end to end along the dimension named above; an argument that names none is the same for every part.
All inputs are finite; a program needn't handle non-finite values.
Results may differ from a plain program's by a relative error of at most 0.001.
Values are sent between devices in bfloat16 or wider.
A program may use at most 768 MiB of HBM per device.

v0:
```python
import jax
import jax.numpy as jnp
from jax import lax
from jax.sharding import PartitionSpec as P

EPSILON = 1e-06


def scatter_rows(owned_grad, row_ids, lengths, n_rows):
    slots_dev, batch_all, emb_dim = owned_grad.shape
    grad_vals = owned_grad.astype(jnp.float32).reshape(slots_dev * batch_all, emb_dim)
    row_offset = (jnp.arange(slots_dev, dtype=jnp.int32) * n_rows)[:, None]
    dropped = slots_dev * n_rows

    def add_position(pos_idx, row_grad):
        pos_ids = lax.dynamic_index_in_dim(row_ids, pos_idx, axis=2, keepdims=False)
        seg_rows = jnp.where(pos_idx < lengths, pos_ids + row_offset, dropped).reshape(-1)
        return row_grad.at[seg_rows].add(grad_vals, mode='drop')

    row_grad = lax.fori_loop(0, row_ids.shape[2], add_position, jnp.zeros((dropped, emb_dim), jnp.float32))
    return row_grad.reshape(slots_dev, n_rows, emb_dim)


def adagrad_rows(tables, row_accum, row_grad, learn_rate):
    new_accum = row_accum + jnp.mean(row_grad * row_grad, axis=-1)
    row_scale = learn_rate / (jnp.sqrt(new_accum) + EPSILON)
    new_tables = (tables.astype(jnp.float32) - row_grad * row_scale[..., None]).astype(jnp.bfloat16)
    return new_tables, new_accum


def solution(mesh):
    n_group = mesh.shape['mp']
    slot_spec = P(('pod', 'mp'))

    def local_step(d_pool, row_ids, lengths, tables, row_accum, learn_rate):
        n_tab = d_pool.shape[1]
        slots_dev = tables.shape[0]
        padded = jnp.pad(d_pool, ((0, 0), (0, slots_dev * n_group - n_tab), (0, 0)))
        owned_all = lax.all_to_all(padded, 'mp', 1, 0, tiled=True)
        owned_grad = jnp.swapaxes(owned_all, 0, 1)
        row_grad = scatter_rows(owned_grad, row_ids, lengths, tables.shape[1])
        return adagrad_rows(tables, row_accum, row_grad, learn_rate)

    return jax.shard_map(local_step, mesh=mesh, in_specs=(slot_spec, slot_spec, slot_spec, slot_spec, slot_spec, P()), out_specs=(slot_spec, slot_spec), check_vma=False)
```

profile of v0, /device:TPU:81, one launch (start us, length us, event | category | flops | bytes accessed | tf_op | source)
XLA Modules:
  0.0 624.8 jit_solution(6824503859330769324)
XLA Ops:
  0.6 0.0 copy-start
  0.6 0.0 copy-start.1
  0.6 13.9 %pad.4 = bf16[2048,32,128]{2,0,1:T(8,128)(2,1)} pad(bf16[2048,26,128]{2,0,1:T(8,128)(2,1)} %param.6, bf16[]{:T(256)} %constant.18.clone.1), padding=0_0x0_6x0_0 | pad | bytes 30408706 | tf_op jit(solution)/shard_map/jit(_pad)/pad | solution.py:38
  14.5 7.7 %all-to-all-start = ((bf16[2048,32,128]{2,0,1:T(8,128)(2,1)}), bf16[2048,32,128]{2,0,1:T(8,128)(2,1)}, u32[]{:S(2)}, u32[]{:S(2)}) async-start(bf16[2048,32,128]{2,0,1:T(8,128)(2,1)} %pad.4), calls=%async_computation | async-start | bytes 33554432 | tf_op jit(solution)/shard_map/all_to_all | solution.py:39
  22.2 0.0 copy-done
  22.2 0.0 copy-done.1
  22.2 0.2 fusion.3
  22.4 0.3 copy.10
  23.4 0.3 compare_select_fusion
  23.6 182.0 %all-to-all-done = bf16[2048,32,128]{2,0,1:T(8,128)(2,1)} async-done(((bf16[2048,32,128]{2,0,1:T(8,128)(2,1)}), bf16[2048,32,128]{2,0,1:T(8,128)(2,1)}, u32[]{:S(2)}, u32[]{:S(2)}) %all-to-all-start) | async-done | bytes 16777248 | tf_op jit(solution)/shard_map/all_to_all | solution.py:39
  205.7 8.5 %convert_bitcast_fusion = f32[8,2048,4,128]{3,1,2,0:T(8,128)S(1)} fusion(bf16[2048,8,4,128]{3,0,2,1:T(8,128)(2,1)} %bitcast.7), kind=kLoop, calls=%fused_computation.1 | loop fusion | flops 8388608 | bytes 50331648 | tf_op jit(solution)/shard_map/reshape | solution.py:11
  214.2 11.0 %copy.8 = f32[8,2048,4,128]{3,1,0,2:T(8,128)} copy(f32[8,2048,4,128]{3,1,2,0:T(8,128)S(1)} %convert_bitcast_fusion) | data formatting | bytes 67108864 | tf_op jit(solution)/shard_map/reshape | solution.py:11
  225.2 0.0 copy-start.2
  225.2 360.6 %scatter_custom_fusion = f32[65536,128]{1,0:T(8,128)} fusion(s32[65536]{0:T(1024)S(1)} %bitcast.25, f32[65536,128]{1,0:T(8,128)} %bitcast.23, f32[]{:T(128)} %constant.8.clone.1), kind=kCustom, calls=%fused_computation.4 | custom fusion | flops 8388608 | bytes 33554944 | tf_op jit(solution)/shard_map/while/body/eval_jaxpr/scatter-add | solution.py:18
  585.9 15.3 %multiply_reduce_fusion = f32[65536]{0:T(1024)S(1)} fusion(f32[65536,128]{1,0:T(8,128)} %scatter_custom_fusion), kind=kLoop, calls=%fused_computation.3 | loop fusion | flops 16711680 | bytes 33816576 | tf_op jit(solution)/shard_map/reduce_sum | solution.py:25
  601.2 0.1 div.17
  601.3 0.0 copy-done.2
  601.3 0.9 add_divide_fusion
  602.2 22.6 %subtract_convert_fusion = bf16[4,16384,128]{2,1,0:T(8,128)(2,1)} fusion(f32[4,16384,128]{2,1,0:T(8,128)} %bitcast.22, bf16[4,16384,128]{2,1,0:T(8,128)(2,1)} %param.9, f32[4,16384]{1,0:T(4,128)S(1)} %get-tuple-element.16), kind=kLoop, calls=%fused_computation.2 | loop fusion | flops 33554432 | bytes 67371008 | tf_op jit(solution)/shard_map/convert_element_type | solution.py:27
  (2 shorter events, 0.0 us)
Async XLA Ops:
  0.6 21.6 %copy-start = (s32[4,16384,1]{1,2,0:T(1,128)S(1)}, s32[4,16384,1]{1,2,0:T(1,128)}, u32[]{:S(2)}) copy-start(s32[4,16384,1]{1,2,0:T(1,128)} %param.7) | copy-start | bytes 786436
  0.6 21.5 %copy-start.1 = (s32[4,16384]{1,0:T(4,128)S(1)}, s32[4,16384]{1,0:T(4,128)}, u32[]{:S(2)}) copy-start(s32[4,16384]{1,0:T(4,128)} %param.8) | copy-start | bytes 786436
  14.5 191.2 %all-to-all-start = ((bf16[2048,32,128]{2,0,1:T(8,128)(2,1)}), bf16[2048,32,128]{2,0,1:T(8,128)(2,1)}, u32[]{:S(2)}, u32[]{:S(2)}) async-start(bf16[2048,32,128]{2,0,1:T(8,128)(2,1)} %pad.4), calls=%async_computation | async-start | bytes 33554432 | tf_op jit(solution)/shard_map/all_to_all | solution.py:39
  225.2 376.1 %copy-start.2 = (f32[4,16384]{1,0:T(4,128)S(1)}, f32[4,16384]{1,0:T(4,128)}, u32[]{:S(2)}) copy-start(f32[4,16384]{1,0:T(4,128)} %param.10) | copy-start | bytes 786436
where the time goes:
time: 625 us
  other arithmetic  408 us (65%)
  waiting for transfers between devices  182 us (29%)
  local copies, waits for them, and re-layouts  25.3 us (4%)
  starting transfers between devices  7.67 us (1%)
    scatter-add x1, other arithmetic, add_position(): return row_grad.at[seg_rows].add(grad_vals, mode='drop')  361 us
    all_to_all x1, waiting for transfers between devices, local_step(): owned_all = lax.all_to_all(padded, 'mp', 1, 0, tiled=True)  182 us
    convert_element_type x1, other arithmetic, adagrad_rows(): (tables.astype(jnp.float32) - row_grad * row_scale[..., None]).astype(jnp...  22.6 us
    reduce_sum x1, other arithmetic, adagrad_rows(): new_accum = row_accum + jnp.mean(row_grad * row_grad, axis=-1)  15.3 us
    pad x1, local copies, waits for them, and re-layouts, local_step(): padded = jnp.pad(d_pool, ((0, 0), (0, slots_dev * n_group - n_tab), (0, 0)))  13.9 us
  transfers between devices with their start and end apart: 1, of which 1 were waited for; matrix products, arithmetic and copies ran while one was open for 0% of the time, Pallas kernels for 0%

commit v1 on v0

v1 whole, which is shorter than its diff:
```python
import functools

import jax
import jax.numpy as jnp
from jax import lax
from jax.experimental import pallas as pl
from jax.experimental.pallas import tpu as pltpu
from jax.sharding import PartitionSpec as P


EPSILON = 1e-06
BANKS = 4
UNROLL = 8
BLOCK = 128


def update_kernel(slot, n_carried, ids_ref, lr_ref, grad_ref, tables_ref, accums_ref, *refs):
    out_tables_ref, out_accums_ref, *scratch = refs[n_carried:]
    table_ref, accum_ref = tables_ref.at[slot], accums_ref.at[slot]
    out_table_ref, out_accum_ref = out_tables_ref.at[slot], out_accums_ref.at[slot]
    banks = scratch[:BANKS]
    stage, table_v, accum_v, table_o, accum_o, grad_v, sem = scratch[BANKS:]
    segs, seg_rows, dim = grad_ref.shape
    n_rows = table_ref.shape[0]
    grad_copy = pltpu.make_async_copy(grad_ref, grad_v, sem.at[0])
    table_copy = pltpu.make_async_copy(table_ref, table_v, sem.at[1])
    accum_copy = pltpu.make_async_copy(accum_ref, accum_v, sem.at[2])
    grad_copy.start()
    table_copy.start()
    accum_copy.start()

    zero = jnp.zeros((BLOCK, dim), jnp.float32)

    def clear(i, carry):
        for bank in banks:
            bank[pl.ds(pl.multiple_of(i * BLOCK, BLOCK), BLOCK), :] = zero
        return carry

    lax.fori_loop(0, n_rows // BLOCK, clear, 0)
    for bank in banks:
        bank[pl.ds(n_rows, 8), :] = zero[:8]
    grad_copy.wait()
    per_bank = segs // BANKS
    for part in range(per_bank):
        def widen(i, carry):
            for j in range(BANKS):
                rows = pl.ds(pl.multiple_of(i * BLOCK, BLOCK), BLOCK)
                stage[j, rows, :] = grad_v[j * per_bank + part, rows, :].astype(jnp.float32)
            return carry

        lax.fori_loop(0, seg_rows // BLOCK, widen, 0)

        def add_rows(i, carry):
            base = i * UNROLL
            for u in range(UNROLL):
                for j in range(BANKS):
                    row = ids_ref[0, (j * per_bank + part) * seg_rows + base + u]
                    banks[j][pl.ds(row, 1), :] += stage[j, pl.ds(base + u, 1), :]
            return carry

        lax.fori_loop(0, seg_rows // UNROLL, add_rows, 0)

    table_copy.wait()
    accum_copy.wait()
    eye = lax.broadcasted_iota(jnp.int32, (BLOCK, dim), 0) == lax.broadcasted_iota(jnp.int32, (BLOCK, dim), 1)
    lr = lr_ref[0]

    def update(i, carry):
        rows = pl.ds(pl.multiple_of(i * BLOCK, BLOCK), BLOCK)
        grad = banks[0][rows, :]
        for bank in banks[1:]:
            grad = grad + bank[rows, :]
        old = jnp.where(eye, accum_v[pl.ds(i, 1), :], 0.0)
        new = jnp.sum(grad * grad * (1.0 / dim) + old, axis=1, keepdims=True)
        scale = lr / (jnp.sqrt(new) + EPSILON)
        table_o[rows, :] = (table_v[rows, :].astype(jnp.float32) - grad * scale).astype(jnp.bfloat16)
        accum_o[pl.ds(i, 1), :] = jnp.sum(jnp.where(eye, new, 0.0), axis=0, keepdims=True)
        return carry

    lax.fori_loop(0, n_rows // BLOCK, update, 0)
    out_copy = pltpu.make_async_copy(table_o, out_table_ref, sem.at[0])
    out_acc = pltpu.make_async_copy(accum_o, out_accum_ref, sem.at[1])
    out_copy.start()
    out_acc.start()
    out_copy.wait()
    out_acc.wait()


def update_slot(slot, ids, lr, grad, tables, accums, carried):
    _, n_rows, dim = tables.shape
    segs, seg_rows, _ = grad.shape
    return pl.pallas_call(
        functools.partial(update_kernel, slot, len(carried)),
        out_shape=tuple(jax.ShapeDtypeStruct(x.shape, x.dtype) for x in (tables, accums)),
        in_specs=[pl.BlockSpec(memory_space=pltpu.SMEM)] * 2 + [pl.BlockSpec(memory_space=pl.ANY)] * (3 + len(carried)),
        out_specs=(pl.BlockSpec(memory_space=pl.ANY),) * 2,
        input_output_aliases={5 + i: i for i in range(len(carried))},
        scratch_shapes=[pltpu.VMEM((n_rows + 8, dim), jnp.float32)] * BANKS + [
            pltpu.VMEM((BANKS, seg_rows, dim), jnp.float32),
            pltpu.VMEM((n_rows, dim), jnp.bfloat16),
            pltpu.VMEM((n_rows // BLOCK, BLOCK), jnp.float32),
            pltpu.VMEM((n_rows, dim), jnp.bfloat16),
            pltpu.VMEM((n_rows // BLOCK, BLOCK), jnp.float32),
            pltpu.VMEM((segs, seg_rows, dim), jnp.bfloat16),
            pltpu.SemaphoreType.DMA((3,)),
        ],
        compiler_params=pltpu.CompilerParams(vmem_limit_bytes=66000000),
        cost_estimate=pl.CostEstimate(flops=n_rows * dim * 400, bytes_accessed=4 * n_rows * dim * 2, transcendentals=0),
    )(ids, lr, grad, tables, accums, *carried)


def solution(mesh):
    n_group = mesh.shape['mp']
    slot_spec = P(('pod', 'mp'))

    def local_step(d_pool, row_ids, lengths, tables, row_accum, learn_rate):
        slots_dev, n_rows, _ = tables.shape
        by_table = jnp.transpose(d_pool, (1, 0, 2))
        n_tab = by_table.shape[0]
        padded = jnp.pad(by_table, ((0, slots_dev * n_group - n_tab), (0, 0), (0, 0)))
        ids = jnp.where(lengths > 0, row_ids[:, :, 0], n_rows)
        lr = learn_rate.reshape(1)
        accums = row_accum.reshape(slots_dev, -1, BLOCK)
        got = []
        for k in range(slots_dev):
            got.append(lax.all_to_all(padded[k::slots_dev], 'mp', 0, 0, tiled=True))
        carried = ()
        for k in range(slots_dev):
            carried = update_slot(k, ids[k:k + 1], lr, got[k], tables, accums, carried)
        return carried[0], carried[1].reshape(row_accum.shape)

    return jax.shard_map(local_step, mesh=mesh, in_specs=(slot_spec, slot_spec, slot_spec, slot_spec, slot_spec, P()), out_specs=(slot_spec, slot_spec), check_vma=False)
```

time: 625 us -> 388 us (0.62)
  the two profiles are of different devices: /device:TPU:81 before, /device:TPU:87 now
where the time goes in v1:
time: 388 us; the launch traced here: 387 us
  Pallas kernels  209 us (54%)
  blocking collectives  105 us (27%)
  waiting for transfers between devices  45.4 us (12%)
  starting transfers between devices  14.7 us (4%)
  local copies, waits for them, and re-layouts  11.8 us (3%)
    pallas_call x4, Pallas kernels, update_slot(): pl.pallas_call(functools.partial(update_kernel, slot, len(carried)), out_...  209 us
    all_to_all x2, blocking collectives, local_step(): got.append(lax.all_to_all(padded[k::slots_dev], 'mp', 0, 0, tiled=True))  105 us
    all_to_all x2, waiting for transfers between devices, local_step(): got.append(lax.all_to_all(padded[k::slots_dev], 'mp', 0, 0, tiled=True))  45.4 us
    all_to_all x2, starting transfers between devices, local_step(): got.append(lax.all_to_all(padded[k::slots_dev], 'mp', 0, 0, tiled=True))  14.7 us
    slice x1, local copies, waits for them, and re-layouts, local_step(): got.append(lax.all_to_all(padded[k::slots_dev], 'mp', 0, 0, tiled=True))  8.33 us
  transfers between devices with their start and end apart: 2, of which 1 were waited for; matrix products, arithmetic and copies ran while one was open for 0% of the time, Pallas kernels for 40%

profile of v1, /device:TPU:87, one launch (start us, length us, event | category | flops | bytes accessed | tf_op | source)
XLA Modules:
  0.0 387.0 jit_solution(4540543167144732181)
XLA Ops:
  0.6 8.3 %pad_slice_fusion = (bf16[8,2048,128]{2,1,0:T(8,128)(2,1)S(1)}, bf16[8,2048,128]{2,1,0:T(8,128)(2,1)S(1)}, bf16[8,2048,128]{2,1,0:T(8,128)(2,1)}, bf16[8,2048,128]{2,1,0:T(8,128)(2,1)}) fusion(bf16[26,2048,128]{2,1,0:T(8,128)(2,1)} %bitcast.16), kind=kLoop, calls=%fused_computation | loop fusion | bytes 30408704 | tf_op jit(solution)/shard_map/slice | solution.py:126
  9.0 51.7 %all_to_all.20.grad_ref = bf16[8,2048,128]{2,1,0:T(8,128)(2,1)} all-to-all(bf16[8,2048,128]{2,1,0:T(8,128)(2,1)S(1)} %get-tuple-element.18), channel_id=1, replica_groups=mesh['pod'=4,'mp'=8] {'mp'}, dimensions={0} | all-to-all | bytes 8388608 | tf_op jit(solution)/shard_map/all_to_all | solution.py:126
  60.7 53.0 %all_to_all.21.grad_ref = bf16[8,2048,128]{2,1,0:T(8,128)(2,1)} all-to-all(bf16[8,2048,128]{2,1,0:T(8,128)(2,1)S(1)} %get-tuple-element.19), channel_id=1, replica_groups=mesh['pod'=4,'mp'=8] {'mp'}, dimensions={0} | all-to-all | bytes 8388608 | tf_op jit(solution)/shard_map/all_to_all | solution.py:126
  113.7 0.0 copy-start.2
  113.7 0.0 copy-start
  113.7 0.0 copy-start.1
  113.7 7.5 %all-to-all-start.2 = ((bf16[8,2048,128]{2,1,0:T(8,128)(2,1)}), bf16[8,2048,128]{2,1,0:T(8,128)(2,1)}, u32[]{:S(2)}, u32[]{:S(2)}) async-start(bf16[8,2048,128]{2,1,0:T(8,128)(2,1)} %get-tuple-element.20), calls=%async_computation.2 | async-start | bytes 8388608 | tf_op jit(solution)/shard_map/all_to_all | solution.py:126
  121.8 0.0 copy-done.2
  121.8 0.7 copy.21
  122.5 0.0 copy-done
  122.5 0.0 copy-done.1
  122.5 0.2 bitcast_select_fusion
  122.8 45.4 %all-to-all-done.2.grad_ref = bf16[8,2048,128]{2,1,0:T(8,128)(2,1)} async-done(((bf16[8,2048,128]{2,1,0:T(8,128)(2,1)}), bf16[8,2048,128]{2,1,0:T(8,128)(2,1)}, u32[]{:S(2)}, u32[]{:S(2)}) %all-to-all-start.2) | async-done | bytes 4194336 | tf_op jit(solution)/shard_map/all_to_all | solution.py:126
  168.2 7.2 %all-to-all-start = ((bf16[8,2048,128]{2,1,0:T(8,128)(2,1)}), bf16[8,2048,128]{2,1,0:T(8,128)(2,1)}, u32[]{:S(2)}, u32[]{:S(2)}) async-start(bf16[8,2048,128]{2,1,0:T(8,128)(2,1)} %get-tuple-element.21), calls=%async_computation | async-start | bytes 8388608 | tf_op jit(solution)/shard_map/all_to_all | solution.py:126
  175.4 0.9 fusion
  176.3 52.2 %shard_map.77 = (bf16[4,16384,128]{2,1,0:T(8,128)(2,1)}, f32[4,128,128]{2,1,0:T(8,128)}) custom-call(s32[1,16384]{1,0:T(1,128)} %get-tuple-element.22.ids_ref, f32[1]{0:T(128)} %bitcast.12.lr_ref, bf16[8,2048,128]{2,1,0:T(8,128)(2,1)} %all_to_all.20.grad_ref, bf16[4,16384,128]{2,1,0:T(8,128)(2,1)} %tables_ref.7, f32[4,128,128]{2,1,0:T(8,128)} %bitcast.17), custom_call_target="tpu_custom_call" | custom-call | flops 838860800 | bytes 16777216 | tf_op jit(solution)/shard_map/pallas_call | solution.py:92
  228.5 52.2 %shard_map.78 = (bf16[4,16384,128]{2,1,0:T(8,128)(2,1)}, f32[4,128,128]{2,1,0:T(8,128)}) custom-call(s32[1,16384]{1,0:T(1,128)} %get-tuple-element.23.ids_ref, f32[1]{0:T(128)} %bitcast.13.lr_ref, bf16[8,2048,128]{2,1,0:T(8,128)(2,1)} %all-to-all-done.2.grad_ref, bf16[4,16384,128]{2,1,0:T(8,128)(2,1)} %tables_ref.7, ...), custom_call_target="tpu_custom_call", output_to_operand_aliasing={{0}: (5, {}), {1}: (6, {})} | custom-call | flops 838860800 | bytes 16777216 | tf_op jit(solution)/shard_map/pallas_call | solution.py:92
  280.7 52.2 %shard_map.79 = (bf16[4,16384,128]{2,1,0:T(8,128)(2,1)}, f32[4,128,128]{2,1,0:T(8,128)}) custom-call(s32[1,16384]{1,0:T(1,128)} %get-tuple-element.24.ids_ref, f32[1]{0:T(128)} %bitcast.14.lr_ref, bf16[8,2048,128]{2,1,0:T(8,128)(2,1)} %all_to_all.21.grad_ref, bf16[4,16384,128]{2,1,0:T(8,128)(2,1)} %tables_ref.7, ...), custom_call_target="tpu_custom_call", output_to_operand_aliasing={{0}: (5, {}), {1}: (6, {})} | custom-call | flops 838860800 | bytes 16777216 | tf_op jit(solution)/shard_map/pallas_call | solution.py:92
  333.0 0.0 all-to-all-done.grad_ref
  333.0 52.2 %shard_map.80 = (bf16[4,16384,128]{2,1,0:T(8,128)(2,1)}, f32[4,128,128]{2,1,0:T(8,128)}) custom-call(s32[1,16384]{1,0:T(1,128)} %get-tuple-element.25.ids_ref, f32[1]{0:T(128)} %bitcast.15.lr_ref, bf16[8,2048,128]{2,1,0:T(8,128)(2,1)} %all-to-all-done.grad_ref, bf16[4,16384,128]{2,1,0:T(8,128)(2,1)} %tables_ref.7, ...), custom_call_target="tpu_custom_call", output_to_operand_aliasing={{0}: (5, {}), {1}: (6, {})} | custom-call | flops 838860800 | bytes 16777216 | tf_op jit(solution)/shard_map/pallas_call | solution.py:92
  385.2 1.8 copy.20
Async XLA Ops:
  113.7 8.1 %copy-start.2 = (f32[4,16384]{1,0:T(4,128)S(1)}, f32[4,16384]{1,0:T(4,128)}, u32[]{:S(2)}) copy-start(f32[4,16384]{1,0:T(4,128)} %param.10) | copy-start | bytes 786436
  113.7 8.9 %copy-start = (s32[4,16384,1]{1,2,0:T(1,128)S(1)}, s32[4,16384,1]{1,2,0:T(1,128)}, u32[]{:S(2)}) copy-start(s32[4,16384,1]{1,2,0:T(1,128)} %param.7) | copy-start | bytes 786436
  113.7 8.9 %copy-start.1 = (s32[4,16384]{1,0:T(4,128)S(1)}, s32[4,16384]{1,0:T(4,128)}, u32[]{:S(2)}) copy-start(s32[4,16384]{1,0:T(4,128)} %param.8) | copy-start | bytes 786436
  113.7 54.5 %all-to-all-start.2 = ((bf16[8,2048,128]{2,1,0:T(8,128)(2,1)}), bf16[8,2048,128]{2,1,0:T(8,128)(2,1)}, u32[]{:S(2)}, u32[]{:S(2)}) async-start(bf16[8,2048,128]{2,1,0:T(8,128)(2,1)} %get-tuple-element.20), calls=%async_computation.2 | async-start | bytes 8388608 | tf_op jit(solution)/shard_map/all_to_all | solution.py:126
  168.2 164.8 %all-to-all-start = ((bf16[8,2048,128]{2,1,0:T(8,128)(2,1)}), bf16[8,2048,128]{2,1,0:T(8,128)(2,1)}, u32[]{:S(2)}, u32[]{:S(2)}) async-start(bf16[8,2048,128]{2,1,0:T(8,128)(2,1)} %get-tuple-element.21), calls=%async_computation | async-start | bytes 8388608 | tf_op jit(solution)/shard_map/all_to_all | solution.py:126

commit v2 on v1

v2 whole, which is shorter than its diff:
```python
import functools

import jax
import jax.numpy as jnp
from jax import lax
from jax.experimental import pallas as pl
from jax.experimental.pallas import tpu as pltpu
from jax.sharding import PartitionSpec as P


EPSILON = 1e-06
BANKS = 4
UNROLL = 8
BLOCK = 128
CHUNK = 1024
MAX_LANE = 64
VMEM_LIMIT = 66000000


def plan_kernel(n_dev, n_rows, ids_ref, lengths_ref, plan_ref, *refs):
    *packed_refs, ids_v, len_v = refs
    n_slots, batch = ids_ref.shape
    part = batch // n_dev
    for d in range(n_dev):
        ids_v[d * n_slots:(d + 1) * n_slots, :] = ids_ref[:, d * part:(d + 1) * part]
        len_v[d * n_slots:(d + 1) * n_slots, :] = lengths_ref[:, d * part:(d + 1) * part]
    rows = n_dev * n_slots
    below = lax.broadcasted_iota(jnp.int32, (BLOCK, BLOCK), 0) < lax.broadcasted_iota(jnp.int32, (BLOCK, BLOCK), 1)
    prefix = jnp.where(below, 1.0, 0.0).astype(jnp.bfloat16)
    lane = lax.broadcasted_iota(jnp.int32, (rows, BLOCK), 1)
    count = jnp.zeros((rows, 1), jnp.int32)
    starts = jnp.zeros((rows, BLOCK), jnp.int32)
    moves = []
    for b in range(part // BLOCK):
        cols = slice(b * BLOCK, (b + 1) * BLOCK)
        valid = len_v[:, cols] > 0
        ones = jnp.where(valid, 1.0, 0.0)
        local = jnp.dot(ones.astype(jnp.bfloat16), prefix, preferred_element_type=jnp.float32).astype(jnp.int32)
        place = jnp.where(valid, local, -1)
        for d in range(n_dev):
            plan_ref[d, :, cols] = place[d * n_slots:(d + 1) * n_slots, :]
        starts = jnp.where(lane == b, count, starts)
        shift = (b * BLOCK + lane) - (count + local)
        moves.append(jnp.where(valid, (shift << 16) | ids_v[:, cols], n_rows))
        count = count + jnp.sum(ones, axis=1, keepdims=True).astype(jnp.int32)
    most = jnp.max(count, axis=0, keepdims=True)
    starts = jnp.where(lane == MAX_LANE, most, starts)
    for d in range(n_dev):
        plan_ref[d, :, part:] = starts[d * n_slots:(d + 1) * n_slots, :]
    move = jnp.concatenate(moves, axis=1)
    step = 1
    while step < part:
        come = pltpu.roll(move, part - step, 1)
        bit = step << 16
        stay = jnp.where((move & bit) != 0, n_rows, move)
        move = jnp.where((come & bit) != 0, come, stay)
        step *= 2
    spot = lax.broadcasted_iota(jnp.int32, (rows, part), 1)
    packed = jnp.where(spot < count, move & 0xFFFF, n_rows)
    for s in range(n_slots):
        for d in range(n_dev):
            packed_refs[s][d:d + 1, :] = packed[d * n_slots + s:d * n_slots + s + 1, :]


def make_plan(ids, lengths, n_dev, n_rows):
    n_slots, batch = ids.shape
    part = batch // n_dev
    return pl.pallas_call(
        functools.partial(plan_kernel, n_dev, n_rows),
        out_shape=(jax.ShapeDtypeStruct((n_dev, n_slots, part + BLOCK), jnp.int32),)
        + (jax.ShapeDtypeStruct((n_dev, part), jnp.int32),) * n_slots,
        in_specs=[pl.BlockSpec(memory_space=pltpu.VMEM)] * 2,
        out_specs=(pl.BlockSpec(memory_space=pltpu.VMEM),) * (1 + n_slots),
        scratch_shapes=[pltpu.VMEM((n_dev * n_slots, part), jnp.int32)] * 2,
        compiler_params=pltpu.CompilerParams(vmem_limit_bytes=32000000),
        cost_estimate=pl.CostEstimate(flops=20000000, bytes_accessed=2000000, transcendentals=0),
    )(ids, lengths)


def pack_kernel(slot, n_used, starts_ref, plan_ref, tables_ref, out_ref, grad_v, stage, pack_v, in_sem, out_sem):
    _, cap, _ = out_ref.shape
    n_slots = plan_ref.shape[1]
    part = tables_ref.shape[1]
    slot_row = lax.broadcasted_iota(jnp.int32, (BLOCK, BLOCK), 0)

    def fetch(d, buf):
        return pltpu.make_async_copy(tables_ref.at[d * n_slots + slot], grad_v.at[buf], in_sem.at[buf])

    def emit(d, buf):
        return pltpu.make_async_copy(pack_v.at[buf], out_ref.at[d], out_sem.at[buf])

    fetch(0, 0).start()

    def table(d, carry):
        buf = d % 2

        @pl.when(d + 1 < n_used)
        def _():
            fetch(d + 1, 1 - buf).start()

        fetch(d, buf).wait()

        @pl.when(d >= 2)
        def _():
            emit(d - 2, buf).wait()

        for b in range(part // BLOCK):
            place = plan_ref[d, slot:slot + 1, b * BLOCK:(b + 1) * BLOCK]
            pick = jnp.where(slot_row == place, 1.0, 0.0).astype(jnp.bfloat16)
            rows = jnp.dot(pick, grad_v[buf, b * BLOCK:(b + 1) * BLOCK, :], preferred_element_type=jnp.float32)
            stage[pl.ds(starts_ref[d, slot, b], BLOCK), :] = rows
        pack_v[buf] = stage[:cap, :].astype(jnp.bfloat16)
        emit(d, buf).start()
        return carry

    lax.fori_loop(0, n_used, table, 0)
    for d in range(max(n_used - 2, 0), n_used):
        emit(d, d % 2).wait()


def pack_slot(slot, cap, starts, plan, by_table):
    n_dev, n_slots, _ = plan.shape
    n_tab, part, dim = by_table.shape
    n_used = len(range(slot, n_tab, n_slots))
    return pl.pallas_call(
        functools.partial(pack_kernel, slot, n_used),
        out_shape=jax.ShapeDtypeStruct((n_dev, cap, dim), by_table.dtype),
        in_specs=[pl.BlockSpec(memory_space=pltpu.SMEM), pl.BlockSpec(memory_space=pltpu.VMEM), pl.BlockSpec(memory_space=pl.ANY)],
        out_specs=pl.BlockSpec(memory_space=pl.ANY),
        scratch_shapes=[
            pltpu.VMEM((2, part, dim), by_table.dtype),
            pltpu.VMEM((cap + BLOCK, dim), jnp.float32),
            pltpu.VMEM((2, cap, dim), by_table.dtype),
            pltpu.SemaphoreType.DMA((2,)),
            pltpu.SemaphoreType.DMA((2,)),
        ],
        compiler_params=pltpu.CompilerParams(vmem_limit_bytes=VMEM_LIMIT),
        cost_estimate=pl.CostEstimate(flops=n_used * part * dim * 20, bytes_accessed=n_used * part * dim * 3, transcendentals=0),
    )(starts, plan, by_table)


def apply_kernel(slot, n_carried, ids_ref, lr_ref, grad_ref, tables_ref, accums_ref, *refs):
    out_tables_ref, out_accums_ref, *scratch = refs[n_carried:]
    out_table_ref, out_accum_ref = out_tables_ref.at[slot], out_accums_ref.at[slot]
    banks = scratch[:BANKS]
    stage, table_v, accum_v, grad_v, sem = scratch[BANKS:]
    segs, seg_rows, dim = grad_ref.shape
    n_rows = tables_ref.shape[1]
    grad_copy = pltpu.make_async_copy(grad_ref, grad_v, sem.at[0])
    table_copy = pltpu.make_async_copy(tables_ref.at[slot], table_v, sem.at[1])
    accum_copy = pltpu.make_async_copy(accums_ref.at[slot], accum_v, sem.at[2])
    grad_copy.start()
    table_copy.start()
    accum_copy.start()

    zero = jnp.zeros((BLOCK, dim), jnp.float32)

    def clear(i, carry):
        for bank in banks:
            bank[pl.ds(pl.multiple_of(i * BLOCK, BLOCK), BLOCK), :] = zero
        return carry

    lax.fori_loop(0, n_rows // BLOCK, clear, 0)
    for bank in banks:
        bank[pl.ds(n_rows, 8), :] = zero[:8]
    grad_copy.wait()
    per_bank = segs // BANKS
    for part in range(per_bank):
        def widen(i, carry):
            for j in range(BANKS):
                rows = pl.ds(pl.multiple_of(i * 64, 64), 64)
                stage[j, rows, :] = grad_v[j * per_bank + part, rows, :].astype(jnp.float32)
            return carry

        lax.fori_loop(0, seg_rows // 64, widen, 0)

        def add_rows(i, carry):
            base = i * UNROLL
            for u in range(UNROLL):
                for j in range(BANKS):
                    row = ids_ref[j * per_bank + part, base + u]
                    banks[j][pl.ds(row, 1), :] += stage[j, pl.ds(base + u, 1), :]
            return carry

        lax.fori_loop(0, seg_rows // UNROLL, add_rows, 0)

    table_copy.wait()
    accum_copy.wait()
    eye = lax.broadcasted_iota(jnp.int32, (BLOCK, dim), 0) == lax.broadcasted_iota(jnp.int32, (BLOCK, dim), 1)
    lr = lr_ref[0]

    def update(c, carry):
        for s in range(CHUNK // BLOCK):
            i = c * (CHUNK // BLOCK) + s
            rows = pl.ds(pl.multiple_of(i * BLOCK, BLOCK), BLOCK)
            grad = banks[0][rows, :]
            for bank in banks[1:]:
                grad = grad + bank[rows, :]
            old = jnp.where(eye, accum_v[pl.ds(i, 1), :], 0.0)
            new = jnp.sum(grad * grad * (1.0 / dim) + old, axis=1, keepdims=True)
            scale = lr / (jnp.sqrt(new) + EPSILON)
            table_v[rows, :] = (table_v[rows, :].astype(jnp.float32) - grad * scale).astype(jnp.bfloat16)
            accum_v[pl.ds(i, 1), :] = jnp.sum(jnp.where(eye, new, 0.0), axis=0, keepdims=True)
        done = pl.ds(pl.multiple_of(c * CHUNK, CHUNK), CHUNK)
        pltpu.make_async_copy(table_v.at[done], out_table_ref.at[done], sem.at[0]).start()
        return carry

    lax.fori_loop(0, n_rows // CHUNK, update, 0)
    out_acc = pltpu.make_async_copy(accum_v, out_accum_ref, sem.at[1])
    out_acc.start()
    pltpu.make_async_copy(table_v, out_table_ref, sem.at[0]).wait()
    out_acc.wait()


def apply_slot(slot, ids, lr, grad, tables, accums, carried):
    _, n_rows, dim = tables.shape
    segs, seg_rows, _ = grad.shape
    return pl.pallas_call(
        functools.partial(apply_kernel, slot, len(carried)),
        out_shape=tuple(jax.ShapeDtypeStruct(x.shape, x.dtype) for x in (tables, accums)),
        in_specs=[pl.BlockSpec(memory_space=pltpu.SMEM)] * 2 + [pl.BlockSpec(memory_space=pl.ANY)] * (3 + len(carried)),
        out_specs=(pl.BlockSpec(memory_space=pl.ANY),) * 2,
        input_output_aliases={5 + i: i for i in range(len(carried))},
        scratch_shapes=[pltpu.VMEM((n_rows + 8, dim), jnp.float32)] * BANKS + [
            pltpu.VMEM((BANKS, seg_rows, dim), jnp.float32),
            pltpu.VMEM((n_rows, dim), tables.dtype),
            pltpu.VMEM((n_rows // BLOCK, BLOCK), jnp.float32),
            pltpu.VMEM((segs, seg_rows, dim), grad.dtype),
            pltpu.SemaphoreType.DMA((3,)),
        ],
        compiler_params=pltpu.CompilerParams(vmem_limit_bytes=VMEM_LIMIT),
        cost_estimate=pl.CostEstimate(flops=n_rows * dim * 400, bytes_accessed=4 * n_rows * dim * 2, transcendentals=0),
    )(ids, lr, grad, tables, accums, *carried)


def solution(mesh):
    n_group = mesh.shape['mp']
    slot_spec = P(('pod', 'mp'))

    def local_step(d_pool, row_ids, lengths, tables, row_accum, learn_rate):
        n_slots, n_rows, _ = tables.shape
        by_table = jnp.transpose(d_pool, (1, 0, 2))
        part = by_table.shape[1]
        plan_out, *ids = make_plan(row_ids[:, :, 0], lengths, n_group, n_rows)
        plan = lax.all_to_all(plan_out, 'mp', 0, 0, tiled=True)
        starts = plan[:, :, part:]
        most = jnp.max(starts[:, :, MAX_LANE])
        lr = learn_rate.reshape(1)
        accums = row_accum.reshape(n_slots, -1, BLOCK)
        caps = tuple(c for c in CAPS(part))

        def exchange(level):
            def run(operands):
                by_table, plan, starts, ids, lr, tables, accums = operands
                got = []
                for k in range(n_slots):
                    pack = pack_slot(k, caps[level], starts, plan, by_table)
                    got.append(lax.all_to_all(pack, 'mp', 0, 0, tiled=True))
                carried = ()
                for k in range(n_slots):
                    carried = apply_slot(k, ids[k], lr, got[k], tables, accums, carried)
                return carried

            return run

        level = sum((most > cap).astype(jnp.int32) for cap in caps[:-1])
        operands = (by_table, plan, starts, tuple(ids), lr, tables, accums)
        new_tables, new_accums = lax.switch(level, [exchange(i) for i in range(len(caps))], operands)
        return new_tables, new_accums.reshape(row_accum.shape)

    return jax.shard_map(local_step, mesh=mesh, in_specs=(slot_spec, slot_spec, slot_spec, slot_spec, slot_spec, P()), out_specs=(slot_spec, slot_spec), check_vma=False)


def CAPS(part):
    return (part * 9 // 16, part)
```

time: 388 us -> 252 us (0.65)
  the two profiles are of different devices: /device:TPU:87 before, /device:TPU:95 now
where the time goes in v2:
time: 252 us; the launch traced here: 251 us
  Pallas kernels  144 us (57%)
  waiting for transfers between devices  61.8 us (25%)
  starting transfers between devices  27.7 us (11%)
  blocking collectives  10.2 us (4%)
  local copies, waits for them, and re-layouts  5.23 us (2%)
    pallas_call x4, Pallas kernels, apply_slot(): pl.pallas_call(functools.partial(apply_kernel, slot, len(carried)), out_s...  115 us
    all_to_all x4, waiting for transfers between devices, run(): got.append(lax.all_to_all(pack, 'mp', 0, 0, tiled=True))  61.8 us
    pallas_call x4, Pallas kernels, pack_slot(): pl.pallas_call(functools.partial(pack_kernel, slot, n_used), out_shape=ja...  27.8 us
    all_to_all x4, starting transfers between devices, run(): got.append(lax.all_to_all(pack, 'mp', 0, 0, tiled=True))  27.7 us
    all_to_all x1, blocking collectives, local_step(): plan = lax.all_to_all(plan_out, 'mp', 0, 0, tiled=True)  10.2 us
  transfers between devices with their start and end apart: 4, of which 3 were waited for; matrix products, arithmetic and copies ran while one was open for 0% of the time, Pallas kernels for 42%

profile of v2, /device:TPU:95, one launch (start us, length us, event | category | flops | bytes accessed | tf_op | source)
XLA Modules:
  0.0 250.5 jit_solution(2859330821897453371)
XLA Ops:
  0.6 1.1 copy.42
  1.8 0.0 copy-start
  1.8 0.9 copy-done
  2.7 1.1 shard_map.85
  3.8 10.2 %all_to_all.37 = s32[8,4,2176]{2,1,0:T(4,128)S(1)} all-to-all(s32[8,4,2176]{2,1,0:T(4,128)S(1)} %get-tuple-element.90), channel_id=1, replica_groups=mesh['pod'=4,'mp'=8] {'mp'}, dimensions={0} | all-to-all | bytes 557056 | tf_op jit(solution)/shard_map/all_to_all | solution.py:245
  14.0 0.7 slice_reduce_fusion
  15.4 235.1 %conditional.1 = (bf16[4,16384,128]{2,1,0:T(8,128)(2,1)}, f32[4,16384]{1,0:T(4,128)}) conditional(s32[]{:T(128)} %clamp.3, (f32[]{:T(128)}, s32[8,4,2176]{2,1,0:T(4,128)S(1)}, bf16[26,2048,128]{2,1,0:T(8,128)(2,1)}, f32[4,16384]{1,0:T(4,128)}, s32[8,2048]{1,0:T(8,128)S(1)}, /*index=5*/bf16[4,16384,128]{2,1,0:T(8,128)(2,1)}, s32[8,2048]{1,0:T(8,128)S(1)}, ...), branch_computations={%region_1.0_spmd, %region_2.0_spmd} | conditional | flops 3491758080 | bytes 140017840 | solution.py:268
  15.4 0.6 slice.8.starts_ref
  16.0 7.5 %branch_0_fun.11 = bf16[8,1152,128]{2,1,0:T(8,128)(2,1)} custom-call(s32[8,4,128]{2,1,0:T(4,128)} %slice.8.starts_ref, s32[8,4,2176]{2,1,0:T(4,128)S(1)} %get-tuple-element.51.plan_ref, bf16[26,2048,128]{2,1,0:T(8,128)(2,1)} %get-tuple-element.52.tables_ref), custom_call_target="tpu_custom_call" | custom-call | flops 36700160 | bytes 5505024 | tf_op jit(solution)/shard_map/cond/branch_0_fun/pallas_call | solution.py:125
  23.5 6.6 %all-to-all-start.3 = ((bf16[8,1152,128]{2,1,0:T(8,128)(2,1)}), bf16[8,1152,128]{2,1,0:T(8,128)(2,1)}, u32[]{:S(2)}, u32[]{:S(2)}) async-start(bf16[8,1152,128]{2,1,0:T(8,128)(2,1)} %branch_0_fun.11), calls=%async_computation.3 | async-start | bytes 4718592 | tf_op jit(solution)/shard_map/cond/branch_0_fun/all_to_all | solution.py:258
  30.1 7.5 %branch_0_fun.10 = bf16[8,1152,128]{2,1,0:T(8,128)(2,1)} custom-call(s32[8,4,128]{2,1,0:T(4,128)} %slice.8.starts_ref, s32[8,4,2176]{2,1,0:T(4,128)S(1)} %get-tuple-element.51.plan_ref, bf16[26,2048,128]{2,1,0:T(8,128)(2,1)} %get-tuple-element.52.tables_ref), custom_call_target="tpu_custom_call" | custom-call | flops 36700160 | bytes 5505024 | tf_op jit(solution)/shard_map/cond/branch_0_fun/pallas_call | solution.py:125
  37.6 19.9 %all-to-all-done.3.grad_ref = bf16[8,1152,128]{2,1,0:T(8,128)(2,1)} async-done(((bf16[8,1152,128]{2,1,0:T(8,128)(2,1)}), bf16[8,1152,128]{2,1,0:T(8,128)(2,1)}, u32[]{:S(2)}, u32[]{:S(2)}) %all-to-all-start.3) | async-done | bytes 2359328 | tf_op jit(solution)/shard_map/cond/branch_0_fun/all_to_all | solution.py:258
  57.4 7.0 %all-to-all-start.2 = ((bf16[8,1152,128]{2,1,0:T(8,128)(2,1)}), bf16[8,1152,128]{2,1,0:T(8,128)(2,1)}, u32[]{:S(2)}, u32[]{:S(2)}) async-start(bf16[8,1152,128]{2,1,0:T(8,128)(2,1)} %branch_0_fun.10), calls=%async_computation.2 | async-start | bytes 4718592 | tf_op jit(solution)/shard_map/cond/branch_0_fun/all_to_all | solution.py:258
  64.5 6.4 %branch_0_fun.9 = bf16[8,1152,128]{2,1,0:T(8,128)(2,1)} custom-call(s32[8,4,128]{2,1,0:T(4,128)} %slice.8.starts_ref, s32[8,4,2176]{2,1,0:T(4,128)S(1)} %get-tuple-element.51.plan_ref, bf16[26,2048,128]{2,1,0:T(8,128)(2,1)} %get-tuple-element.52.tables_ref), custom_call_target="tpu_custom_call" | custom-call | flops 31457280 | bytes 4718592 | tf_op jit(solution)/shard_map/cond/branch_0_fun/pallas_call | solution.py:125
  70.9 21.0 %all-to-all-done.2.grad_ref = bf16[8,1152,128]{2,1,0:T(8,128)(2,1)} async-done(((bf16[8,1152,128]{2,1,0:T(8,128)(2,1)}), bf16[8,1152,128]{2,1,0:T(8,128)(2,1)}, u32[]{:S(2)}, u32[]{:S(2)}) %all-to-all-start.2) | async-done | bytes 2359328 | tf_op jit(solution)/shard_map/cond/branch_0_fun/all_to_all | solution.py:258
  91.9 7.1 %all-to-all-start.1 = ((bf16[8,1152,128]{2,1,0:T(8,128)(2,1)}), bf16[8,1152,128]{2,1,0:T(8,128)(2,1)}, u32[]{:S(2)}, u32[]{:S(2)}) async-start(bf16[8,1152,128]{2,1,0:T(8,128)(2,1)} %branch_0_fun.9), calls=%async_computation.1 | async-start | bytes 4718592 | tf_op jit(solution)/shard_map/cond/branch_0_fun/all_to_all | solution.py:258
  98.9 6.4 %branch_0_fun.8 = bf16[8,1152,128]{2,1,0:T(8,128)(2,1)} custom-call(s32[8,4,128]{2,1,0:T(4,128)} %slice.8.starts_ref, s32[8,4,2176]{2,1,0:T(4,128)S(1)} %get-tuple-element.51.plan_ref, bf16[26,2048,128]{2,1,0:T(8,128)(2,1)} %get-tuple-element.52.tables_ref), custom_call_target="tpu_custom_call" | custom-call | flops 31457280 | bytes 4718592 | tf_op jit(solution)/shard_map/cond/branch_0_fun/pallas_call | solution.py:125
  105.3 0.0 copy-start.1
  105.3 21.0 %all-to-all-done.1.grad_ref = bf16[8,1152,128]{2,1,0:T(8,128)(2,1)} async-done(((bf16[8,1152,128]{2,1,0:T(8,128)(2,1)}), bf16[8,1152,128]{2,1,0:T(8,128)(2,1)}, u32[]{:S(2)}, u32[]{:S(2)}) %all-to-all-start.1) | async-done | bytes 2359328 | tf_op jit(solution)/shard_map/cond/branch_0_fun/all_to_all | solution.py:258
  126.3 7.0 %all-to-all-start = ((bf16[8,1152,128]{2,1,0:T(8,128)(2,1)}), bf16[8,1152,128]{2,1,0:T(8,128)(2,1)}, u32[]{:S(2)}, u32[]{:S(2)}) async-start(bf16[8,1152,128]{2,1,0:T(8,128)(2,1)} %branch_0_fun.8), calls=%async_computation | async-start | bytes 4718592 | tf_op jit(solution)/shard_map/cond/branch_0_fun/all_to_all | solution.py:258
  133.3 0.0 copy-done.1
  133.3 0.7 copy.39
  134.1 28.6 %branch_0_fun.12 = (bf16[4,16384,128]{2,1,0:T(8,128)(2,1)}, f32[4,128,128]{2,1,0:T(8,128)}) custom-call(s32[8,2048]{1,0:T(8,128)S(1)} %get-tuple-element.57.ids_ref, f32[1]{0:T(128)} %bitcast.lr_ref, bf16[8,1152,128]{2,1,0:T(8,128)(2,1)} %all-to-all-done.3.grad_ref, bf16[4,16384,128]{2,1,0:T(8,128)(2,1)} %get-tuple-element.106.tables_ref, ...), custom_call_target="tpu_custom_call" | custom-call | flops 838860800 | bytes 16777216 | tf_op jit(solution)/shard_map/cond/branch_0_fun/pallas_call | solution.py:218
  162.7 28.7 %branch_0_fun.13 = (bf16[4,16384,128]{2,1,0:T(8,128)(2,1)}, f32[4,128,128]{2,1,0:T(8,128)}) custom-call(s32[8,2048]{1,0:T(8,128)S(1)} %get-tuple-element.56.ids_ref, f32[1]{0:T(128)} %bitcast.lr_ref, bf16[8,1152,128]{2,1,0:T(8,128)(2,1)} %all-to-all-done.2.grad_ref, ...), custom_call_target="tpu_custom_call", output_to_operand_aliasing={{0}: (5, {}), {1}: (6, {})} | custom-call | flops 838860800 | bytes 16777216 | tf_op jit(solution)/shard_map/cond/branch_0_fun/pallas_call | solution.py:218
  191.4 28.7 %branch_0_fun.14 = (bf16[4,16384,128]{2,1,0:T(8,128)(2,1)}, f32[4,128,128]{2,1,0:T(8,128)}) custom-call(s32[8,2048]{1,0:T(8,128)S(1)} %get-tuple-element.55.ids_ref, f32[1]{0:T(128)} %bitcast.lr_ref, bf16[8,1152,128]{2,1,0:T(8,128)(2,1)} %all-to-all-done.1.grad_ref, ...), custom_call_target="tpu_custom_call", output_to_operand_aliasing={{0}: (5, {}), {1}: (6, {})} | custom-call | flops 838860800 | bytes 16777216 | tf_op jit(solution)/shard_map/cond/branch_0_fun/pallas_call | solution.py:218
  220.0 0.0 all-to-all-done.grad_ref
  220.0 28.7 %branch_0_fun.15 = (bf16[4,16384,128]{2,1,0:T(8,128)(2,1)}, f32[4,128,128]{2,1,0:T(8,128)}) custom-call(s32[8,2048]{1,0:T(8,128)S(1)} %get-tuple-element.49.ids_ref, f32[1]{0:T(128)} %bitcast.lr_ref, bf16[8,1152,128]{2,1,0:T(8,128)(2,1)} %all-to-all-done.grad_ref, ...), custom_call_target="tpu_custom_call", output_to_operand_aliasing={{0}: (5, {}), {1}: (6, {})} | custom-call | flops 838860800 | bytes 16777216 | tf_op jit(solution)/shard_map/cond/branch_0_fun/pallas_call | solution.py:218
  248.7 1.8 copy.38
Async XLA Ops:
  1.8 1.0 copy-start
  23.5 33.9 %all-to-all-start.3 = ((bf16[8,1152,128]{2,1,0:T(8,128)(2,1)}), bf16[8,1152,128]{2,1,0:T(8,128)(2,1)}, u32[]{:S(2)}, u32[]{:S(2)}) async-start(bf16[8,1152,128]{2,1,0:T(8,128)(2,1)} %branch_0_fun.11), calls=%async_computation.3 | async-start | bytes 4718592 | tf_op jit(solution)/shard_map/cond/branch_0_fun/all_to_all | solution.py:258
  57.4 34.4 %all-to-all-start.2 = ((bf16[8,1152,128]{2,1,0:T(8,128)(2,1)}), bf16[8,1152,128]{2,1,0:T(8,128)(2,1)}, u32[]{:S(2)}, u32[]{:S(2)}) async-start(bf16[8,1152,128]{2,1,0:T(8,128)(2,1)} %branch_0_fun.10), calls=%async_computation.2 | async-start | bytes 4718592 | tf_op jit(solution)/shard_map/cond/branch_0_fun/all_to_all | solution.py:258
  91.9 34.4 %all-to-all-start.1 = ((bf16[8,1152,128]{2,1,0:T(8,128)(2,1)}), bf16[8,1152,128]{2,1,0:T(8,128)(2,1)}, u32[]{:S(2)}, u32[]{:S(2)}) async-start(bf16[8,1152,128]{2,1,0:T(8,128)(2,1)} %branch_0_fun.9), calls=%async_computation.1 | async-start | bytes 4718592 | tf_op jit(solution)/shard_map/cond/branch_0_fun/all_to_all | solution.py:258
  105.3 28.0 %copy-start.1 = (f32[4,16384]{1,0:T(4,128)S(1)}, f32[4,16384]{1,0:T(4,128)}, u32[]{:S(2)}) copy-start(f32[4,16384]{1,0:T(4,128)} %get-tuple-element.104) | copy-start | bytes 786436 | tf_op jit(solution)/shard_map/cond
  126.3 93.7 %all-to-all-start = ((bf16[8,1152,128]{2,1,0:T(8,128)(2,1)}), bf16[8,1152,128]{2,1,0:T(8,128)(2,1)}, u32[]{:S(2)}, u32[]{:S(2)}) async-start(bf16[8,1152,128]{2,1,0:T(8,128)(2,1)} %branch_0_fun.8), calls=%async_computation | async-start | bytes 4718592 | tf_op jit(solution)/shard_map/cond/branch_0_fun/all_to_all | solution.py:258

commit v3 on v2

--- a/solution.py
+++ b/solution.py
@@ -9,6 +9,7 @@
 
 
 EPSILON = 1e-06
+TINY = 1e-36
 BANKS = 4
 UNROLL = 8
 BLOCK = 128
@@ -58,8 +59,10 @@
     spot = lax.broadcasted_iota(jnp.int32, (rows, part), 1)
     packed = jnp.where(spot < count, move & 0xFFFF, n_rows)
     for s in range(n_slots):
-        for d in range(n_dev):
-            packed_refs[s][d:d + 1, :] = packed[d * n_slots + s:d * n_slots + s + 1, :]
+        for j in range(n_dev // 2):
+            low, high = ((2 * j + h) * n_slots + s for h in range(2))
+            packed_refs[s][:, j * part:(j + 1) * part] = packed[low:low + 1, :] | (packed[high:high + 1, :] << 16)
+        packed_refs[s][:, n_dev // 2 * part:] = jnp.broadcast_to(most, (1, BLOCK))
 
 
 def make_plan(ids, lengths, n_dev, n_rows):
@@ -68,7 +71,7 @@
     return pl.pallas_call(
         functools.partial(plan_kernel, n_dev, n_rows),
         out_shape=(jax.ShapeDtypeStruct((n_dev, n_slots, part + BLOCK), jnp.int32),)
-        + (jax.ShapeDtypeStruct((n_dev, part), jnp.int32),) * n_slots,
+        + (jax.ShapeDtypeStruct((1, batch // 2 + BLOCK), jnp.int32),) * n_slots,
         in_specs=[pl.BlockSpec(memory_space=pltpu.VMEM)] * 2,
         out_specs=(pl.BlockSpec(memory_space=pltpu.VMEM),) * (1 + n_slots),
         scratch_shapes=[pltpu.VMEM((n_dev * n_slots, part), jnp.int32)] * 2,
@@ -89,16 +92,12 @@
     def emit(d, buf):
         return pltpu.make_async_copy(pack_v.at[buf], out_ref.at[d], out_sem.at[buf])
 
-    fetch(0, 0).start()
+    for d in range(n_used):
+        fetch(d, d).start()
 
     def table(d, carry):
         buf = d % 2
-
-        @pl.when(d + 1 < n_used)
-        def _():
-            fetch(d + 1, 1 - buf).start()
-
-        fetch(d, buf).wait()
+        fetch(d, d).wait()
 
         @pl.when(d >= 2)
         def _():
@@ -107,7 +106,7 @@
         for b in range(part // BLOCK):
             place = plan_ref[d, slot:slot + 1, b * BLOCK:(b + 1) * BLOCK]
             pick = jnp.where(slot_row == place, 1.0, 0.0).astype(jnp.bfloat16)
-            rows = jnp.dot(pick, grad_v[buf, b * BLOCK:(b + 1) * BLOCK, :], preferred_element_type=jnp.float32)
+            rows = jnp.dot(pick, grad_v[d, b * BLOCK:(b + 1) * BLOCK, :], preferred_element_type=jnp.float32)
             stage[pl.ds(starts_ref[d, slot, b], BLOCK), :] = rows
         pack_v[buf] = stage[:cap, :].astype(jnp.bfloat16)
         emit(d, buf).start()
@@ -128,10 +127,10 @@
         in_specs=[pl.BlockSpec(memory_space=pltpu.SMEM), pl.BlockSpec(memory_space=pltpu.VMEM), pl.BlockSpec(memory_space=pl.ANY)],
         out_specs=pl.BlockSpec(memory_space=pl.ANY),
         scratch_shapes=[
-            pltpu.VMEM((2, part, dim), by_table.dtype),
+            pltpu.VMEM((n_used, part, dim), by_table.dtype),
             pltpu.VMEM((cap + BLOCK, dim), jnp.float32),
             pltpu.VMEM((2, cap, dim), by_table.dtype),
-            pltpu.SemaphoreType.DMA((2,)),
+            pltpu.SemaphoreType.DMA((n_used,)),
             pltpu.SemaphoreType.DMA((2,)),
         ],
         compiler_params=pltpu.CompilerParams(vmem_limit_bytes=VMEM_LIMIT),
@@ -140,18 +139,16 @@
 
 
 def apply_kernel(slot, n_carried, ids_ref, lr_ref, grad_ref, tables_ref, accums_ref, *refs):
-    out_tables_ref, out_accums_ref, *scratch = refs[n_carried:]
-    out_table_ref, out_accum_ref = out_tables_ref.at[slot], out_accums_ref.at[slot]
+    carried_refs, (out_tables_ref, out_accums_ref, *scratch) = refs[:n_carried], refs[n_carried:]
     banks = scratch[:BANKS]
-    stage, table_v, accum_v, grad_v, sem = scratch[BANKS:]
+    stage, table_v, grad_v, sem = scratch[BANKS:]
     segs, seg_rows, dim = grad_ref.shape
     n_rows = tables_ref.shape[1]
+    id_stride = (ids_ref.shape[1] - BLOCK) // BANKS
     grad_copy = pltpu.make_async_copy(grad_ref, grad_v, sem.at[0])
     table_copy = pltpu.make_async_copy(tables_ref.at[slot], table_v, sem.at[1])
-    accum_copy = pltpu.make_async_copy(accums_ref.at[slot], accum_v, sem.at[2])
     grad_copy.start()
     table_copy.start()
-    accum_copy.start()
 
     zero = jnp.zeros((BLOCK, dim), jnp.float32)
 
@@ -164,28 +161,35 @@
     for bank in banks:
         bank[pl.ds(n_rows, 8), :] = zero[:8]
     grad_copy.wait()
-    per_bank = segs // BANKS
-    for part in range(per_bank):
-        def widen(i, carry):
-            for j in range(BANKS):
-                rows = pl.ds(pl.multiple_of(i * 64, 64), 64)
-                stage[j, rows, :] = grad_v[j * per_bank + part, rows, :].astype(jnp.float32)
-            return carry
-
-        lax.fori_loop(0, seg_rows // 64, widen, 0)
-
-        def add_rows(i, carry):
-            base = i * UNROLL
-            for u in range(UNROLL):
-                for j in range(BANKS):
-                    row = ids_ref[j * per_bank + part, base + u]
-                    banks[j][pl.ds(row, 1), :] += stage[j, pl.ds(base + u, 1), :]
-            return carry
-
-        lax.fori_loop(0, seg_rows // UNROLL, add_rows, 0)
+
+    def widen(i, carry):
+        for j in range(segs):
+            rows = pl.ds(pl.multiple_of(i * 32, 32), 32)
+            stage[j, rows, :] = grad_v[j, rows, :].astype(jnp.float32)
+        return carry
+
+    lax.fori_loop(0, seg_rows // 32, widen, 0)
+
+    def add_rows(i, carry):
+        base = i * UNROLL
+        for u in range(UNROLL):
+            for j, bank in enumerate(banks):
+                pair = ids_ref[0, j * id_stride + u + base]
+                first, second = pair & 0xFFFF, pair >> 16
+                same = jnp.full((1, dim), first) == jnp.full((1, dim), second)
+                add_first = stage[2 * j, pl.ds(base + u, 1), :]
+                add_second = stage[2 * j + 1, pl.ds(base + u, 1), :]
+                add_second = jnp.where(same, add_first + add_second, add_second)
+                old_first = bank[pl.ds(first, 1), :]
+                old_second = bank[pl.ds(second, 1), :]
+                bank[pl.ds(first, 1), :] = old_first + add_first
+                bank[pl.ds(second, 1), :] = old_second + add_second
+        return carry
+
+    lax.fori_loop(0, (ids_ref[0, BANKS * id_stride] + UNROLL - 1) // UNROLL, add_rows, 0)
 
     table_copy.wait()
-    accum_copy.wait()
+    out_accums_ref[...] = (carried_refs[1] if n_carried else accums_ref)[...]
     eye = lax.broadcasted_iota(jnp.int32, (BLOCK, dim), 0) == lax.broadcasted_iota(jnp.int32, (BLOCK, dim), 1)
     lr = lr_ref[0]
 
@@ -193,23 +197,22 @@
         for s in range(CHUNK // BLOCK):
             i = c * (CHUNK // BLOCK) + s
             rows = pl.ds(pl.multiple_of(i * BLOCK, BLOCK), BLOCK)
+            cols = pl.ds(pl.multiple_of(i * BLOCK, BLOCK), BLOCK)
             grad = banks[0][rows, :]
             for bank in banks[1:]:
                 grad = grad + bank[rows, :]
-            old = jnp.where(eye, accum_v[pl.ds(i, 1), :], 0.0)
+            old = jnp.where(eye, accums_ref[slot:slot + 1, cols], 0.0)
             new = jnp.sum(grad * grad * (1.0 / dim) + old, axis=1, keepdims=True)
-            scale = lr / (jnp.sqrt(new) + EPSILON)
+            out_accums_ref[slot:slot + 1, cols] = jnp.sum(jnp.where(eye, new, 0.0), axis=0, keepdims=True)
+            root = lax.rsqrt(jnp.maximum(new, TINY))
+            scale = lr * root / (1.0 + EPSILON * root)
             table_v[rows, :] = (table_v[rows, :].astype(jnp.float32) - grad * scale).astype(jnp.bfloat16)
-            accum_v[pl.ds(i, 1), :] = jnp.sum(jnp.where(eye, new, 0.0), axis=0, keepdims=True)
         done = pl.ds(pl.multiple_of(c * CHUNK, CHUNK), CHUNK)
-        pltpu.make_async_copy(table_v.at[done], out_table_ref.at[done], sem.at[0]).start()
+        pltpu.make_async_copy(table_v.at[done], out_tables_ref.at[slot, done], sem.at[0]).start()
         return carry
 
     lax.fori_loop(0, n_rows // CHUNK, update, 0)
-    out_acc = pltpu.make_async_copy(accum_v, out_accum_ref, sem.at[1])
-    out_acc.start()
-    pltpu.make_async_copy(table_v, out_table_ref, sem.at[0]).wait()
-    out_acc.wait()
+    pltpu.make_async_copy(table_v, out_tables_ref.at[slot], sem.at[0]).wait()
 
 
 def apply_slot(slot, ids, lr, grad, tables, accums, carried):
@@ -218,15 +221,17 @@
     return pl.pallas_call(
         functools.partial(apply_kernel, slot, len(carried)),
         out_shape=tuple(jax.ShapeDtypeStruct(x.shape, x.dtype) for x in (tables, accums)),
-        in_specs=[pl.BlockSpec(memory_space=pltpu.SMEM)] * 2 + [pl.BlockSpec(memory_space=pl.ANY)] * (3 + len(carried)),
-        out_specs=(pl.BlockSpec(memory_space=pl.ANY),) * 2,
-        input_output_aliases={5 + i: i for i in range(len(carried))},
+        in_specs=[pl.BlockSpec(memory_space=pltpu.SMEM)] * 2
+        + [pl.BlockSpec(memory_space=pl.ANY)] * 2
+        + [pl.BlockSpec(memory_space=pltpu.VMEM)]
+        + [pl.BlockSpec(memory_space=pl.ANY), pl.BlockSpec(memory_space=pltpu.VMEM)][:len(carried)],
+        out_specs=(pl.BlockSpec(memory_space=pl.ANY), pl.BlockSpec(memory_space=pltpu.VMEM)),
+        input_output_aliases={5: 0} if carried else {},
         scratch_shapes=[pltpu.VMEM((n_rows + 8, dim), jnp.float32)] * BANKS + [
-            pltpu.VMEM((BANKS, seg_rows, dim), jnp.float32),
+            pltpu.VMEM((segs, seg_rows, dim), jnp.float32),
             pltpu.VMEM((n_rows, dim), tables.dtype),
-            pltpu.VMEM((n_rows // BLOCK, BLOCK), jnp.float32),
             pltpu.VMEM((segs, seg_rows, dim), grad.dtype),
-            pltpu.SemaphoreType.DMA((3,)),
+            pltpu.SemaphoreType.DMA((2,)),
         ],
         compiler_params=pltpu.CompilerParams(vmem_limit_bytes=VMEM_LIMIT),
         cost_estimate=pl.CostEstimate(flops=n_rows * dim * 400, bytes_accessed=4 * n_rows * dim * 2, transcendentals=0),
@@ -246,7 +251,6 @@
         starts = plan[:, :, part:]
         most = jnp.max(starts[:, :, MAX_LANE])
         lr = learn_rate.reshape(1)
-        accums = row_accum.reshape(n_slots, -1, BLOCK)
         caps = tuple(c for c in CAPS(part))
 
         def exchange(level):
@@ -259,14 +263,13 @@
                 carried = ()
                 for k in range(n_slots):
                     carried = apply_slot(k, ids[k], lr, got[k], tables, accums, carried)
-                return carried
+                return tuple(carried)
 
             return run
 
         level = sum((most > cap).astype(jnp.int32) for cap in caps[:-1])
-        operands = (by_table, plan, starts, tuple(ids), lr, tables, accums)
-        new_tables, new_accums = lax.switch(level, [exchange(i) for i in range(len(caps))], operands)
-        return new_tables, new_accums.reshape(row_accum.shape)
+        operands = (by_table, plan, starts, tuple(ids), lr, tables, row_accum)
+        return lax.switch(level, [exchange(i) for i in range(len(caps))], operands)
 
     return jax.shard_map(local_step, mesh=mesh, in_specs=(slot_spec, slot_spec, slot_spec, slot_spec, slot_spec, P()), out_specs=(slot_spec, slot_spec), check_vma=False)
 

time: 252 us -> 215 us (0.85)
  the two profiles are of different devices: /device:TPU:95 before, /device:TPU:81 now
where the time goes in v3:
time: 215 us; the launch traced here: 212 us
  Pallas kernels  104 us (48%)
  waiting for transfers between devices  70.4 us (33%)
  starting transfers between devices  20.4 us (9%)
  blocking collectives  13 us (6%)
  local copies, waits for them, and re-layouts  2.68 us (1%)
    pallas_call x4, Pallas kernels, apply_slot(): pl.pallas_call(functools.partial(apply_kernel, slot, len(carried)), out_s...  79.4 us
    all_to_all x4, waiting for transfers between devices, run(): got.append(lax.all_to_all(pack, 'mp', 0, 0, tiled=True))  70.4 us
    pallas_call x4, Pallas kernels, pack_slot(): pl.pallas_call(functools.partial(pack_kernel, slot, n_used), out_shape=ja...  23.4 us
    all_to_all x4, starting transfers between devices, run(): got.append(lax.all_to_all(pack, 'mp', 0, 0, tiled=True))  20.4 us
    all_to_all x1, blocking collectives, local_step(): plan = lax.all_to_all(plan_out, 'mp', 0, 0, tiled=True)  13 us
  transfers between devices with their start and end apart: 4, of which 3 were waited for; matrix products, arithmetic and copies ran while one was open for 0% of the time, Pallas kernels for 36%

profile of v3, /device:TPU:81, one launch (start us, length us, event | category | flops | bytes accessed | tf_op | source)
XLA Modules:
  0.0 212.5 jit_solution(4751142830340393981)
XLA Ops:
  0.6 1.1 copy.26
  1.8 0.0 copy-start
  1.8 0.9 copy-done
  2.7 1.1 shard_map.87
  3.8 13.0 %all_to_all.37 = s32[8,4,2176]{2,1,0:T(4,128)S(1)} all-to-all(s32[8,4,2176]{2,1,0:T(4,128)S(1)} %get-tuple-element.79), channel_id=1, replica_groups=mesh['pod'=4,'mp'=8] {'mp'}, dimensions={0} | all-to-all | bytes 557056 | tf_op jit(solution)/shard_map/all_to_all | solution.py:250
  16.8 0.7 slice_reduce_fusion
  18.2 194.3 %conditional.1 = ((bf16[4,16384,128]{2,1,0:T(8,128)(2,1)}, f32[4,16384]{1,0:T(4,128)})) conditional(s32[]{:T(128)} %clamp.3, (s32[8,4,2176]{2,1,0:T(4,128)S(1)}, s32[8,4,2176]{2,1,0:T(4,128)S(1)}, bf16[26,2048,128]{2,1,0:T(8,128)(2,1)}, s32[1,8320]{1,0:T(1,128)S(1)}, f32[]{:T(128)}, /*index=5*/bf16[4,16384,128]{2,1,0:T(8,128)(2,1)}, ...), branch_computations={%region_1.0_spmd, %region_2.0_spmd} | conditional | flops 3491758080 | bytes 138969248 | solution.py:272
  18.2 0.6 slice.9.starts_ref
  18.8 6.2 %branch_0_fun.11 = bf16[8,1152,128]{2,1,0:T(8,128)(2,1)} custom-call(s32[8,4,128]{2,1,0:T(4,128)} %slice.9.starts_ref, s32[8,4,2176]{2,1,0:T(4,128)S(1)} %get-tuple-element.43.plan_ref, bf16[26,2048,128]{2,1,0:T(8,128)(2,1)} %get-tuple-element.44.tables_ref), custom_call_target="tpu_custom_call" | custom-call | flops 36700160 | bytes 5505024 | tf_op jit(solution)/shard_map/cond/branch_0_fun/pallas_call | solution.py:124
  25.0 4.8 %all-to-all-start.3 = ((bf16[8,1152,128]{2,1,0:T(8,128)(2,1)}), bf16[8,1152,128]{2,1,0:T(8,128)(2,1)}, u32[]{:S(2)}, u32[]{:S(2)}) async-start(bf16[8,1152,128]{2,1,0:T(8,128)(2,1)} %branch_0_fun.11), calls=%async_computation.3 | async-start | bytes 4718592 | tf_op jit(solution)/shard_map/cond/branch_0_fun/all_to_all | solution.py:262
  29.8 6.2 %branch_0_fun.10 = bf16[8,1152,128]{2,1,0:T(8,128)(2,1)} custom-call(s32[8,4,128]{2,1,0:T(4,128)} %slice.9.starts_ref, s32[8,4,2176]{2,1,0:T(4,128)S(1)} %get-tuple-element.43.plan_ref, bf16[26,2048,128]{2,1,0:T(8,128)(2,1)} %get-tuple-element.44.tables_ref), custom_call_target="tpu_custom_call" | custom-call | flops 36700160 | bytes 5505024 | tf_op jit(solution)/shard_map/cond/branch_0_fun/pallas_call | solution.py:124
  36.0 23.0 %all-to-all-done.3.grad_ref = bf16[8,1152,128]{2,1,0:T(8,128)(2,1)} async-done(((bf16[8,1152,128]{2,1,0:T(8,128)(2,1)}), bf16[8,1152,128]{2,1,0:T(8,128)(2,1)}, u32[]{:S(2)}, u32[]{:S(2)}) %all-to-all-start.3) | async-done | bytes 2359328 | tf_op jit(solution)/shard_map/cond/branch_0_fun/all_to_all | solution.py:262
  59.0 5.2 %all-to-all-start.2 = ((bf16[8,1152,128]{2,1,0:T(8,128)(2,1)}), bf16[8,1152,128]{2,1,0:T(8,128)(2,1)}, u32[]{:S(2)}, u32[]{:S(2)}) async-start(bf16[8,1152,128]{2,1,0:T(8,128)(2,1)} %branch_0_fun.10), calls=%async_computation.2 | async-start | bytes 4718592 | tf_op jit(solution)/shard_map/cond/branch_0_fun/all_to_all | solution.py:262
  64.2 5.5 %branch_0_fun.9 = bf16[8,1152,128]{2,1,0:T(8,128)(2,1)} custom-call(s32[8,4,128]{2,1,0:T(4,128)} %slice.9.starts_ref, s32[8,4,2176]{2,1,0:T(4,128)S(1)} %get-tuple-element.43.plan_ref, bf16[26,2048,128]{2,1,0:T(8,128)(2,1)} %get-tuple-element.44.tables_ref), custom_call_target="tpu_custom_call" | custom-call | flops 31457280 | bytes 4718592 | tf_op jit(solution)/shard_map/cond/branch_0_fun/pallas_call | solution.py:124
  69.7 23.7 %all-to-all-done.2.grad_ref = bf16[8,1152,128]{2,1,0:T(8,128)(2,1)} async-done(((bf16[8,1152,128]{2,1,0:T(8,128)(2,1)}), bf16[8,1152,128]{2,1,0:T(8,128)(2,1)}, u32[]{:S(2)}, u32[]{:S(2)}) %all-to-all-start.2) | async-done | bytes 2359328 | tf_op jit(solution)/shard_map/cond/branch_0_fun/all_to_all | solution.py:262
  93.4 5.2 %all-to-all-start.1 = ((bf16[8,1152,128]{2,1,0:T(8,128)(2,1)}), bf16[8,1152,128]{2,1,0:T(8,128)(2,1)}, u32[]{:S(2)}, u32[]{:S(2)}) async-start(bf16[8,1152,128]{2,1,0:T(8,128)(2,1)} %branch_0_fun.9), calls=%async_computation.1 | async-start | bytes 4718592 | tf_op jit(solution)/shard_map/cond/branch_0_fun/all_to_all | solution.py:262
  98.6 5.5 %branch_0_fun.8 = bf16[8,1152,128]{2,1,0:T(8,128)(2,1)} custom-call(s32[8,4,128]{2,1,0:T(4,128)} %slice.9.starts_ref, s32[8,4,2176]{2,1,0:T(4,128)S(1)} %get-tuple-element.43.plan_ref, bf16[26,2048,128]{2,1,0:T(8,128)(2,1)} %get-tuple-element.44.tables_ref), custom_call_target="tpu_custom_call" | custom-call | flops 31457280 | bytes 4718592 | tf_op jit(solution)/shard_map/cond/branch_0_fun/pallas_call | solution.py:124
  104.1 0.0 copy-start.1
  104.1 23.7 %all-to-all-done.1.grad_ref = bf16[8,1152,128]{2,1,0:T(8,128)(2,1)} async-done(((bf16[8,1152,128]{2,1,0:T(8,128)(2,1)}), bf16[8,1152,128]{2,1,0:T(8,128)(2,1)}, u32[]{:S(2)}, u32[]{:S(2)}) %all-to-all-start.1) | async-done | bytes 2359328 | tf_op jit(solution)/shard_map/cond/branch_0_fun/all_to_all | solution.py:262
  127.8 5.2 %all-to-all-start = ((bf16[8,1152,128]{2,1,0:T(8,128)(2,1)}), bf16[8,1152,128]{2,1,0:T(8,128)(2,1)}, u32[]{:S(2)}, u32[]{:S(2)}) async-start(bf16[8,1152,128]{2,1,0:T(8,128)(2,1)} %branch_0_fun.8), calls=%async_computation | async-start | bytes 4718592 | tf_op jit(solution)/shard_map/cond/branch_0_fun/all_to_all | solution.py:262
  133.0 0.0 copy-done.1
  133.0 19.9 %branch_0_fun.12 = (bf16[4,16384,128]{2,1,0:T(8,128)(2,1)}, f32[4,16384]{1,0:T(4,128)}) custom-call(s32[1,8320]{1,0:T(1,128)S(1)} %get-tuple-element.49.ids_ref, f32[1]{0:T(128)} %bitcast.lr_ref, bf16[8,1152,128]{2,1,0:T(8,128)(2,1)} %all-to-all-done.3.grad_ref, bf16[4,16384,128]{2,1,0:T(8,128)(2,1)} %get-tuple-element.100.tables_ref, f32[4,16384]{1,0:T(4,128)S(1)} %copy-done.1), custom_call_target="tpu_custom_call" | custom-call | flops 838860800 | bytes 16777216 | tf_op jit(solution)/shard_map/cond/branch_0_fun/pallas_call | solution.py:221
  152.9 19.9 %branch_0_fun.13 = (bf16[4,16384,128]{2,1,0:T(8,128)(2,1)}, f32[4,16384]{1,0:T(4,128)}) custom-call(s32[1,8320]{1,0:T(1,128)S(1)} %get-tuple-element.48.ids_ref, f32[1]{0:T(128)} %bitcast.lr_ref, bf16[8,1152,128]{2,1,0:T(8,128)(2,1)} %all-to-all-done.2.grad_ref, ...), custom_call_target="tpu_custom_call", output_to_operand_aliasing={{0}: (5, {})} | custom-call | flops 838860800 | bytes 16777216 | tf_op jit(solution)/shard_map/cond/branch_0_fun/pallas_call | solution.py:221
  172.8 19.8 %branch_0_fun.14 = (bf16[4,16384,128]{2,1,0:T(8,128)(2,1)}, f32[4,16384]{1,0:T(4,128)}) custom-call(s32[1,8320]{1,0:T(1,128)S(1)} %get-tuple-element.47.ids_ref, f32[1]{0:T(128)} %bitcast.lr_ref, bf16[8,1152,128]{2,1,0:T(8,128)(2,1)} %all-to-all-done.1.grad_ref, ...), custom_call_target="tpu_custom_call", output_to_operand_aliasing={{0}: (5, {})} | custom-call | flops 838860800 | bytes 16777216 | tf_op jit(solution)/shard_map/cond/branch_0_fun/pallas_call | solution.py:221
  192.6 0.0 all-to-all-done.grad_ref
  192.6 19.8 %branch_0_fun.15 = (bf16[4,16384,128]{2,1,0:T(8,128)(2,1)}, f32[4,16384]{1,0:T(4,128)}) custom-call(s32[1,8320]{1,0:T(1,128)S(1)} %get-tuple-element.40.ids_ref, f32[1]{0:T(128)} %bitcast.lr_ref, bf16[8,1152,128]{2,1,0:T(8,128)(2,1)} %all-to-all-done.grad_ref, bf16[4,16384,128]{2,1,0:T(8,128)(2,1)} %get-tuple-element.100.tables_ref, ...), custom_call_target="tpu_custom_call", output_to_operand_aliasing={{0}: (5, {})} | custom-call | flops 838860800 | bytes 16777216 | tf_op jit(solution)/shard_map/cond/branch_0_fun/pallas_call | solution.py:221
Async XLA Ops:
  1.8 1.0 copy-start
  25.0 34.0 %all-to-all-start.3 = ((bf16[8,1152,128]{2,1,0:T(8,128)(2,1)}), bf16[8,1152,128]{2,1,0:T(8,128)(2,1)}, u32[]{:S(2)}, u32[]{:S(2)}) async-start(bf16[8,1152,128]{2,1,0:T(8,128)(2,1)} %branch_0_fun.11), calls=%async_computation.3 | async-start | bytes 4718592 | tf_op jit(solution)/shard_map/cond/branch_0_fun/all_to_all | solution.py:262
  59.0 34.4 %all-to-all-start.2 = ((bf16[8,1152,128]{2,1,0:T(8,128)(2,1)}), bf16[8,1152,128]{2,1,0:T(8,128)(2,1)}, u32[]{:S(2)}, u32[]{:S(2)}) async-start(bf16[8,1152,128]{2,1,0:T(8,128)(2,1)} %branch_0_fun.10), calls=%async_computation.2 | async-start | bytes 4718592 | tf_op jit(solution)/shard_map/cond/branch_0_fun/all_to_all | solution.py:262
  93.4 34.4 %all-to-all-start.1 = ((bf16[8,1152,128]{2,1,0:T(8,128)(2,1)}), bf16[8,1152,128]{2,1,0:T(8,128)(2,1)}, u32[]{:S(2)}, u32[]{:S(2)}) async-start(bf16[8,1152,128]{2,1,0:T(8,128)(2,1)} %branch_0_fun.9), calls=%async_computation.1 | async-start | bytes 4718592 | tf_op jit(solution)/shard_map/cond/branch_0_fun/all_to_all | solution.py:262
  104.1 28.9 %copy-start.1 = (f32[4,16384]{1,0:T(4,128)S(1)}, f32[4,16384]{1,0:T(4,128)}, u32[]{:S(2)}) copy-start(f32[4,16384]{1,0:T(4,128)} %get-tuple-element.102.accums_ref) | copy-start | bytes 786436 | tf_op jit(solution)/shard_map/cond
  127.8 64.8 %all-to-all-start = ((bf16[8,1152,128]{2,1,0:T(8,128)(2,1)}), bf16[8,1152,128]{2,1,0:T(8,128)(2,1)}, u32[]{:S(2)}, u32[]{:S(2)}) async-start(bf16[8,1152,128]{2,1,0:T(8,128)(2,1)} %branch_0_fun.8), calls=%async_computation | async-start | bytes 4718592 | tf_op jit(solution)/shard_map/cond/branch_0_fun/all_to_all | solution.py:262

commit v4 on v3

--- a/solution.py
+++ b/solution.py
@@ -18,8 +18,9 @@
 VMEM_LIMIT = 66000000
 
 
-def plan_kernel(n_dev, n_rows, ids_ref, lengths_ref, plan_ref, *refs):
+def plan_kernel(n_dev, n_rows, me_ref, ids_ref, lengths_ref, plan_ref, *refs):
     *packed_refs, ids_v, len_v = refs
+    me = me_ref[0]
     n_slots, batch = ids_ref.shape
     part = batch // n_dev
     for d in range(n_dev):
@@ -57,97 +58,99 @@
         move = jnp.where((come & bit) != 0, come, stay)
         step *= 2
     spot = lax.broadcasted_iota(jnp.int32, (rows, part), 1)
-    packed = jnp.where(spot < count, move & 0xFFFF, n_rows)
+    ids_v[...] = jnp.where(spot < count, move & 0xFFFF, n_rows)
     for s in range(n_slots):
         for j in range(n_dev // 2):
-            low, high = ((2 * j + h) * n_slots + s for h in range(2))
-            packed_refs[s][:, j * part:(j + 1) * part] = packed[low:low + 1, :] | (packed[high:high + 1, :] << 16)
+            low, high = (ids_v[pl.ds((me + (n_dev - 2 * j - h)) % n_dev * n_slots + s, 1), :] for h in range(2))
+            packed_refs[s][:, j * part:(j + 1) * part] = low | (high << 16)
         packed_refs[s][:, n_dev // 2 * part:] = jnp.broadcast_to(most, (1, BLOCK))
 
 
-def make_plan(ids, lengths, n_dev, n_rows):
+def make_plan(me, ids, lengths, n_dev, n_rows):
     n_slots, batch = ids.shape
     part = batch // n_dev
     return pl.pallas_call(
         functools.partial(plan_kernel, n_dev, n_rows),
         out_shape=(jax.ShapeDtypeStruct((n_dev, n_slots, part + BLOCK), jnp.int32),)
         + (jax.ShapeDtypeStruct((1, batch // 2 + BLOCK), jnp.int32),) * n_slots,
-        in_specs=[pl.BlockSpec(memory_space=pltpu.VMEM)] * 2,
+        in_specs=[pl.BlockSpec(memory_space=pltpu.SMEM)] + [pl.BlockSpec(memory_space=pltpu.VMEM)] * 2,
         out_specs=(pl.BlockSpec(memory_space=pltpu.VMEM),) * (1 + n_slots),
         scratch_shapes=[pltpu.VMEM((n_dev * n_slots, part), jnp.int32)] * 2,
         compiler_params=pltpu.CompilerParams(vmem_limit_bytes=32000000),
         cost_estimate=pl.CostEstimate(flops=20000000, bytes_accessed=2000000, transcendentals=0),
-    )(ids, lengths)
-
-
-def pack_kernel(slot, n_used, starts_ref, plan_ref, tables_ref, out_ref, grad_v, stage, pack_v, in_sem, out_sem):
-    _, cap, _ = out_ref.shape
-    n_slots = plan_ref.shape[1]
-    part = tables_ref.shape[1]
+    )(me, ids, lengths)
+
+
+def pack_kernel(slot, me_ref, starts_ref, plan_ref, tables_ref, *refs):
+    n_dev, n_slots, _ = plan_ref.shape
+    n_tab, part, _ = tables_ref.shape
+    out_refs, (grad_v, stage, pack_v, in_sem, out_sem) = refs[:n_dev], refs[n_dev:]
+    cap = pack_v.shape[1]
     slot_row = lax.broadcasted_iota(jnp.int32, (BLOCK, BLOCK), 0)
-
-    def fetch(d, buf):
-        return pltpu.make_async_copy(tables_ref.at[d * n_slots + slot], grad_v.at[buf], in_sem.at[buf])
-
-    def emit(d, buf):
-        return pltpu.make_async_copy(pack_v.at[buf], out_ref.at[d], out_sem.at[buf])
-
-    for d in range(n_used):
-        fetch(d, d).start()
-
-    def table(d, carry):
-        buf = d % 2
-        fetch(d, d).wait()
-
-        @pl.when(d >= 2)
+    me = me_ref[0]
+
+    def fetch(o):
+        table = jnp.minimum((me + o) % n_dev * n_slots + slot, n_tab - 1)
+        return pltpu.make_async_copy(tables_ref.at[table], grad_v.at[o], in_sem.at[o])
+
+    for o in range(n_dev):
+        fetch(o).start()
+
+    def one(o, carry):
+        d = (me + o) % n_dev
+        fetch(o).wait()
+
+        @pl.when(d * n_slots + slot < n_tab)
         def _():
-            emit(d - 2, buf).wait()
-
-        for b in range(part // BLOCK):
-            place = plan_ref[d, slot:slot + 1, b * BLOCK:(b + 1) * BLOCK]
-            pick = jnp.where(slot_row == place, 1.0, 0.0).astype(jnp.bfloat16)
-            rows = jnp.dot(pick, grad_v[d, b * BLOCK:(b + 1) * BLOCK, :], preferred_element_type=jnp.float32)
-            stage[pl.ds(starts_ref[d, slot, b], BLOCK), :] = rows
-        pack_v[buf] = stage[:cap, :].astype(jnp.bfloat16)
-        emit(d, buf).start()
-        return carry
-
-    lax.fori_loop(0, n_used, table, 0)
-    for d in range(max(n_used - 2, 0), n_used):
-        emit(d, d % 2).wait()
-
-
-def pack_slot(slot, cap, starts, plan, by_table):
-    n_dev, n_slots, _ = plan.shape
-    n_tab, part, dim = by_table.shape
-    n_used = len(range(slot, n_tab, n_slots))
+            for b in range(part // BLOCK):
+                place = plan_ref[d, slot:slot + 1, b * BLOCK:(b + 1) * BLOCK]
+                pick = jnp.where(slot_row == place, 1.0, 0.0).astype(jnp.bfloat16)
+                rows = jnp.dot(pick, grad_v[o, b * BLOCK:(b + 1) * BLOCK, :], preferred_element_type=jnp.float32)
+                stage[pl.ds(starts_ref[d, slot, b], BLOCK), :] = rows
+            pack_v[o] = stage[:cap, :].astype(jnp.bfloat16)
+
+        return carry
+
+    lax.fori_loop(0, n_dev, one, 0)
+    copies = [pltpu.make_async_copy(pack_v.at[o], out_refs[o], out_sem.at[o]) for o in range(n_dev)]
+    for copy in copies:
+        copy.start()
+    for copy in copies:
+        copy.wait()
+
+
+def pack_slot(slot, cap, me, starts, plan, by_table):
+    n_dev, _, _ = plan.shape
+    _, part, dim = by_table.shape
     return pl.pallas_call(
-        functools.partial(pack_kernel, slot, n_used),
-        out_shape=jax.ShapeDtypeStruct((n_dev, cap, dim), by_table.dtype),
-        in_specs=[pl.BlockSpec(memory_space=pltpu.SMEM), pl.BlockSpec(memory_space=pltpu.VMEM), pl.BlockSpec(memory_space=pl.ANY)],
-        out_specs=pl.BlockSpec(memory_space=pl.ANY),
+        functools.partial(pack_kernel, slot),
+        out_shape=(jax.ShapeDtypeStruct((cap, dim), by_table.dtype),) * n_dev,
+        in_specs=[pl.BlockSpec(memory_space=pltpu.SMEM)] * 2 + [pl.BlockSpec(memory_space=pltpu.VMEM), pl.BlockSpec(memory_space=pl.ANY)],
+        out_specs=(pl.BlockSpec(memory_space=pl.ANY),) * n_dev,
         scratch_shapes=[
-            pltpu.VMEM((n_used, part, dim), by_table.dtype),
+            pltpu.VMEM((n_dev, part, dim), by_table.dtype),
             pltpu.VMEM((cap + BLOCK, dim), jnp.float32),
-            pltpu.VMEM((2, cap, dim), by_table.dtype),
-            pltpu.SemaphoreType.DMA((n_used,)),
-            pltpu.SemaphoreType.DMA((2,)),
+            pltpu.VMEM((n_dev, cap, dim), by_table.dtype),
+            pltpu.SemaphoreType.DMA((n_dev,)),
+            pltpu.SemaphoreType.DMA((n_dev,)),
         ],
         compiler_params=pltpu.CompilerParams(vmem_limit_bytes=VMEM_LIMIT),
-        cost_estimate=pl.CostEstimate(flops=n_used * part * dim * 20, bytes_accessed=n_used * part * dim * 3, transcendentals=0),
-    )(starts, plan, by_table)
-
-
-def apply_kernel(slot, n_carried, ids_ref, lr_ref, grad_ref, tables_ref, accums_ref, *refs):
-    carried_refs, (out_tables_ref, out_accums_ref, *scratch) = refs[:n_carried], refs[n_carried:]
+        cost_estimate=pl.CostEstimate(flops=n_dev * part * dim * 20, bytes_accessed=n_dev * part * dim * 3, transcendentals=0),
+    )(me, starts, plan, by_table)
+
+
+def apply_kernel(slot, n_carried, n_dev, ids_ref, lr_ref, tables_ref, accums_ref, *refs):
+    grad_refs, carried_refs = refs[:n_dev], refs[n_dev:n_dev + n_carried]
+    out_tables_ref, out_accums_ref, *scratch = refs[n_dev + n_carried:]
     banks = scratch[:BANKS]
     stage, table_v, grad_v, sem = scratch[BANKS:]
-    segs, seg_rows, dim = grad_ref.shape
+    segs, seg_rows, dim = grad_v.shape
     n_rows = tables_ref.shape[1]
     id_stride = (ids_ref.shape[1] - BLOCK) // BANKS
-    grad_copy = pltpu.make_async_copy(grad_ref, grad_v, sem.at[0])
+    grad_copies = [pltpu.make_async_copy(ref, grad_v.at[o], sem.at[2 + o]) for o, ref in enumerate(grad_refs)]
     table_copy = pltpu.make_async_copy(tables_ref.at[slot], table_v, sem.at[1])
-    grad_copy.start()
+    for copy in grad_copies:
+        copy.start()
     table_copy.start()
 
     zero = jnp.zeros((BLOCK, dim), jnp.float32)
@@ -160,7 +163,8 @@
     lax.fori_loop(0, n_rows // BLOCK, clear, 0)
     for bank in banks:
         bank[pl.ds(n_rows, 8), :] = zero[:8]
-    grad_copy.wait()
+    for copy in grad_copies:
+        copy.wait()
 
     def widen(i, carry):
         for j in range(segs):
@@ -215,27 +219,32 @@
     pltpu.make_async_copy(table_v, out_tables_ref.at[slot], sem.at[0]).wait()
 
 
-def apply_slot(slot, ids, lr, grad, tables, accums, carried):
+def apply_slot(slot, ids, lr, grads, tables, accums, carried):
     _, n_rows, dim = tables.shape
-    segs, seg_rows, _ = grad.shape
+    segs, (seg_rows, _) = len(grads), grads[0].shape
     return pl.pallas_call(
-        functools.partial(apply_kernel, slot, len(carried)),
+        functools.partial(apply_kernel, slot, len(carried), segs),
         out_shape=tuple(jax.ShapeDtypeStruct(x.shape, x.dtype) for x in (tables, accums)),
         in_specs=[pl.BlockSpec(memory_space=pltpu.SMEM)] * 2
-        + [pl.BlockSpec(memory_space=pl.ANY)] * 2
-        + [pl.BlockSpec(memory_space=pltpu.VMEM)]
+        + [pl.BlockSpec(memory_space=pl.ANY), pl.BlockSpec(memory_space=pltpu.VMEM)]
+        + [pl.BlockSpec(memory_space=pl.ANY)] * segs
         + [pl.BlockSpec(memory_space=pl.ANY), pl.BlockSpec(memory_space=pltpu.VMEM)][:len(carried)],
         out_specs=(pl.BlockSpec(memory_space=pl.ANY), pl.BlockSpec(memory_space=pltpu.VMEM)),
-        input_output_aliases={5: 0} if carried else {},
+        input_output_aliases={4 + segs: 0} if carried else {},
         scratch_shapes=[pltpu.VMEM((n_rows + 8, dim), jnp.float32)] * BANKS + [
             pltpu.VMEM((segs, seg_rows, dim), jnp.float32),
             pltpu.VMEM((n_rows, dim), tables.dtype),
-            pltpu.VMEM((segs, seg_rows, dim), grad.dtype),
-            pltpu.SemaphoreType.DMA((2,)),
+            pltpu.VMEM((segs, seg_rows, dim), grads[0].dtype),
+            pltpu.SemaphoreType.DMA((2 + segs,)),
         ],
         compiler_params=pltpu.CompilerParams(vmem_limit_bytes=VMEM_LIMIT),
         cost_estimate=pl.CostEstimate(flops=n_rows * dim * 400, bytes_accessed=4 * n_rows * dim * 2, transcendentals=0),
-    )(ids, lr, grad, tables, accums, *carried)
+    )(ids, lr, tables, accums, *grads, *carried)
+
+
+def routes(n_dev, n_slots, n_tab, slot, offset):
+    pairs = [(d, (d + offset) % n_dev) for d in range(n_dev)]
+    return [(src, dst) for src, dst in pairs if dst * n_slots + slot < n_tab]
 
 
 def solution(mesh):
@@ -246,7 +255,9 @@
         n_slots, n_rows, _ = tables.shape
         by_table = jnp.transpose(d_pool, (1, 0, 2))
         part = by_table.shape[1]
-        plan_out, *ids = make_plan(row_ids[:, :, 0], lengths, n_group, n_rows)
+        me = lax.axis_index('mp').reshape(1)
+        n_tab = by_table.shape[0]
+        plan_out, *ids = make_plan(me, row_ids[:, :, 0], lengths, n_group, n_rows)
         plan = lax.all_to_all(plan_out, 'mp', 0, 0, tiled=True)
         starts = plan[:, :, part:]
         most = jnp.max(starts[:, :, MAX_LANE])
@@ -255,11 +266,11 @@
 
         def exchange(level):
             def run(operands):
-                by_table, plan, starts, ids, lr, tables, accums = operands
+                me, by_table, plan, starts, ids, lr, tables, accums = operands
                 got = []
                 for k in range(n_slots):
-                    pack = pack_slot(k, caps[level], starts, plan, by_table)
-                    got.append(lax.all_to_all(pack, 'mp', 0, 0, tiled=True))
+                    pack = pack_slot(k, caps[level], me, starts, plan, by_table)
+                    got.append([pack[0]] + [lax.ppermute(pack[o], 'mp', routes(n_group, n_slots, n_tab, k, o)) for o in range(1, n_group)])
                 carried = ()
                 for k in range(n_slots):
                     carried = apply_slot(k, ids[k], lr, got[k], tables, accums, carried)
@@ -268,7 +279,7 @@
             return run
 
         level = sum((most > cap).astype(jnp.int32) for cap in caps[:-1])
-        operands = (by_table, plan, starts, tuple(ids), lr, tables, row_accum)
+        operands = (me, by_table, plan, starts, tuple(ids), lr, tables, row_accum)
         return lax.switch(level, [exchange(i) for i in range(len(caps))], operands)
 
     return jax.shard_map(local_step, mesh=mesh, in_specs=(slot_spec, slot_spec, slot_spec, slot_spec, slot_spec, P()), out_specs=(slot_spec, slot_spec), check_vma=False)

time: 215 us -> 232 us (1.079)
  starting transfers between devices: 20.4 us -> 72.1 us
  waiting for transfers between devices: 70.4 us -> 35.7 us
    ppermute x0 -> x28, starting transfers between devices: none -> 72.1 us  [run(): lax.ppermute(pack[o], 'mp', routes(n_group, n_slots, n_tab, k, o))]
    all_to_all x4 -> x0, waiting for transfers between devices: 70.4 us -> none  [run(): got.append(lax.all_to_all(pack, 'mp', 0, 0, tiled=True))]
    ppermute x0 -> x28, waiting for transfers between devices: none -> 35.7 us  [run(): lax.ppermute(pack[o], 'mp', routes(n_group, n_slots, n_tab, k, o))]
    all_to_all x4 -> x0, starting transfers between devices: 20.4 us -> none  [run(): got.append(lax.all_to_all(pack, 'mp', 0, 0, tiled=True))]
  transfers between devices with their start and end apart: 4 -> 28, of which waited for: 3 -> 7; matrix products, arithmetic and copies ran while one was open for 0% -> 0% of each run, Pallas kernels for 36% -> 33%
where the time goes in v4:
time: 232 us; the launch traced here: 230 us
  Pallas kernels  104 us (45%)
  starting transfers between devices  72.1 us (31%)
  waiting for transfers between devices  35.7 us (15%)
  blocking collectives  13 us (6%)
  local copies, waits for them, and re-layouts  2.7 us (1%)
    pallas_call x4, Pallas kernels, apply_slot(): pl.pallas_call(functools.partial(apply_kernel, slot, len(carried), segs),...  79.8 us
    ppermute x28, starting transfers between devices, run(): lax.ppermute(pack[o], 'mp', routes(n_group, n_slots, n_tab, k, o))  72.1 us
    ppermute x28, waiting for transfers between devices, run(): lax.ppermute(pack[o], 'mp', routes(n_group, n_slots, n_tab, k, o))  35.7 us
    pallas_call x4, Pallas kernels, pack_slot(): pl.pallas_call(functools.partial(pack_kernel, slot), out_shape=(jax.Shape...  23 us
    all_to_all x1, blocking collectives, local_step(): plan = lax.all_to_all(plan_out, 'mp', 0, 0, tiled=True)  13 us
  transfers between devices with their start and end apart: 28, of which 7 were waited for; matrix products, arithmetic and copies ran while one was open for 0% of the time, Pallas kernels for 33%

profile of v4, /device:TPU:81, one launch (start us, length us, event | category | flops | bytes accessed | tf_op | source)
XLA Modules:
  0.0 230.4 jit_solution(8412048240474774612)
XLA Ops:
  0.6 1.1 copy.26
  1.8 0.9 copy-done
  2.7 1.1 shard_map.87
  3.8 13.0 %all_to_all.5 = s32[8,4,2176]{2,1,0:T(4,128)S(1)} all-to-all(s32[8,4,2176]{2,1,0:T(4,128)S(1)} %get-tuple-element.149), channel_id=1, replica_groups=mesh['pod'=4,'mp'=8] {'mp'}, dimensions={0} | all-to-all | bytes 557056 | tf_op jit(solution)/shard_map/all_to_all | solution.py:261
  16.8 0.7 slice_reduce_fusion
  18.2 212.0 %conditional.1 = ((bf16[4,16384,128]{2,1,0:T(8,128)(2,1)}, f32[4,16384]{1,0:T(4,128)})) conditional(s32[]{:T(128)} %clamp.3, (s32[1]{0:T(128)}, s32[8,4,2176]{2,1,0:T(4,128)S(1)}, s32[8,4,2176]{2,1,0:T(4,128)S(1)}, bf16[26,2048,128]{2,1,0:T(8,128)(2,1)}, s32[1,8320]{1,0:T(1,128)S(1)}, /*index=5*/f32[]{:T(128)}, bf16[4,16384,128]{2,1,0:T(8,128)(2,1)}, ...), branch_computations={%region_1.0_spmd, %region_2.0_spmd} | conditional | flops 3523215360 | bytes 152077440 | solution.py:283
  18.8 5.9 %branch_0_fun.11 = (bf16[1152,128]{1,0:T(8,128)(2,1)}, bf16[1152,128]{1,0:T(8,128)(2,1)}, bf16[1152,128]{1,0:T(8,128)(2,1)}, bf16[1152,128]{1,0:T(8,128)(2,1)}, ...) custom-call(s32[1]{0:T(128)} %get-tuple-element.48.me_ref, ...), custom_call_target="tpu_custom_call" | custom-call | flops 41943040 | bytes 6291456 | tf_op jit(solution)/shard_map/cond/branch_0_fun/pallas_call | solution.py:125
  24.8 2.6 %collective-permute-start.21 = (bf16[1152,128]{1,0:T(8,128)(2,1)}, bf16[1152,128]{1,0:T(8,128)(2,1)S(1)}, u32[]{:S(2)}, u32[]{:S(2)}) collective-permute-start(bf16[1152,128]{1,0:T(8,128)(2,1)} %get-tuple-element.80), channel_id=1, source_target_pairs={{0,1},{1,2},{2,3},{3,4},{4,5},{5,6},{7,0},{8,9},{9,10},{10,11},{11... | collective-permute-start | bytes 884744 | tf_op jit(solution)/shard_map/cond/branch_0_fun/ppermute | solution.py:273
  27.4 2.2 collective-permute-start.22
  29.6 3.1 %collective-permute-start.23 = (bf16[1152,128]{1,0:T(8,128)(2,1)}, bf16[1152,128]{1,0:T(8,128)(2,1)}, u32[]{:S(2)}, u32[]{:S(2)}) collective-permute-start(bf16[1152,128]{1,0:T(8,128)(2,1)} %get-tuple-element.82), channel_id=1, source_target_pairs={{0,3},{1,4},{2,5},{3,6},{5,0},{6,1},{7,2},{8,11},{9,12},{10,13},{1... | collective-permute-start | bytes 884744 | tf_op jit(solution)/shard_map/cond/branch_0_fun/ppermute | solution.py:273
  32.7 3.8 %collective-permute-start.24 = (bf16[1152,128]{1,0:T(8,128)(2,1)}, bf16[1152,128]{1,0:T(8,128)(2,1)}, u32[]{:S(2)}, u32[]{:S(2)}) collective-permute-start(bf16[1152,128]{1,0:T(8,128)(2,1)} %get-tuple-element.83), channel_id=1, source_target_pairs={{0,4},{1,5},{2,6},{4,0},{5,1},{6,2},{7,3},{8,12},{9,13},{10,14},{1... | collective-permute-start | bytes 884744 | tf_op jit(solution)/shard_map/cond/branch_0_fun/ppermute | solution.py:273
  36.5 2.4 %collective-permute-start.25 = (bf16[1152,128]{1,0:T(8,128)(2,1)}, bf16[1152,128]{1,0:T(8,128)(2,1)}, u32[]{:S(2)}, u32[]{:S(2)}) collective-permute-start(bf16[1152,128]{1,0:T(8,128)(2,1)} %get-tuple-element.84), channel_id=1, source_target_pairs={{0,5},{1,6},{3,0},{4,1},{5,2},{6,3},{7,4},{8,13},{9,14},{11,8},{12... | collective-permute-start | bytes 884744 | tf_op jit(solution)/shard_map/cond/branch_0_fun/ppermute | solution.py:273
  38.9 5.9 %branch_0_fun.10 = (bf16[1152,128]{1,0:T(8,128)(2,1)}, bf16[1152,128]{1,0:T(8,128)(2,1)}, bf16[1152,128]{1,0:T(8,128)(2,1)}, bf16[1152,128]{1,0:T(8,128)(2,1)}, ...) custom-call(s32[1]{0:T(128)} %get-tuple-element.48.me_ref, ...), custom_call_target="tpu_custom_call" | custom-call | flops 41943040 | bytes 6291456 | tf_op jit(solution)/shard_map/cond/branch_0_fun/pallas_call | solution.py:125
  44.9 1.4 collective-permute-start.26
  46.3 7.4 %collective-permute-done.22.refs_2_ = bf16[1152,128]{1,0:T(8,128)(2,1)} collective-permute-done((bf16[1152,128]{1,0:T(8,128)(2,1)}, bf16[1152,128]{1,0:T(8,128)(2,1)}, u32[]{:S(2)}, u32[]{:S(2)}) %collective-permute-start.22) | collective-permute-done | bytes 294944 | tf_op jit(solution)/shard_map/cond/branch_0_fun/ppermute | solution.py:273
  53.7 1.9 collective-permute-start.27
  56.3 3.1 %collective-permute-start.14 = (bf16[1152,128]{1,0:T(8,128)(2,1)}, bf16[1152,128]{1,0:T(8,128)(2,1)S(1)}, u32[]{:S(2)}, u32[]{:S(2)}) collective-permute-start(bf16[1152,128]{1,0:T(8,128)(2,1)} %get-tuple-element.71), channel_id=1, source_target_pairs={{0,1},{1,2},{2,3},{3,4},{4,5},{5,6},{7,0},{8,9},{9,10},{10,11},{11... | collective-permute-start | bytes 884744 | tf_op jit(solution)/shard_map/cond/branch_0_fun/ppermute | solution.py:273
  59.4 2.0 collective-permute-start.15
  61.3 2.0 collective-permute-start.16
  63.3 5.2 %collective-permute-start.17 = (bf16[1152,128]{1,0:T(8,128)(2,1)}, bf16[1152,128]{1,0:T(8,128)(2,1)}, u32[]{:S(2)}, u32[]{:S(2)}) collective-permute-start(bf16[1152,128]{1,0:T(8,128)(2,1)} %get-tuple-element.74), channel_id=1, source_target_pairs={{0,4},{1,5},{2,6},{4,0},{5,1},{6,2},{7,3},{8,12},{9,13},{10,14},{1... | collective-permute-start | bytes 884744 | tf_op jit(solution)/shard_map/cond/branch_0_fun/ppermute | solution.py:273
  68.5 2.0 collective-permute-start.18
  70.5 1.3 collective-permute-start.19
  71.8 5.6 %branch_0_fun.9 = (bf16[1152,128]{1,0:T(8,128)(2,1)}, bf16[1152,128]{1,0:T(8,128)(2,1)}, bf16[1152,128]{1,0:T(8,128)(2,1)}, bf16[1152,128]{1,0:T(8,128)(2,1)}, b...) custom-call(s32[1]{0:T(128)} %get-tuple-element.48.me_ref, ...), custom_call_target="tpu_custom_call" | custom-call | flops 41943040 | bytes 6291456 | tf_op jit(solution)/shard_map/cond/branch_0_fun/pallas_call | solution.py:125
  77.4 6.8 %collective-permute-done.15.refs_2_ = bf16[1152,128]{1,0:T(8,128)(2,1)} collective-permute-done((bf16[1152,128]{1,0:T(8,128)(2,1)}, bf16[1152,128]{1,0:T(8,128)(2,1)}, u32[]{:S(2)}, u32[]{:S(2)}) %collective-permute-start.15) | collective-permute-done | bytes 294944 | tf_op jit(solution)/shard_map/cond/branch_0_fun/ppermute | solution.py:273
  84.2 2.3 collective-permute-start.20
  86.5 0.7 collective-permute-done.16.refs_3_
  87.2 1.9 collective-permute-start.10
  89.1 1.3 collective-permute-start.11
  90.5 1.3 collective-permute-start.12
  91.8 5.9 %collective-permute-start.13 = (bf16[1152,128]{1,0:T(8,128)(2,1)}, bf16[1152,128]{1,0:T(8,128)(2,1)}, u32[]{:S(2)}, u32[]{:S(2)}) collective-permute-start(bf16[1152,128]{1,0:T(8,128)(2,1)} %get-tuple-element.68), channel_id=1, source_target_pairs={{1,0},{2,1},{3,2},{4,3},{5,4},{6,5},{9,8},{10,9},{11,10},{12,11},{... | collective-permute-start | bytes 884744 | tf_op jit(solution)/shard_map/cond/branch_0_fun/ppermute | solution.py:273
  97.7 5.5 %branch_0_fun.8 = (bf16[1152,128]{1,0:T(8,128)(2,1)}, bf16[1152,128]{1,0:T(8,128)(2,1)}, bf16[1152,128]{1,0:T(8,128)(2,1)}, bf16[1152,128]{1,0:T(8,128)(2,1)}, b...) custom-call(s32[1]{0:T(128)} %get-tuple-element.48.me_ref, ...), custom_call_target="tpu_custom_call" | custom-call | flops 41943040 | bytes 6291456 | tf_op jit(solution)/shard_map/cond/branch_0_fun/pallas_call | solution.py:125
  103.3 4.2 %collective-permute-start.7 = (bf16[1152,128]{1,0:T(8,128)(2,1)}, bf16[1152,128]{1,0:T(8,128)(2,1)}, u32[]{:S(2)}, u32[]{:S(2)}) collective-permute-start(bf16[1152,128]{1,0:T(8,128)(2,1)} %get-tuple-element.62), channel_id=1, source_target_pairs={{0,1},{1,2},{2,3},{3,4},{4,5},{7,0},{8,9},{9,10},{10,11},{11,12},{... | collective-permute-start | bytes 884744 | tf_op jit(solution)/shard_map/cond/branch_0_fun/ppermute | solution.py:273
  107.5 2.0 collective-permute-start.8
  109.6 2.0 collective-permute-start.9
  111.6 2.3 %collective-permute-start = (bf16[1152,128]{1,0:T(8,128)(2,1)}, bf16[1152,128]{1,0:T(8,128)(2,1)}, u32[]{:S(2)}, u32[]{:S(2)}) collective-permute-start(bf16[1152,128]{1,0:T(8,128)(2,1)} %get-tuple-element.53), channel_id=1, source_target_pairs={{0,1},{1,2},{2,3},{3,4},{4,5},{7,0},{8,9},{9,10},{10,11},{11,12},{... | collective-permute-start | bytes 884744 | tf_op jit(solution)/shard_map/cond/branch_0_fun/ppermute | solution.py:273
  113.9 5.4 %collective-permute-start.1 = (bf16[1152,128]{1,0:T(8,128)(2,1)}, bf16[1152,128]{1,0:T(8,128)(2,1)}, u32[]{:S(2)}, u32[]{:S(2)}) collective-permute-start(bf16[1152,128]{1,0:T(8,128)(2,1)} %get-tuple-element.54), channel_id=1, source_target_pairs={{0,2},{1,3},{2,4},{3,5},{6,0},{7,1},{8,10},{9,11},{10,12},{11,13},... | collective-permute-start | bytes 884744 | tf_op jit(solution)/shard_map/cond/branch_0_fun/ppermute | solution.py:273
  119.3 2.0 collective-permute-start.2
  121.3 1.6 collective-permute-done.8.refs_2_
  122.9 4.0 %collective-permute-start.3 = (bf16[1152,128]{1,0:T(8,128)(2,1)}, bf16[1152,128]{1,0:T(8,128)(2,1)}, u32[]{:S(2)}, u32[]{:S(2)}) collective-permute-start(bf16[1152,128]{1,0:T(8,128)(2,1)} %get-tuple-element.56), channel_id=1, source_target_pairs={{0,4},{1,5},{4,0},{5,1},{6,2},{7,3},{8,12},{9,13},{12,8},{13,9},{1... | collective-permute-start | bytes 884744 | tf_op jit(solution)/shard_map/cond/branch_0_fun/ppermute | solution.py:273
  126.9 9.5 %collective-permute-done.9.refs_3_ = bf16[1152,128]{1,0:T(8,128)(2,1)} collective-permute-done((bf16[1152,128]{1,0:T(8,128)(2,1)}, bf16[1152,128]{1,0:T(8,128)(2,1)}, u32[]{:S(2)}, u32[]{:S(2)}) %collective-permute-start.9) | collective-permute-done | bytes 294944 | tf_op jit(solution)/shard_map/cond/branch_0_fun/ppermute | solution.py:273
  136.3 1.3 collective-permute-start.4
  137.6 1.3 collective-permute-start.5
  139.0 9.2 %collective-permute-done.1.refs_2_ = bf16[1152,128]{1,0:T(8,128)(2,1)} collective-permute-done((bf16[1152,128]{1,0:T(8,128)(2,1)}, bf16[1152,128]{1,0:T(8,128)(2,1)}, u32[]{:S(2)}, u32[]{:S(2)}) %collective-permute-start.1) | collective-permute-done | bytes 294944 | tf_op jit(solution)/shard_map/cond/branch_0_fun/ppermute | solution.py:273
  148.1 1.9 collective-permute-start.6
  150.1 20.0 %branch_0_fun.12 = (bf16[4,16384,128]{2,1,0:T(8,128)(2,1)}, f32[4,16384]{1,0:T(4,128)}) custom-call(s32[1,8320]{1,0:T(1,128)S(1)} %get-tuple-element.78.ids_ref, f32[1]{0:T(128)} %bitcast.lr_ref, bf16[4,16384,128]{2,1,0:T(8,128)(2,1)} %get-tuple-element.170.tables_ref, f32[4,16384]{1,0:T(4,128)S(1)} %copy-done.1, ...), custom_call_target="tpu_custom_call" | custom-call | flops 838860800 | bytes 16777216 | tf_op jit(solution)/shard_map/cond/branch_0_fun/pallas_call | solution.py:225
  170.1 20.0 %branch_0_fun.13 = (bf16[4,16384,128]{2,1,0:T(8,128)(2,1)}, f32[4,16384]{1,0:T(4,128)}) custom-call(s32[1,8320]{1,0:T(1,128)S(1)} %get-tuple-element.69.ids_ref, f32[1]{0:T(128)} %bitcast.lr_ref, bf16[4,16384,128]{2,1,0:T(8,128)(2,1)} %get-tuple-element.170.tables_ref, f32[4,16384]{1,0:T(4,128)S(1)} %copy-done.1, ...), custom_call_target="tpu_custom_call", output_to_operand_aliasing={{0}: (12, {})} | custom-call | flops 838860800 | bytes 16777216 | tf_op jit(solution)/shard_map/cond/branch_0_fun/pallas_call | solution.py:225
  190.0 20.0 %branch_0_fun.14 = (bf16[4,16384,128]{2,1,0:T(8,128)(2,1)}, f32[4,16384]{1,0:T(4,128)}) custom-call(s32[1,8320]{1,0:T(1,128)S(1)} %get-tuple-element.60.ids_ref, f32[1]{0:T(128)} %bitcast.lr_ref, bf16[4,16384,128]{2,1,0:T(8,128)(2,1)} %get-tuple-element.170.tables_ref, f32[4,16384]{1,0:T(4,128)S(1)} %copy-done.1, ...), custom_call_target="tpu_custom_call", output_to_operand_aliasing={{0}: (12, {})} | custom-call | flops 838860800 | bytes 16777216 | tf_op jit(solution)/shard_map/cond/branch_0_fun/pallas_call | solution.py:225
  210.1 19.9 %branch_0_fun.15 = (bf16[4,16384,128]{2,1,0:T(8,128)(2,1)}, f32[4,16384]{1,0:T(4,128)}) custom-call(s32[1,8320]{1,0:T(1,128)S(1)} %get-tuple-element.44.ids_ref, f32[1]{0:T(128)} %bitcast.lr_ref, bf16[4,16384,128]{2,1,0:T(8,128)(2,1)} %get-tuple-element.170.tables_ref, f32[4,16384]{1,0:T(4,128)S(1)} %copy-done.1, ...), custom_call_target="tpu_custom_call", output_to_operand_aliasing={{0}: (12, {})} | custom-call | flops 838860800 | bytes 16777216 | tf_op jit(solution)/shard_map/cond/branch_0_fun/pallas_call | solution.py:225
  (34 shorter events, 1.3 us)
Async XLA Ops:
  1.8 1.0 copy-start
  24.8 20.1 %collective-permute-start.21 = (bf16[1152,128]{1,0:T(8,128)(2,1)}, bf16[1152,128]{1,0:T(8,128)(2,1)S(1)}, u32[]{:S(2)}, u32[]{:S(2)}) collective-permute-start(bf16[1152,128]{1,0:T(8,128)(2,1)} %get-tuple-element.80), channel_id=1, source_target_pairs={{0,1},{1,2},{2,3},{3,4},{4,5},{5,6},{7,0},{8,9},{9,10},{10,11},{11... | collective-permute-start | bytes 884744 | tf_op jit(solution)/shard_map/cond/branch_0_fun/ppermute | solution.py:273
  27.4 26.3 %collective-permute-start.22 = (bf16[1152,128]{1,0:T(8,128)(2,1)}, bf16[1152,128]{1,0:T(8,128)(2,1)}, u32[]{:S(2)}, u32[]{:S(2)}) collective-permute-start(bf16[1152,128]{1,0:T(8,128)(2,1)} %get-tuple-element.81), channel_id=1, source_target_pairs={{0,2},{1,3},{2,4},{3,5},{4,6},{6,0},{7,1},{8,10},{9,11},{10,12},{1... | collective-permute-start | bytes 884744 | tf_op jit(solution)/shard_map/cond/branch_0_fun/ppermute | solution.py:273
  29.6 26.7 %collective-permute-start.23 = (bf16[1152,128]{1,0:T(8,128)(2,1)}, bf16[1152,128]{1,0:T(8,128)(2,1)}, u32[]{:S(2)}, u32[]{:S(2)}) collective-permute-start(bf16[1152,128]{1,0:T(8,128)(2,1)} %get-tuple-element.82), channel_id=1, source_target_pairs={{0,3},{1,4},{2,5},{3,6},{5,0},{6,1},{7,2},{8,11},{9,12},{10,13},{1... | collective-permute-start | bytes 884744 | tf_op jit(solution)/shard_map/cond/branch_0_fun/ppermute | solution.py:273
  32.7 26.7 %collective-permute-start.24 = (bf16[1152,128]{1,0:T(8,128)(2,1)}, bf16[1152,128]{1,0:T(8,128)(2,1)}, u32[]{:S(2)}, u32[]{:S(2)}) collective-permute-start(bf16[1152,128]{1,0:T(8,128)(2,1)} %get-tuple-element.83), channel_id=1, source_target_pairs={{0,4},{1,5},{2,6},{4,0},{5,1},{6,2},{7,3},{8,12},{9,13},{10,14},{1... | collective-permute-start | bytes 884744 | tf_op jit(solution)/shard_map/cond/branch_0_fun/ppermute | solution.py:273
  36.5 24.9 %collective-permute-start.25 = (bf16[1152,128]{1,0:T(8,128)(2,1)}, bf16[1152,128]{1,0:T(8,128)(2,1)}, u32[]{:S(2)}, u32[]{:S(2)}) collective-permute-start(bf16[1152,128]{1,0:T(8,128)(2,1)} %get-tuple-element.84), channel_id=1, source_target_pairs={{0,5},{1,6},{3,0},{4,1},{5,2},{6,3},{7,4},{8,13},{9,14},{11,8},{12... | collective-permute-start | bytes 884744 | tf_op jit(solution)/shard_map/cond/branch_0_fun/ppermute | solution.py:273
  44.9 105.2 %copy-start.1 = (f32[4,16384]{1,0:T(4,128)S(1)}, f32[4,16384]{1,0:T(4,128)}, u32[]{:S(2)}) copy-start(f32[4,16384]{1,0:T(4,128)} %get-tuple-element.172.accums_ref) | copy-start | bytes 786436 | tf_op jit(solution)/shard_map/cond
  44.9 11.4 %copy-start.4 = (bf16[1152,128]{1,0:T(8,128)(2,1)}, bf16[1152,128]{1,0:T(8,128)(2,1)S(1)}, u32[]{:S(2)}) copy-start(bf16[1152,128]{1,0:T(8,128)(2,1)S(1)} %collective-permute-done.21.refs_1_) | copy-start | bytes 884740 | tf_op jit(solution)/shard_map/cond
  44.9 18.4 %collective-permute-start.26 = (bf16[1152,128]{1,0:T(8,128)(2,1)}, bf16[1152,128]{1,0:T(8,128)(2,1)S(1)}, u32[]{:S(2)}, u32[]{:S(2)}) collective-permute-start(bf16[1152,128]{1,0:T(8,128)(2,1)} %get-tuple-element.85), channel_id=1, source_target_pairs={{0,6},{2,0},{3,1},{4,2},{5,3},{6,4},{7,5},{8,14},{10,8},{11,9},{12... | collective-permute-start | bytes 884744 | tf_op jit(solution)/shard_map/cond/branch_0_fun/ppermute | solution.py:273
  53.7 14.8 %collective-permute-start.27 = (bf16[1152,128]{1,0:T(8,128)(2,1)}, bf16[1152,128]{1,0:T(8,128)(2,1)S(1)}, u32[]{:S(2)}, u32[]{:S(2)}) collective-permute-start(bf16[1152,128]{1,0:T(8,128)(2,1)} %get-tuple-element.86), channel_id=1, source_target_pairs={{1,0},{2,1},{3,2},{4,3},{5,4},{6,5},{7,6},{9,8},{10,9},{11,10},{12... | collective-permute-start | bytes 884744 | tf_op jit(solution)/shard_map/cond/branch_0_fun/ppermute | solution.py:273
  56.3 14.2 %collective-permute-start.14 = (bf16[1152,128]{1,0:T(8,128)(2,1)}, bf16[1152,128]{1,0:T(8,128)(2,1)S(1)}, u32[]{:S(2)}, u32[]{:S(2)}) collective-permute-start(bf16[1152,128]{1,0:T(8,128)(2,1)} %get-tuple-element.71), channel_id=1, source_target_pairs={{0,1},{1,2},{2,3},{3,4},{4,5},{5,6},{7,0},{8,9},{9,10},{10,11},{11... | collective-permute-start | bytes 884744 | tf_op jit(solution)/shard_map/cond/branch_0_fun/ppermute | solution.py:273
  59.4 24.8 %collective-permute-start.15 = (bf16[1152,128]{1,0:T(8,128)(2,1)}, bf16[1152,128]{1,0:T(8,128)(2,1)}, u32[]{:S(2)}, u32[]{:S(2)}) collective-permute-start(bf16[1152,128]{1,0:T(8,128)(2,1)} %get-tuple-element.72), channel_id=1, source_target_pairs={{0,2},{1,3},{2,4},{3,5},{4,6},{6,0},{7,1},{8,10},{9,11},{10,12},{1... | collective-permute-start | bytes 884744 | tf_op jit(solution)/shard_map/cond/branch_0_fun/ppermute | solution.py:273
  61.3 25.8 %collective-permute-start.16 = (bf16[1152,128]{1,0:T(8,128)(2,1)}, bf16[1152,128]{1,0:T(8,128)(2,1)}, u32[]{:S(2)}, u32[]{:S(2)}) collective-permute-start(bf16[1152,128]{1,0:T(8,128)(2,1)} %get-tuple-element.73), channel_id=1, source_target_pairs={{0,3},{1,4},{2,5},{3,6},{5,0},{6,1},{7,2},{8,11},{9,12},{10,13},{1... | collective-permute-start | bytes 884744 | tf_op jit(solution)/shard_map/cond/branch_0_fun/ppermute | solution.py:273
  63.3 7.2 %copy-start.5 = (bf16[1152,128]{1,0:T(8,128)(2,1)}, bf16[1152,128]{1,0:T(8,128)(2,1)S(1)}, u32[]{:S(2)}) copy-start(bf16[1152,128]{1,0:T(8,128)(2,1)S(1)} %collective-permute-done.26.refs_6_) | copy-start | bytes 884740 | tf_op jit(solution)/shard_map/cond
  63.3 25.8 %collective-permute-start.17 = (bf16[1152,128]{1,0:T(8,128)(2,1)}, bf16[1152,128]{1,0:T(8,128)(2,1)}, u32[]{:S(2)}, u32[]{:S(2)}) collective-permute-start(bf16[1152,128]{1,0:T(8,128)(2,1)} %get-tuple-element.74), channel_id=1, source_target_pairs={{0,4},{1,5},{2,6},{4,0},{5,1},{6,2},{7,3},{8,12},{9,13},{10,14},{1... | collective-permute-start | bytes 884744 | tf_op jit(solution)/shard_map/cond/branch_0_fun/ppermute | solution.py:273
  68.5 2.0 copy-start.6
  68.5 21.9 %collective-permute-start.18 = (bf16[1152,128]{1,0:T(8,128)(2,1)}, bf16[1152,128]{1,0:T(8,128)(2,1)}, u32[]{:S(2)}, u32[]{:S(2)}) collective-permute-start(bf16[1152,128]{1,0:T(8,128)(2,1)} %get-tuple-element.75), channel_id=1, source_target_pairs={{0,5},{1,6},{3,0},{4,1},{5,2},{6,3},{7,4},{8,13},{9,14},{11,8},{12... | collective-permute-start | bytes 884744 | tf_op jit(solution)/shard_map/cond/branch_0_fun/ppermute | solution.py:273
  70.5 99.6 %copy-start.3 = (bf16[1152,128]{1,0:T(8,128)(2,1)}, bf16[1152,128]{1,0:T(8,128)(2,1)S(1)}, u32[]{:S(2)}) copy-start(bf16[1152,128]{1,0:T(8,128)(2,1)S(1)} %collective-permute-done.14.refs_1_) | copy-start | bytes 884740 | tf_op jit(solution)/shard_map/cond
  70.5 21.2 %collective-permute-start.19 = (bf16[1152,128]{1,0:T(8,128)(2,1)}, bf16[1152,128]{1,0:T(8,128)(2,1)}, u32[]{:S(2)}, u32[]{:S(2)}) collective-permute-start(bf16[1152,128]{1,0:T(8,128)(2,1)} %get-tuple-element.76), channel_id=1, source_target_pairs={{0,6},{2,0},{3,1},{4,2},{5,3},{6,4},{7,5},{8,14},{10,8},{11,9},{12... | collective-permute-start | bytes 884744 | tf_op jit(solution)/shard_map/cond/branch_0_fun/ppermute | solution.py:273
  84.2 19.1 %collective-permute-start.20 = (bf16[1152,128]{1,0:T(8,128)(2,1)}, bf16[1152,128]{1,0:T(8,128)(2,1)}, u32[]{:S(2)}, u32[]{:S(2)}) collective-permute-start(bf16[1152,128]{1,0:T(8,128)(2,1)} %get-tuple-element.77), channel_id=1, source_target_pairs={{1,0},{2,1},{3,2},{4,3},{5,4},{6,5},{7,6},{9,8},{10,9},{11,10},{12... | collective-permute-start | bytes 884744 | tf_op jit(solution)/shard_map/cond/branch_0_fun/ppermute | solution.py:273
  87.2 20.3 %collective-permute-start.10 = (bf16[1152,128]{1,0:T(8,128)(2,1)}, bf16[1152,128]{1,0:T(8,128)(2,1)}, u32[]{:S(2)}, u32[]{:S(2)}) collective-permute-start(bf16[1152,128]{1,0:T(8,128)(2,1)} %get-tuple-element.65), channel_id=1, source_target_pairs={{0,4},{1,5},{4,0},{5,1},{6,2},{7,3},{8,12},{9,13},{12,8},{13,9},{1... | collective-permute-start | bytes 884744 | tf_op jit(solution)/shard_map/cond/branch_0_fun/ppermute | solution.py:273
  89.1 20.4 %collective-permute-start.11 = (bf16[1152,128]{1,0:T(8,128)(2,1)}, bf16[1152,128]{1,0:T(8,128)(2,1)}, u32[]{:S(2)}, u32[]{:S(2)}) collective-permute-start(bf16[1152,128]{1,0:T(8,128)(2,1)} %get-tuple-element.66), channel_id=1, source_target_pairs={{0,5},{3,0},{4,1},{5,2},{6,3},{7,4},{8,13},{11,8},{12,9},{13,10},{... | collective-permute-start | bytes 884744 | tf_op jit(solution)/shard_map/cond/branch_0_fun/ppermute | solution.py:273
  90.5 21.1 %collective-permute-start.12 = (bf16[1152,128]{1,0:T(8,128)(2,1)}, bf16[1152,128]{1,0:T(8,128)(2,1)}, u32[]{:S(2)}, u32[]{:S(2)}) collective-permute-start(bf16[1152,128]{1,0:T(8,128)(2,1)} %get-tuple-element.67), channel_id=1, source_target_pairs={{2,0},{3,1},{4,2},{5,3},{6,4},{7,5},{10,8},{11,9},{12,10},{13,11},... | collective-permute-start | bytes 884744 | tf_op jit(solution)/shard_map/cond/branch_0_fun/ppermute | solution.py:273
  91.8 22.1 %collective-permute-start.13 = (bf16[1152,128]{1,0:T(8,128)(2,1)}, bf16[1152,128]{1,0:T(8,128)(2,1)}, u32[]{:S(2)}, u32[]{:S(2)}) collective-permute-start(bf16[1152,128]{1,0:T(8,128)(2,1)} %get-tuple-element.68), channel_id=1, source_target_pairs={{1,0},{2,1},{3,2},{4,3},{5,4},{6,5},{9,8},{10,9},{11,10},{12,11},{... | collective-permute-start | bytes 884744 | tf_op jit(solution)/shard_map/cond/branch_0_fun/ppermute | solution.py:273
  103.3 16.0 %collective-permute-start.7 = (bf16[1152,128]{1,0:T(8,128)(2,1)}, bf16[1152,128]{1,0:T(8,128)(2,1)}, u32[]{:S(2)}, u32[]{:S(2)}) collective-permute-start(bf16[1152,128]{1,0:T(8,128)(2,1)} %get-tuple-element.62), channel_id=1, source_target_pairs={{0,1},{1,2},{2,3},{3,4},{4,5},{7,0},{8,9},{9,10},{10,11},{11,12},{... | collective-permute-start | bytes 884744 | tf_op jit(solution)/shard_map/cond/branch_0_fun/ppermute | solution.py:273
  107.5 15.3 %collective-permute-start.8 = (bf16[1152,128]{1,0:T(8,128)(2,1)}, bf16[1152,128]{1,0:T(8,128)(2,1)}, u32[]{:S(2)}, u32[]{:S(2)}) collective-permute-start(bf16[1152,128]{1,0:T(8,128)(2,1)} %get-tuple-element.63), channel_id=1, source_target_pairs={{0,2},{1,3},{2,4},{3,5},{6,0},{7,1},{8,10},{9,11},{10,12},{11,13},... | collective-permute-start | bytes 884744 | tf_op jit(solution)/shard_map/cond/branch_0_fun/ppermute | solution.py:273
  109.6 26.7 %collective-permute-start.9 = (bf16[1152,128]{1,0:T(8,128)(2,1)}, bf16[1152,128]{1,0:T(8,128)(2,1)}, u32[]{:S(2)}, u32[]{:S(2)}) collective-permute-start(bf16[1152,128]{1,0:T(8,128)(2,1)} %get-tuple-element.64), channel_id=1, source_target_pairs={{0,3},{1,4},{2,5},{5,0},{6,1},{7,2},{8,11},{9,12},{10,13},{13,8},{... | collective-permute-start | bytes 884744 | tf_op jit(solution)/shard_map/cond/branch_0_fun/ppermute | solution.py:273
  111.6 26.1 %collective-permute-start = (bf16[1152,128]{1,0:T(8,128)(2,1)}, bf16[1152,128]{1,0:T(8,128)(2,1)}, u32[]{:S(2)}, u32[]{:S(2)}) collective-permute-start(bf16[1152,128]{1,0:T(8,128)(2,1)} %get-tuple-element.53), channel_id=1, source_target_pairs={{0,1},{1,2},{2,3},{3,4},{4,5},{7,0},{8,9},{9,10},{10,11},{11,12},{... | collective-permute-start | bytes 884744 | tf_op jit(solution)/shard_map/cond/branch_0_fun/ppermute | solution.py:273
  113.9 34.2 %collective-permute-start.1 = (bf16[1152,128]{1,0:T(8,128)(2,1)}, bf16[1152,128]{1,0:T(8,128)(2,1)}, u32[]{:S(2)}, u32[]{:S(2)}) collective-permute-start(bf16[1152,128]{1,0:T(8,128)(2,1)} %get-tuple-element.54), channel_id=1, source_target_pairs={{0,2},{1,3},{2,4},{3,5},{6,0},{7,1},{8,10},{9,11},{10,12},{11,13},... | collective-permute-start | bytes 884744 | tf_op jit(solution)/shard_map/cond/branch_0_fun/ppermute | solution.py:273
  119.3 90.7 %collective-permute-start.2 = (bf16[1152,128]{1,0:T(8,128)(2,1)}, bf16[1152,128]{1,0:T(8,128)(2,1)}, u32[]{:S(2)}, u32[]{:S(2)}) collective-permute-start(bf16[1152,128]{1,0:T(8,128)(2,1)} %get-tuple-element.55), channel_id=1, source_target_pairs={{0,3},{1,4},{2,5},{5,0},{6,1},{7,2},{8,11},{9,12},{10,13},{13,8},{... | collective-permute-start | bytes 884744 | tf_op jit(solution)/shard_map/cond/branch_0_fun/ppermute | solution.py:273
  122.9 87.2 %collective-permute-start.3 = (bf16[1152,128]{1,0:T(8,128)(2,1)}, bf16[1152,128]{1,0:T(8,128)(2,1)}, u32[]{:S(2)}, u32[]{:S(2)}) collective-permute-start(bf16[1152,128]{1,0:T(8,128)(2,1)} %get-tuple-element.56), channel_id=1, source_target_pairs={{0,4},{1,5},{4,0},{5,1},{6,2},{7,3},{8,12},{9,13},{12,8},{13,9},{1... | collective-permute-start | bytes 884744 | tf_op jit(solution)/shard_map/cond/branch_0_fun/ppermute | solution.py:273
  136.3 73.7 %collective-permute-start.4 = (bf16[1152,128]{1,0:T(8,128)(2,1)}, bf16[1152,128]{1,0:T(8,128)(2,1)}, u32[]{:S(2)}, u32[]{:S(2)}) collective-permute-start(bf16[1152,128]{1,0:T(8,128)(2,1)} %get-tuple-element.57), channel_id=1, source_target_pairs={{0,5},{3,0},{4,1},{5,2},{6,3},{7,4},{8,13},{11,8},{12,9},{13,10},{... | collective-permute-start | bytes 884744 | tf_op jit(solution)/shard_map/cond/branch_0_fun/ppermute | solution.py:273
  137.6 72.4 %collective-permute-start.5 = (bf16[1152,128]{1,0:T(8,128)(2,1)}, bf16[1152,128]{1,0:T(8,128)(2,1)}, u32[]{:S(2)}, u32[]{:S(2)}) collective-permute-start(bf16[1152,128]{1,0:T(8,128)(2,1)} %get-tuple-element.58), channel_id=1, source_target_pairs={{2,0},{3,1},{4,2},{5,3},{6,4},{7,5},{10,8},{11,9},{12,10},{13,11},... | collective-permute-start | bytes 884744 | tf_op jit(solution)/shard_map/cond/branch_0_fun/ppermute | solution.py:273
  148.1 61.9 %collective-permute-start.6 = (bf16[1152,128]{1,0:T(8,128)(2,1)}, bf16[1152,128]{1,0:T(8,128)(2,1)}, u32[]{:S(2)}, u32[]{:S(2)}) collective-permute-start(bf16[1152,128]{1,0:T(8,128)(2,1)} %get-tuple-element.59), channel_id=1, source_target_pairs={{1,0},{2,1},{3,2},{4,3},{5,4},{6,5},{9,8},{10,9},{11,10},{12,11},{... | collective-permute-start | bytes 884744 | tf_op jit(solution)/shard_map/cond/branch_0_fun/ppermute | solution.py:273

commit v5 on v3

--- a/solution.py
+++ b/solution.py
@@ -80,72 +80,116 @@
     )(ids, lengths)
 
 
-def pack_kernel(slot, n_used, starts_ref, plan_ref, tables_ref, out_ref, grad_v, stage, pack_v, in_sem, out_sem):
-    _, cap, _ = out_ref.shape
+def share_kernel(n_dev, plan_ref, plans_ref, starts_ref, most_ref, send_sem, recv_sem, own_sem):
+    pod, me = lax.axis_index('pod'), lax.axis_index('mp')
+    barrier = pltpu.get_barrier_semaphore()
+    for o in range(1, n_dev):
+        pl.semaphore_signal(barrier, inc=1, device_id=(pod, (me + o) % n_dev), device_id_type=pl.DeviceIdType.MESH)
+    pl.semaphore_wait(barrier, n_dev - 1)
+    copies = [
+        pltpu.make_async_remote_copy(
+            src_ref=plan_ref.at[(me + o) % n_dev],
+            dst_ref=plans_ref.at[me],
+            send_sem=send_sem.at[o],
+            recv_sem=recv_sem.at[o],
+            device_id=(pod, (me + o) % n_dev),
+            device_id_type=pl.DeviceIdType.MESH,
+        )
+        for o in range(1, n_dev)
+    ]
+    for copy in copies:
+        copy.start()
+    own = pltpu.make_async_copy(plan_ref.at[me], plans_ref.at[me], own_sem)
+    own.start()
+    own.wait()
+    for copy in copies:
+        copy.wait()
+    part = plans_ref.shape[2] - BLOCK
+    starts = plans_ref[:, :, part:]
+    starts_ref[...] = starts
+    most_ref[0] = jnp.max(starts[:, :, MAX_LANE:MAX_LANE + 1])
+
+
+def share_plan(plan):
+    n_dev, n_slots, _ = plan.shape
+    return pl.pallas_call(
+        functools.partial(share_kernel, n_dev),
+        out_shape=(
+            jax.ShapeDtypeStruct(plan.shape, plan.dtype),
+            jax.ShapeDtypeStruct((n_dev, n_slots, BLOCK), plan.dtype),
+            jax.ShapeDtypeStruct((1,), plan.dtype),
+        ),
+        in_specs=[pl.BlockSpec(memory_space=pltpu.VMEM)],
+        out_specs=(pl.BlockSpec(memory_space=pltpu.VMEM), pl.BlockSpec(memory_space=pltpu.VMEM), pl.BlockSpec(memory_space=pltpu.SMEM)),
+        scratch_shapes=[pltpu.SemaphoreType.DMA((n_dev,)), pltpu.SemaphoreType.DMA((n_dev,)), pltpu.SemaphoreType.DMA],
+        compiler_params=pltpu.CompilerParams(collective_id=0, has_side_effects=True, vmem_limit_bytes=16000000),
+        cost_estimate=pl.CostEstimate(flops=20000000, bytes_accessed=2000000, transcendentals=0),
+    )(plan)
+
+
+def pack_kernel(slots, starts_ref, plan_ref, tables_ref, out_ref, grad_v, stage, pack_v, in_sem, out_sem):
     n_slots = plan_ref.shape[1]
-    part = tables_ref.shape[1]
+    cap = out_ref.shape[2]
+    n_tab, part, _ = tables_ref.shape
     slot_row = lax.broadcasted_iota(jnp.int32, (BLOCK, BLOCK), 0)
-
-    def fetch(d, buf):
-        return pltpu.make_async_copy(tables_ref.at[d * n_slots + slot], grad_v.at[buf], in_sem.at[buf])
-
-    def emit(d, buf):
-        return pltpu.make_async_copy(pack_v.at[buf], out_ref.at[d], out_sem.at[buf])
-
-    for d in range(n_used):
-        fetch(d, d).start()
-
-    def table(d, carry):
-        buf = d % 2
-        fetch(d, d).wait()
-
-        @pl.when(d >= 2)
-        def _():
-            emit(d - 2, buf).wait()
-
-        for b in range(part // BLOCK):
-            place = plan_ref[d, slot:slot + 1, b * BLOCK:(b + 1) * BLOCK]
-            pick = jnp.where(slot_row == place, 1.0, 0.0).astype(jnp.bfloat16)
-            rows = jnp.dot(pick, grad_v[d, b * BLOCK:(b + 1) * BLOCK, :], preferred_element_type=jnp.float32)
-            stage[pl.ds(starts_ref[d, slot, b], BLOCK), :] = rows
-        pack_v[buf] = stage[:cap, :].astype(jnp.bfloat16)
-        emit(d, buf).start()
-        return carry
-
-    lax.fori_loop(0, n_used, table, 0)
-    for d in range(max(n_used - 2, 0), n_used):
-        emit(d, d % 2).wait()
-
-
-def pack_slot(slot, cap, starts, plan, by_table):
-    n_dev, n_slots, _ = plan.shape
-    n_tab, part, dim = by_table.shape
-    n_used = len(range(slot, n_tab, n_slots))
+    used = [[d for d in range(out_ref.shape[0]) if d * n_slots + slot < n_tab] for slot in slots]
+
+    def fetch(i, d):
+        return pltpu.make_async_copy(tables_ref.at[d * n_slots + slots[i]], grad_v.at[i, d], in_sem.at[i, d])
+
+    def emit(i, d):
+        return pltpu.make_async_copy(pack_v.at[i, d], out_ref.at[d, i], out_sem.at[i, d])
+
+    for i, dests in enumerate(used):
+        for d in dests:
+            fetch(i, d).start()
+    for i, dests in enumerate(used):
+        def table(d, carry):
+            fetch(i, d).wait()
+            for b in range(part // BLOCK):
+                place = plan_ref[d, slots[i]:slots[i] + 1, b * BLOCK:(b + 1) * BLOCK]
+                pick = jnp.where(slot_row == place, 1.0, 0.0).astype(jnp.bfloat16)
+                rows = jnp.dot(pick, grad_v[i, d, b * BLOCK:(b + 1) * BLOCK, :], preferred_element_type=jnp.float32)
+                stage[pl.ds(starts_ref[d, slots[i], b], BLOCK), :] = rows
+            pack_v[i, d] = stage[:cap, :].astype(jnp.bfloat16)
+            emit(i, d).start()
+            return carry
+
+        lax.fori_loop(0, len(dests), table, 0)
+    for i, dests in enumerate(used):
+        for d in dests:
+            emit(i, d).wait()
+
+
+def pack_slots(slots, cap, starts, plan, by_table):
+    n_dev = plan.shape[0]
+    _, part, dim = by_table.shape
+    n = len(slots)
     return pl.pallas_call(
-        functools.partial(pack_kernel, slot, n_used),
-        out_shape=jax.ShapeDtypeStruct((n_dev, cap, dim), by_table.dtype),
+        functools.partial(pack_kernel, slots),
+        out_shape=jax.ShapeDtypeStruct((n_dev, n, cap, dim), by_table.dtype),
         in_specs=[pl.BlockSpec(memory_space=pltpu.SMEM), pl.BlockSpec(memory_space=pltpu.VMEM), pl.BlockSpec(memory_space=pl.ANY)],
         out_specs=pl.BlockSpec(memory_space=pl.ANY),
         scratch_shapes=[
-            pltpu.VMEM((n_used, part, dim), by_table.dtype),
+            pltpu.VMEM((n, n_dev, part, dim), by_table.dtype),
             pltpu.VMEM((cap + BLOCK, dim), jnp.float32),
-            pltpu.VMEM((2, cap, dim), by_table.dtype),
-            pltpu.SemaphoreType.DMA((n_used,)),
-            pltpu.SemaphoreType.DMA((2,)),
+            pltpu.VMEM((n, n_dev, cap, dim), by_table.dtype),
+            pltpu.SemaphoreType.DMA((n, n_dev)),
+            pltpu.SemaphoreType.DMA((n, n_dev)),
         ],
         compiler_params=pltpu.CompilerParams(vmem_limit_bytes=VMEM_LIMIT),
-        cost_estimate=pl.CostEstimate(flops=n_used * part * dim * 20, bytes_accessed=n_used * part * dim * 3, transcendentals=0),
+        cost_estimate=pl.CostEstimate(flops=n * n_dev * part * dim * 20, bytes_accessed=n * n_dev * part * dim * 3, transcendentals=0),
     )(starts, plan, by_table)
 
 
-def apply_kernel(slot, n_carried, ids_ref, lr_ref, grad_ref, tables_ref, accums_ref, *refs):
+def apply_kernel(slot, place, n_carried, ids_ref, lr_ref, grad_ref, tables_ref, accums_ref, *refs):
     carried_refs, (out_tables_ref, out_accums_ref, *scratch) = refs[:n_carried], refs[n_carried:]
     banks = scratch[:BANKS]
     stage, table_v, grad_v, sem = scratch[BANKS:]
-    segs, seg_rows, dim = grad_ref.shape
+    segs, seg_rows, dim = grad_v.shape
     n_rows = tables_ref.shape[1]
     id_stride = (ids_ref.shape[1] - BLOCK) // BANKS
-    grad_copy = pltpu.make_async_copy(grad_ref, grad_v, sem.at[0])
+    grad_copy = pltpu.make_async_copy(grad_ref.at[:, place], grad_v, sem.at[0])
     table_copy = pltpu.make_async_copy(tables_ref.at[slot], table_v, sem.at[1])
     grad_copy.start()
     table_copy.start()
@@ -215,11 +259,11 @@
     pltpu.make_async_copy(table_v, out_tables_ref.at[slot], sem.at[0]).wait()
 
 
-def apply_slot(slot, ids, lr, grad, tables, accums, carried):
+def apply_slot(slot, place, ids, lr, grad, tables, accums, carried):
     _, n_rows, dim = tables.shape
-    segs, seg_rows, _ = grad.shape
+    segs, _, seg_rows, _ = grad.shape
     return pl.pallas_call(
-        functools.partial(apply_kernel, slot, len(carried)),
+        functools.partial(apply_kernel, slot, place, len(carried)),
         out_shape=tuple(jax.ShapeDtypeStruct(x.shape, x.dtype) for x in (tables, accums)),
         in_specs=[pl.BlockSpec(memory_space=pltpu.SMEM)] * 2
         + [pl.BlockSpec(memory_space=pl.ANY)] * 2
@@ -247,9 +291,8 @@
         by_table = jnp.transpose(d_pool, (1, 0, 2))
         part = by_table.shape[1]
         plan_out, *ids = make_plan(row_ids[:, :, 0], lengths, n_group, n_rows)
-        plan = lax.all_to_all(plan_out, 'mp', 0, 0, tiled=True)
-        starts = plan[:, :, part:]
-        most = jnp.max(starts[:, :, MAX_LANE])
+        plan, starts, most = share_plan(plan_out)
+        most = most[0]
         lr = learn_rate.reshape(1)
         caps = tuple(c for c in CAPS(part))
 
@@ -257,12 +300,13 @@
             def run(operands):
                 by_table, plan, starts, ids, lr, tables, accums = operands
                 got = []
-                for k in range(n_slots):
-                    pack = pack_slot(k, caps[level], starts, plan, by_table)
-                    got.append(lax.all_to_all(pack, 'mp', 0, 0, tiled=True))
+                for c, slots in enumerate(CHUNKS(n_slots)):
+                    pack = pack_slots(slots, caps[level], starts, plan, by_table)
+                    swapped = lax.all_to_all(pack, 'mp', 0, 0, tiled=True)
+                    got += [(k, i, c, swapped) for i, k in enumerate(slots)]
                 carried = ()
-                for k in range(n_slots):
-                    carried = apply_slot(k, ids[k], lr, got[k], tables, accums, carried)
+                for k, i, c, swapped in got:
+                    carried = apply_slot(k, i, ids[k], lr, swapped, tables, accums, carried)
                 return tuple(carried)
 
             return run
@@ -276,3 +320,7 @@
 
 def CAPS(part):
     return (part * 9 // 16, part)
+
+
+def CHUNKS(n_slots):
+    return (0,), tuple(range(1, n_slots - 1)), (n_slots - 1,)

time: 215 us -> 201 us (0.935)
  blocking collectives: 13 us -> 0 us
  starting transfers between devices: 20.4 us -> 15.3 us
  Pallas kernels: 104 us -> 108 us
    all_to_all x1 -> x0, blocking collectives: 13 us -> none  [local_step(): plan = lax.all_to_all(plan_out, 'mp', 0, 0, tiled=True)]
    all_to_all x4 -> x3, starting transfers between devices: 20.4 us -> 15.3 us  [run(): swapped = lax.all_to_all(pack, 'mp', 0, 0, tiled=True)]
    pallas_call x8, Pallas kernels: 103 us -> 107 us  [the longest x4 79.5 us: apply_slot(): pl.pallas_call(functools.partial(apply_kernel, slot, place, len(carried))...]
    all_to_all x4 -> x3, waiting for transfers between devices: 70.4 us -> 71.9 us  [run(): swapped = lax.all_to_all(pack, 'mp', 0, 0, tiled=True)]
  transfers between devices with their start and end apart: 4 -> 3, of which waited for: 3 -> 2; matrix products, arithmetic and copies ran while one was open for 0% -> 0% of each run, Pallas kernels for 36% -> 36%
where the time goes in v5:
time: 201 us; the launch traced here: 198 us
  Pallas kernels  108 us (54%)
  waiting for transfers between devices  71.9 us (36%)
  starting transfers between devices  15.3 us (8%)
  local copies, waits for them, and re-layouts  2.07 us (1%)
    pallas_call x4, Pallas kernels, apply_slot(): pl.pallas_call(functools.partial(apply_kernel, slot, place, len(carried))...  79.5 us
    all_to_all x3, waiting for transfers between devices, run(): swapped = lax.all_to_all(pack, 'mp', 0, 0, tiled=True)  71.9 us
    pallas_call x3, Pallas kernels, pack_slots(): pl.pallas_call(functools.partial(pack_kernel, slots), out_shape=jax.Shape...  16.8 us
    all_to_all x3, starting transfers between devices, run(): swapped = lax.all_to_all(pack, 'mp', 0, 0, tiled=True)  15.3 us
    pallas_call x1, Pallas kernels, share_plan(): pl.pallas_call(functools.partial(share_kernel, n_dev), out_shape=(jax.Sha...  10.4 us
  transfers between devices with their start and end apart: 3, of which 2 were waited for; matrix products, arithmetic and copies ran while one was open for 0% of the time, Pallas kernels for 36%

profile of v5, /device:TPU:81, one launch (start us, length us, event | category | flops | bytes accessed | tf_op | source)
XLA Modules:
  0.0 198.4 jit_solution(8597846842386998969)
XLA Ops:
  0.6 1.1 copy.26
  1.8 0.0 copy-start
  1.8 0.9 copy-done
  2.7 1.1 shard_map.87
  3.8 10.4 %shard_map.88 = (s32[8,4,2176]{2,1,0:T(4,128)S(1)}, s32[8,4,128]{2,1,0:T(4,128)S(1)}, s32[1]{0:T(128)}) custom-call(s32[8,4,2176]{2,1,0:T(4,128)S(1)} %get-tuple-element.82.plan_ref), custom_call_target="tpu_custom_call" | custom-call | flops 20000000 | bytes 2000000 | tf_op jit(solution)/shard_map/pallas_call | solution.py:115
  14.9 183.5 %conditional.1 = ((bf16[4,16384,128]{2,1,0:T(8,128)(2,1)}, f32[4,16384]{1,0:T(4,128)})) conditional(s32[]{:T(128)} %bitcast.2, (s32[8,4,128]{2,1,0:T(4,128)S(1)}, s32[8,4,2176]{2,1,0:T(4,128)S(1)}, bf16[26,2048,128]{2,1,0:T(8,128)(2,1)}, s32[1,8320]{1,0:T(1,128)S(1)}, f32[]{:T(128)}, /*index=5*/bf16[4,16384,128]{2,1,0:T(8,128)(2,1)}, ...), branch_computations={%region_0.0_spmd, %region_1.0_spmd} | conditional | flops 3523215360 | bytes 143655040 | solution.py:316
  14.9 5.0 %branch_0_fun.9 = bf16[8,1,1152,128]{3,2,1,0:T(8,128)(2,1)} custom-call(s32[8,4,128]{2,1,0:T(4,128)S(1)} %get-tuple-element.42.starts_ref, s32[8,4,2176]{2,1,0:T(4,128)S(1)} %get-tuple-element.43.plan_ref, bf16[26,2048,128]{2,1,0:T(8,128)(2,1)} %get-tuple-element.44.tables_ref), custom_call_target="tpu_custom_call" | custom-call | flops 41943040 | bytes 6291456 | tf_op jit(solution)/shard_map/cond/branch_0_fun/pallas_call | solution.py:168
  19.9 4.6 %all-to-all-start.2 = ((bf16[8,1,1152,128]{3,2,1,0:T(8,128)(2,1)}), bf16[8,1,1152,128]{3,2,1,0:T(8,128)(2,1)}, u32[]{:S(2)}, u32[]{:S(2)}) async-start(bf16[8,1,1152,128]{3,2,1,0:T(8,128)(2,1)} %branch_0_fun.9), calls=%async_computation.2 | async-start | bytes 4718592 | tf_op jit(solution)/shard_map/cond/branch_0_fun/all_to_all | solution.py:305
  24.5 7.1 %branch_0_fun.8 = bf16[8,2,1152,128]{3,2,1,0:T(8,128)(2,1)} custom-call(s32[8,4,128]{2,1,0:T(4,128)S(1)} %get-tuple-element.42.starts_ref, s32[8,4,2176]{2,1,0:T(4,128)S(1)} %get-tuple-element.43.plan_ref, bf16[26,2048,128]{2,1,0:T(8,128)(2,1)} %get-tuple-element.44.tables_ref), custom_call_target="tpu_custom_call" | custom-call | flops 83886080 | bytes 12582912 | tf_op jit(solution)/shard_map/cond/branch_0_fun/pallas_call | solution.py:168
  31.6 22.1 %all-to-all-done.2.grad_ref = bf16[8,1,1152,128]{3,2,1,0:T(8,128)(2,1)} async-done(((bf16[8,1,1152,128]{3,2,1,0:T(8,128)(2,1)}), bf16[8,1,1152,128]{3,2,1,0:T(8,128)(2,1)}, u32[]{:S(2)}, u32[]{:S(2)}) %all-to-all-start.2) | async-done | bytes 2359328 | tf_op jit(solution)/shard_map/cond/branch_0_fun/all_to_all | solution.py:305
  53.7 5.5 %all-to-all-start.1 = ((bf16[8,2,1152,128]{3,2,1,0:T(8,128)(2,1)}), bf16[8,2,1152,128]{3,2,1,0:T(8,128)(2,1)}, u32[]{:S(2)}, u32[]{:S(2)}) async-start(bf16[8,2,1152,128]{3,2,1,0:T(8,128)(2,1)} %branch_0_fun.8), calls=%async_computation.1 | async-start | bytes 9437184 | tf_op jit(solution)/shard_map/cond/branch_0_fun/all_to_all | solution.py:305
  59.2 0.0 copy-start.1
  59.2 4.7 %branch_0_fun.7 = bf16[8,1,1152,128]{3,2,1,0:T(8,128)(2,1)} custom-call(s32[8,4,128]{2,1,0:T(4,128)S(1)} %get-tuple-element.42.starts_ref, s32[8,4,2176]{2,1,0:T(4,128)S(1)} %get-tuple-element.43.plan_ref, bf16[26,2048,128]{2,1,0:T(8,128)(2,1)} %get-tuple-element.44.tables_ref), custom_call_target="tpu_custom_call" | custom-call | flops 41943040 | bytes 6291456 | tf_op jit(solution)/shard_map/cond/branch_0_fun/pallas_call | solution.py:168
  63.9 49.8 %all-to-all-done.1.grad_ref = bf16[8,2,1152,128]{3,2,1,0:T(8,128)(2,1)} async-done(((bf16[8,2,1152,128]{3,2,1,0:T(8,128)(2,1)}), bf16[8,2,1152,128]{3,2,1,0:T(8,128)(2,1)}, u32[]{:S(2)}, u32[]{:S(2)}) %all-to-all-start.1) | async-done | bytes 4718624 | tf_op jit(solution)/shard_map/cond/branch_0_fun/all_to_all | solution.py:305
  113.7 5.2 %all-to-all-start = ((bf16[8,1,1152,128]{3,2,1,0:T(8,128)(2,1)}), bf16[8,1,1152,128]{3,2,1,0:T(8,128)(2,1)}, u32[]{:S(2)}, u32[]{:S(2)}) async-start(bf16[8,1,1152,128]{3,2,1,0:T(8,128)(2,1)} %branch_0_fun.7), calls=%async_computation | async-start | bytes 4718592 | tf_op jit(solution)/shard_map/cond/branch_0_fun/all_to_all | solution.py:305
  118.9 0.0 copy-done.1
  118.9 19.9 %branch_0_fun.10 = (bf16[4,16384,128]{2,1,0:T(8,128)(2,1)}, f32[4,16384]{1,0:T(4,128)}) custom-call(s32[1,8320]{1,0:T(1,128)S(1)} %get-tuple-element.49.ids_ref, f32[1]{0:T(128)} %bitcast.lr_ref, bf16[8,1,1152,128]{3,2,1,0:T(8,128)(2,1)} %all-to-all-done.2.grad_ref, bf16[4,16384,128]{2,1,0:T(8,128)(2,1)} %get-tuple-element.104.tables_ref, ...), custom_call_target="tpu_custom_call" | custom-call | flops 838860800 | bytes 16777216 | tf_op jit(solution)/shard_map/cond/branch_0_fun/pallas_call | solution.py:265
  138.8 19.9 %branch_0_fun.11 = (bf16[4,16384,128]{2,1,0:T(8,128)(2,1)}, f32[4,16384]{1,0:T(4,128)}) custom-call(s32[1,8320]{1,0:T(1,128)S(1)} %get-tuple-element.48.ids_ref, f32[1]{0:T(128)} %bitcast.lr_ref, bf16[8,2,1152,128]{3,2,1,0:T(8,128)(2,1)} %all-to-all-done.1.grad_ref, ...), custom_call_target="tpu_custom_call", output_to_operand_aliasing={{0}: (5, {})} | custom-call | flops 838860800 | bytes 16777216 | tf_op jit(solution)/shard_map/cond/branch_0_fun/pallas_call | solution.py:265
  158.6 19.9 %branch_0_fun.12 = (bf16[4,16384,128]{2,1,0:T(8,128)(2,1)}, f32[4,16384]{1,0:T(4,128)}) custom-call(s32[1,8320]{1,0:T(1,128)S(1)} %get-tuple-element.47.ids_ref, f32[1]{0:T(128)} %bitcast.lr_ref, bf16[8,2,1152,128]{3,2,1,0:T(8,128)(2,1)} %all-to-all-done.1.grad_ref, ...), custom_call_target="tpu_custom_call", output_to_operand_aliasing={{0}: (5, {})} | custom-call | flops 838860800 | bytes 16777216 | tf_op jit(solution)/shard_map/cond/branch_0_fun/pallas_call | solution.py:265
  178.5 0.0 all-to-all-done.grad_ref
  178.5 19.9 %branch_0_fun.13 = (bf16[4,16384,128]{2,1,0:T(8,128)(2,1)}, f32[4,16384]{1,0:T(4,128)}) custom-call(s32[1,8320]{1,0:T(1,128)S(1)} %get-tuple-element.40.ids_ref, f32[1]{0:T(128)} %bitcast.lr_ref, bf16[8,1,1152,128]{3,2,1,0:T(8,128)(2,1)} %all-to-all-done.grad_ref, ...), custom_call_target="tpu_custom_call", output_to_operand_aliasing={{0}: (5, {})} | custom-call | flops 838860800 | bytes 16777216 | tf_op jit(solution)/shard_map/cond/branch_0_fun/pallas_call | solution.py:265
Async XLA Ops:
  1.8 1.0 copy-start
  19.9 33.8 %all-to-all-start.2 = ((bf16[8,1,1152,128]{3,2,1,0:T(8,128)(2,1)}), bf16[8,1,1152,128]{3,2,1,0:T(8,128)(2,1)}, u32[]{:S(2)}, u32[]{:S(2)}) async-start(bf16[8,1,1152,128]{3,2,1,0:T(8,128)(2,1)} %branch_0_fun.9), calls=%async_computation.2 | async-start | bytes 4718592 | tf_op jit(solution)/shard_map/cond/branch_0_fun/all_to_all | solution.py:305
  53.7 60.0 %all-to-all-start.1 = ((bf16[8,2,1152,128]{3,2,1,0:T(8,128)(2,1)}), bf16[8,2,1152,128]{3,2,1,0:T(8,128)(2,1)}, u32[]{:S(2)}, u32[]{:S(2)}) async-start(bf16[8,2,1152,128]{3,2,1,0:T(8,128)(2,1)} %branch_0_fun.8), calls=%async_computation.1 | async-start | bytes 9437184 | tf_op jit(solution)/shard_map/cond/branch_0_fun/all_to_all | solution.py:305
  59.2 59.7 %copy-start.1 = (f32[4,16384]{1,0:T(4,128)S(1)}, f32[4,16384]{1,0:T(4,128)}, u32[]{:S(2)}) copy-start(f32[4,16384]{1,0:T(4,128)} %get-tuple-element.106.accums_ref) | copy-start | bytes 786436 | tf_op jit(solution)/shard_map/cond
  113.7 64.8 %all-to-all-start = ((bf16[8,1,1152,128]{3,2,1,0:T(8,128)(2,1)}), bf16[8,1,1152,128]{3,2,1,0:T(8,128)(2,1)}, u32[]{:S(2)}, u32[]{:S(2)}) async-start(bf16[8,1,1152,128]{3,2,1,0:T(8,128)(2,1)} %branch_0_fun.7), calls=%async_computation | async-start | bytes 4718592 | tf_op jit(solution)/shard_map/cond/branch_0_fun/all_to_all | solution.py:305

commit v6 on v5

v6 whole, which is shorter than its diff:
```python
import functools

import jax
import jax.numpy as jnp
from jax import lax
from jax.experimental import pallas as pl
from jax.experimental.pallas import tpu as pltpu
from jax.sharding import PartitionSpec as P


EPSILON = 1e-06
TINY = 1e-36
BANKS = 4
UNROLL = 8
BLOCK = 128
CHUNK = 1024
MAX_LANE = 64
VMEM_LIMIT = 66000000


def gather_parts(src_ref, dst, n_dev):
    n_slots, batch = src_ref.shape
    part = batch // n_dev
    for d in range(n_dev):
        dst[d * n_slots:(d + 1) * n_slots, :] = src_ref[:, d * part:(d + 1) * part]


def block_prefix(len_v, b, prefix):
    valid = len_v[:, b * BLOCK:(b + 1) * BLOCK] > 0
    ones = jnp.where(valid, 1.0, 0.0)
    local = jnp.dot(ones.astype(jnp.bfloat16), prefix, preferred_element_type=jnp.float32).astype(jnp.int32)
    return valid, local, jnp.sum(ones, axis=1, keepdims=True).astype(jnp.int32)


def prefix_matrix():
    below = lax.broadcasted_iota(jnp.int32, (BLOCK, BLOCK), 0) < lax.broadcasted_iota(jnp.int32, (BLOCK, BLOCK), 1)
    return jnp.where(below, 1.0, 0.0).astype(jnp.bfloat16)


def plan_kernel(lengths_ref, plan_ref, len_v):
    n_dev, n_slots, width = plan_ref.shape
    part, rows = width - BLOCK, n_dev * n_slots
    gather_parts(lengths_ref, len_v, n_dev)
    prefix = prefix_matrix()
    lane = lax.broadcasted_iota(jnp.int32, (rows, BLOCK), 1)
    count = jnp.zeros((rows, 1), jnp.int32)
    starts = jnp.zeros((rows, BLOCK), jnp.int32)
    for b in range(part // BLOCK):
        valid, local, more = block_prefix(len_v, b, prefix)
        place = jnp.where(valid, local, -1)
        for d in range(n_dev):
            plan_ref[d, :, b * BLOCK:(b + 1) * BLOCK] = place[d * n_slots:(d + 1) * n_slots, :]
        starts = jnp.where(lane == b, count, starts)
        count = count + more
    starts = jnp.where(lane == MAX_LANE, jnp.max(count, axis=0, keepdims=True), starts)
    for d in range(n_dev):
        plan_ref[d, :, part:] = starts[d * n_slots:(d + 1) * n_slots, :]


def make_plan(lengths, n_dev):
    n_slots, batch = lengths.shape
    part = batch // n_dev
    return pl.pallas_call(
        plan_kernel,
        out_shape=jax.ShapeDtypeStruct((n_dev, n_slots, part + BLOCK), jnp.int32),
        in_specs=[pl.BlockSpec(memory_space=pltpu.VMEM)],
        out_specs=pl.BlockSpec(memory_space=pltpu.VMEM),
        scratch_shapes=[pltpu.VMEM((n_dev * n_slots, part), jnp.int32)],
        compiler_params=pltpu.CompilerParams(vmem_limit_bytes=16000000),
        cost_estimate=pl.CostEstimate(flops=10000000, bytes_accessed=1000000, transcendentals=0),
    )(lengths)


def ids_kernel(n_dev, n_rows, ids_ref, lengths_ref, *refs):
    *packed_refs, ids_v, len_v = refs
    n_slots, batch = ids_ref.shape
    part, rows = batch // n_dev, n_dev * n_slots
    gather_parts(ids_ref, ids_v, n_dev)
    gather_parts(lengths_ref, len_v, n_dev)
    prefix = prefix_matrix()
    lane = lax.broadcasted_iota(jnp.int32, (rows, BLOCK), 1)
    count = jnp.zeros((rows, 1), jnp.int32)
    moves = []
    for b in range(part // BLOCK):
        valid, local, more = block_prefix(len_v, b, prefix)
        shift = (b * BLOCK + lane) - (count + local)
        moves.append(jnp.where(valid, (shift << 16) | ids_v[:, b * BLOCK:(b + 1) * BLOCK], n_rows))
        count = count + more
    move = jnp.concatenate(moves, axis=1)
    step = 1
    while step < part:
        come = pltpu.roll(move, part - step, 1)
        bit = step << 16
        stay = jnp.where((move & bit) != 0, n_rows, move)
        move = jnp.where((come & bit) != 0, come, stay)
        step *= 2
    spot = lax.broadcasted_iota(jnp.int32, (rows, part), 1)
    packed = jnp.where(spot < count, move & 0xFFFF, n_rows)
    most = jnp.max(count, axis=0, keepdims=True)
    for s in range(n_slots):
        for j in range(n_dev // 2):
            low, high = ((2 * j + h) * n_slots + s for h in range(2))
            packed_refs[s][:, j * part:(j + 1) * part] = packed[low:low + 1, :] | (packed[high:high + 1, :] << 16)
        packed_refs[s][:, n_dev // 2 * part:] = jnp.broadcast_to(most, (1, BLOCK))


def pack_ids(ids, lengths, n_dev, n_rows):
    n_slots, batch = ids.shape
    part = batch // n_dev
    assert n_rows < 1 << 15 and part <= 1 << 15
    return pl.pallas_call(
        functools.partial(ids_kernel, n_dev, n_rows),
        out_shape=(jax.ShapeDtypeStruct((1, batch // 2 + BLOCK), jnp.int32),) * n_slots,
        in_specs=[pl.BlockSpec(memory_space=pltpu.VMEM)] * 2,
        out_specs=(pl.BlockSpec(memory_space=pltpu.VMEM),) * n_slots,
        scratch_shapes=[pltpu.VMEM((n_dev * n_slots, part), jnp.int32)] * 2,
        compiler_params=pltpu.CompilerParams(vmem_limit_bytes=32000000),
        cost_estimate=pl.CostEstimate(flops=20000000, bytes_accessed=2000000, transcendentals=0),
    )(ids, lengths)


def share_kernel(n_dev, plan_ref, plans_ref, starts_ref, most_ref, send_sem, recv_sem, own_sem):
    pod, me = lax.axis_index('pod'), lax.axis_index('mp')
    barrier = pltpu.get_barrier_semaphore()
    for o in range(1, n_dev):
        pl.semaphore_signal(barrier, inc=1, device_id=(pod, (me + o) % n_dev), device_id_type=pl.DeviceIdType.MESH)
    pl.semaphore_wait(barrier, n_dev - 1)
    copies = [
        pltpu.make_async_remote_copy(
            src_ref=plan_ref.at[(me + o) % n_dev],
            dst_ref=plans_ref.at[me],
            send_sem=send_sem.at[o],
            recv_sem=recv_sem.at[o],
            device_id=(pod, (me + o) % n_dev),
            device_id_type=pl.DeviceIdType.MESH,
        )
        for o in range(1, n_dev)
    ]
    for copy in copies:
        copy.start()
    own = pltpu.make_async_copy(plan_ref.at[me], plans_ref.at[me], own_sem)
    own.start()
    own.wait()
    for copy in copies:
        copy.wait()
    part = plans_ref.shape[2] - BLOCK
    starts = plans_ref[:, :, part:]
    starts_ref[...] = starts
    most_ref[0] = jnp.max(starts[:, :, MAX_LANE:MAX_LANE + 1])


def share_plan(plan):
    n_dev, n_slots, _ = plan.shape
    return pl.pallas_call(
        functools.partial(share_kernel, n_dev),
        out_shape=(
            jax.ShapeDtypeStruct(plan.shape, plan.dtype),
            jax.ShapeDtypeStruct((n_dev, n_slots, BLOCK), plan.dtype),
            jax.ShapeDtypeStruct((1,), plan.dtype),
        ),
        in_specs=[pl.BlockSpec(memory_space=pltpu.VMEM)],
        out_specs=(pl.BlockSpec(memory_space=pltpu.VMEM), pl.BlockSpec(memory_space=pltpu.VMEM), pl.BlockSpec(memory_space=pltpu.SMEM)),
        scratch_shapes=[pltpu.SemaphoreType.DMA((n_dev,)), pltpu.SemaphoreType.DMA((n_dev,)), pltpu.SemaphoreType.DMA],
        compiler_params=pltpu.CompilerParams(collective_id=0, has_side_effects=True, vmem_limit_bytes=16000000),
        cost_estimate=pl.CostEstimate(flops=20000000, bytes_accessed=2000000, transcendentals=0),
    )(plan)


def pack_kernel(slots, starts_ref, plan_ref, tables_ref, out_ref, grad_v, stage, pack_v, in_sem, out_sem):
    n_slots = plan_ref.shape[1]
    cap = out_ref.shape[2]
    n_tab, part, _ = tables_ref.shape
    slot_row = lax.broadcasted_iota(jnp.int32, (BLOCK, BLOCK), 0)
    used = [[d for d in range(out_ref.shape[0]) if d * n_slots + slot < n_tab] for slot in slots]

    def fetch(i, d):
        return pltpu.make_async_copy(tables_ref.at[d * n_slots + slots[i]], grad_v.at[i, d], in_sem.at[i, d])

    def emit(i, d):
        return pltpu.make_async_copy(pack_v.at[i, d], out_ref.at[d, i], out_sem.at[i, d])

    for i, dests in enumerate(used):
        for d in dests:
            fetch(i, d).start()
    for i, dests in enumerate(used):
        def table(d, carry):
            fetch(i, d).wait()
            for b in range(part // BLOCK):
                place = plan_ref[d, slots[i]:slots[i] + 1, b * BLOCK:(b + 1) * BLOCK]
                pick = jnp.where(slot_row == place, 1.0, 0.0).astype(jnp.bfloat16)
                rows = jnp.dot(pick, grad_v[i, d, b * BLOCK:(b + 1) * BLOCK, :], preferred_element_type=jnp.float32)
                stage[pl.ds(starts_ref[d, slots[i], b], BLOCK), :] = rows
            pack_v[i, d] = stage[:cap, :].astype(jnp.bfloat16)
            emit(i, d).start()
            return carry

        lax.fori_loop(0, len(dests), table, 0)
    for i, dests in enumerate(used):
        for d in dests:
            emit(i, d).wait()


def pack_slots(slots, cap, starts, plan, by_table):
    n_dev = plan.shape[0]
    _, part, dim = by_table.shape
    n = len(slots)
    return pl.pallas_call(
        functools.partial(pack_kernel, slots),
        out_shape=jax.ShapeDtypeStruct((n_dev, n, cap, dim), by_table.dtype),
        in_specs=[pl.BlockSpec(memory_space=pltpu.SMEM), pl.BlockSpec(memory_space=pltpu.VMEM), pl.BlockSpec(memory_space=pl.ANY)],
        out_specs=pl.BlockSpec(memory_space=pl.ANY),
        scratch_shapes=[
            pltpu.VMEM((n, n_dev, part, dim), by_table.dtype),
            pltpu.VMEM((cap + BLOCK, dim), jnp.float32),
            pltpu.VMEM((n, n_dev, cap, dim), by_table.dtype),
            pltpu.SemaphoreType.DMA((n, n_dev)),
            pltpu.SemaphoreType.DMA((n, n_dev)),
        ],
        compiler_params=pltpu.CompilerParams(vmem_limit_bytes=VMEM_LIMIT),
        cost_estimate=pl.CostEstimate(flops=n * n_dev * part * dim * 20, bytes_accessed=n * n_dev * part * dim * 3, transcendentals=0),
    )(starts, plan, by_table)


def apply_kernel(slots, n_carried, lr_ref, grad_ref, tables_ref, accums_ref, *refs):
    n = len(slots)
    ids_refs, carried_refs = refs[:n], refs[n:n + n_carried]
    out_tables_ref, out_accums_ref, *scratch = refs[n + n_carried:]
    ids_s, banks, (stage, table_v, grad_v, sem, out_sem) = scratch[:n], scratch[n:n + BANKS], scratch[n + BANKS:]
    _, segs, seg_rows, dim = grad_v.shape
    n_rows = tables_ref.shape[1]
    id_stride = (ids_refs[0].shape[1] - BLOCK) // BANKS
    copies = [
        (
            pltpu.make_async_copy(grad_ref.at[:, i], grad_v.at[i], sem.at[i, 0]),
            pltpu.make_async_copy(ids_refs[i], ids_s[i], sem.at[i, 1]),
            pltpu.make_async_copy(tables_ref.at[slot], table_v.at[i], sem.at[i, 2]),
        )
        for i, slot in enumerate(slots)
    ]
    for grad_copy, ids_copy, table_copy in copies:
        ids_copy.start()
        grad_copy.start()
        table_copy.start()

    zero = jnp.zeros((BLOCK, dim), jnp.float32)

    def clear(i, carry):
        for bank in banks:
            bank[pl.ds(pl.multiple_of(i * BLOCK, BLOCK), BLOCK), :] = zero
        return carry

    lax.fori_loop(0, n_rows // BLOCK, clear, 0)
    for bank in banks:
        bank[pl.ds(n_rows, 8), :] = zero[:8]
    out_accums_ref[...] = (carried_refs[1] if n_carried else accums_ref)[...]
    eye = lax.broadcasted_iota(jnp.int32, (BLOCK, dim), 0) == lax.broadcasted_iota(jnp.int32, (BLOCK, dim), 1)
    lr = lr_ref[0]

    for i, slot in enumerate(slots):
        grad_copy, ids_copy, table_copy = copies[i]
        ids_copy.wait()
        grad_copy.wait()

        def widen(t, carry):
            for j in range(segs):
                rows = pl.ds(pl.multiple_of(t * 32, 32), 32)
                stage[j, rows, :] = grad_v[i, j, rows, :].astype(jnp.float32)
            return carry

        lax.fori_loop(0, seg_rows // 32, widen, 0)

        def add_rows(t, carry):
            base = t * UNROLL
            for u in range(UNROLL):
                for j, bank in enumerate(banks):
                    pair = ids_s[i][0, j * id_stride + u + base]
                    first, second = pair & 0xFFFF, pair >> 16
                    same = jnp.full((1, dim), first) == jnp.full((1, dim), second)
                    add_first = stage[2 * j, pl.ds(base + u, 1), :]
                    add_second = stage[2 * j + 1, pl.ds(base + u, 1), :]
                    add_second = jnp.where(same, add_first + add_second, add_second)
                    old_first = bank[pl.ds(first, 1), :]
                    old_second = bank[pl.ds(second, 1), :]
                    bank[pl.ds(first, 1), :] = old_first + add_first
                    bank[pl.ds(second, 1), :] = old_second + add_second
            return carry

        lax.fori_loop(0, (ids_s[i][0, BANKS * id_stride] + UNROLL - 1) // UNROLL, add_rows, 0)
        table_copy.wait()

        def update(c, carry):
            for s in range(CHUNK // BLOCK):
                first_row = pl.multiple_of((c * (CHUNK // BLOCK) + s) * BLOCK, BLOCK)
                rows = pl.ds(first_row, BLOCK)
                grad = banks[0][rows, :]
                for bank in banks[1:]:
                    grad = grad + bank[rows, :]
                if i + 1 < n:
                    for bank in banks:
                        bank[rows, :] = zero
                old = jnp.where(eye, accums_ref[slot:slot + 1, rows], 0.0)
                new = jnp.sum(grad * grad * (1.0 / dim) + old, axis=1, keepdims=True)
                out_accums_ref[slot:slot + 1, rows] = jnp.sum(jnp.where(eye, new, 0.0), axis=0, keepdims=True)
                root = lax.rsqrt(jnp.maximum(new, TINY))
                scale = lr * root / (1.0 + EPSILON * root)
                table_v[i, rows, :] = (table_v[i, rows, :].astype(jnp.float32) - grad * scale).astype(jnp.bfloat16)
            done = pl.ds(pl.multiple_of(c * CHUNK, CHUNK), CHUNK)
            pltpu.make_async_copy(table_v.at[i, done], out_tables_ref.at[slot, done], out_sem.at[i]).start()
            return carry

        lax.fori_loop(0, n_rows // CHUNK, update, 0)
    for i, slot in enumerate(slots):
        pltpu.make_async_copy(table_v.at[i], out_tables_ref.at[slot], out_sem.at[i]).wait()


def apply_slots(slots, ids, lr, grad, tables, accums, carried):
    _, n_rows, dim = tables.shape
    segs, n, seg_rows, _ = grad.shape
    assert segs == 2 * BANKS
    return pl.pallas_call(
        functools.partial(apply_kernel, slots, len(carried)),
        out_shape=tuple(jax.ShapeDtypeStruct(x.shape, x.dtype) for x in (tables, accums)),
        in_specs=[pl.BlockSpec(memory_space=pltpu.SMEM)]
        + [pl.BlockSpec(memory_space=pl.ANY)] * 2
        + [pl.BlockSpec(memory_space=pltpu.VMEM)]
        + [pl.BlockSpec(memory_space=pl.ANY)] * n
        + [pl.BlockSpec(memory_space=pl.ANY), pl.BlockSpec(memory_space=pltpu.VMEM)][:len(carried)],
        out_specs=(pl.BlockSpec(memory_space=pl.ANY), pl.BlockSpec(memory_space=pltpu.VMEM)),
        input_output_aliases={4 + n: 0} if carried else {},
        scratch_shapes=[pltpu.SMEM(ids[0].shape, jnp.int32)] * n
        + [pltpu.VMEM((n_rows + 8, dim), jnp.float32)] * BANKS
        + [
            pltpu.VMEM((segs, seg_rows, dim), jnp.float32),
            pltpu.VMEM((n, n_rows, dim), tables.dtype),
            pltpu.VMEM((n, segs, seg_rows, dim), grad.dtype),
            pltpu.SemaphoreType.DMA((n, 3)),
            pltpu.SemaphoreType.DMA((n,)),
        ],
        compiler_params=pltpu.CompilerParams(vmem_limit_bytes=VMEM_LIMIT),
        cost_estimate=pl.CostEstimate(flops=n * n_rows * dim * 400, bytes_accessed=4 * n * n_rows * dim * 2, transcendentals=0),
    )(lr, grad, tables, accums, *(ids[k] for k in slots), *carried)


def solution(mesh):
    n_group = mesh.shape['mp']
    slot_spec = P(('pod', 'mp'))

    def local_step(d_pool, row_ids, lengths, tables, row_accum, learn_rate):
        n_slots, n_rows, _ = tables.shape
        by_table = jnp.transpose(d_pool, (1, 0, 2))
        part = by_table.shape[1]
        plan_out = make_plan(lengths, n_group)
        plan, starts, most = share_plan(plan_out)
        most = most[0]
        lr = learn_rate.reshape(1)
        caps = CAPS(part)

        def exchange(level):
            def run(operands):
                by_table, plan, starts, row_ids, lengths, lr, tables, accums = operands
                got = []
                for slots in CHUNKS(n_slots):
                    pack = pack_slots(slots, caps[level], starts, plan, by_table)
                    got.append(lax.all_to_all(pack, 'mp', 0, 0, tiled=True))
                ids = pack_ids(row_ids[:, :, 0], lengths, n_group, n_rows)
                carried = ()
                for c, slots in enumerate(CHUNKS(n_slots)):
                    carried = apply_slots(slots, ids, lr, got[c], tables, accums, carried)
                return tuple(carried)

            return run

        level = sum((most > cap).astype(jnp.int32) for cap in caps[:-1])
        operands = (by_table, plan, starts, row_ids, lengths, lr, tables, row_accum)
        return lax.switch(level, [exchange(i) for i in range(len(caps))], operands)

    return jax.shard_map(local_step, mesh=mesh, in_specs=(slot_spec, slot_spec, slot_spec, slot_spec, slot_spec, P()), out_specs=(slot_spec, slot_spec), check_vma=False)


def CAPS(part):
    return part * 35 // 64, part * 39 // 64, part


def CHUNKS(n_slots):
    return (0,), tuple(range(1, n_slots - 1)), (n_slots - 1,)
```

time: 201 us -> 197 us (0.980)
  Pallas kernels: 108 us -> 104 us
  waiting for transfers between devices: 71.9 us -> 69.8 us
    pallas_call x5, Pallas kernels: 80.5 us -> 76.7 us  [the longest x3 74.4 us: apply_slots(): pl.pallas_call(functools.partial(apply_kernel, slots, len(carried)), out_...]
    cond x2 -> x12, local copies, waits for them, and re-layouts: 0.01 us -> 2.43 us
    all_to_all x3, waiting for transfers between devices: 71.9 us -> 69.8 us  [run(): got.append(lax.all_to_all(pack, 'mp', 0, 0, tiled=True))]
    unnamed x3 -> x0, local copies, waits for them, and re-layouts: 2.07 us -> none
  transfers between devices with their start and end apart: 3 -> 3, of which waited for: 2 -> 2; matrix products, arithmetic and copies ran while one was open for 0% -> 1% of each run, Pallas kernels for 36% -> 35%
where the time goes in v6:
time: 197 us; the launch traced here: 195 us
  Pallas kernels  104 us (53%)
  waiting for transfers between devices  69.8 us (35%)
  starting transfers between devices  15.2 us (8%)
  local copies, waits for them, and re-layouts  3.55 us (2%)
  between operations  2.09 us (1%)
    pallas_call x3, Pallas kernels, apply_slots(): pl.pallas_call(functools.partial(apply_kernel, slots, len(carried)), out_...  74.4 us
    all_to_all x3, waiting for transfers between devices, run(): got.append(lax.all_to_all(pack, 'mp', 0, 0, tiled=True))  69.8 us
    pallas_call x3, Pallas kernels, pack_slots(): pl.pallas_call(functools.partial(pack_kernel, slots), out_shape=jax.Shape...  16.8 us
    all_to_all x3, starting transfers between devices, run(): got.append(lax.all_to_all(pack, 'mp', 0, 0, tiled=True))  15.2 us
    pallas_call x1, Pallas kernels, share_plan(): pl.pallas_call(functools.partial(share_kernel, n_dev), out_shape=(jax.Sha...  10.4 us
  transfers between devices with their start and end apart: 3, of which 2 were waited for; matrix products, arithmetic and copies ran while one was open for 1% of the time, Pallas kernels for 35%

profile of v6, /device:TPU:81, one launch (start us, length us, event | category | flops | bytes accessed | tf_op | source)
XLA Modules:
  0.0 194.8 jit_solution(10773451322836461763)
XLA Ops:
  0.6 1.2 shard_map.95.plan_ref
  1.8 10.4 %shard_map.96 = (s32[8,4,2176]{2,1,0:T(4,128)S(1)}, s32[8,4,128]{2,1,0:T(4,128)S(1)}, s32[1]{0:T(128)}) custom-call(s32[8,4,2176]{2,1,0:T(4,128)S(1)} %shard_map.95.plan_ref), custom_call_target="tpu_custom_call" | custom-call | flops 20000000 | bytes 2000000 | tf_op jit(solution)/shard_map/pallas_call | solution.py:154
  13.5 181.1 %conditional.1 = ((bf16[4,16384,128]{2,1,0:T(8,128)(2,1)}, f32[4,16384]{1,0:T(4,128)})) conditional(s32[]{:T(128)} %bitcast.6, (s32[8,4,128]{2,1,0:T(4,128)S(1)}, s32[8,4,2176]{2,1,0:T(4,128)S(1)}, bf16[26,2048,128]{2,1,0:T(8,128)(2,1)}, s32[4,16384,1]{1,2,0:T(1,128)}, s32[4,16384]{1,0:T(4,128)}, /*index=5*/f32[]{:T(128)}, ...), branch_computations={%region_0.0_spmd, %region_1.0_spmd, %region_2.0_spmd} | conditional | flops 3543215360 | bytes 148809120 | solution.py:375
  13.5 5.0 %branch_0_fun.10 = bf16[8,1,1120,128]{3,2,1,0:T(8,128)(2,1)} custom-call(s32[8,4,128]{2,1,0:T(4,128)S(1)} %get-tuple-element.49.starts_ref, s32[8,4,2176]{2,1,0:T(4,128)S(1)} %get-tuple-element.50.plan_ref, bf16[26,2048,128]{2,1,0:T(8,128)(2,1)} %get-tuple-element.51.tables_ref), custom_call_target="tpu_custom_call" | custom-call | flops 41943040 | bytes 6291456 | tf_op jit(solution)/shard_map/cond/branch_0_fun/pallas_call | solution.py:207
  18.5 4.6 %all-to-all-start.2 = ((bf16[8,1,1120,128]{3,2,1,0:T(8,128)(2,1)}), bf16[8,1,1120,128]{3,2,1,0:T(8,128)(2,1)}, u32[]{:S(2)}, u32[]{:S(2)}) async-start(bf16[8,1,1120,128]{3,2,1,0:T(8,128)(2,1)} %branch_0_fun.10), calls=%async_computation.2 | async-start | bytes 4587520 | tf_op jit(solution)/shard_map/cond/branch_0_fun/all_to_all | solution.py:364
  23.1 7.1 %branch_0_fun.9 = bf16[8,2,1120,128]{3,2,1,0:T(8,128)(2,1)} custom-call(s32[8,4,128]{2,1,0:T(4,128)S(1)} %get-tuple-element.49.starts_ref, s32[8,4,2176]{2,1,0:T(4,128)S(1)} %get-tuple-element.50.plan_ref, bf16[26,2048,128]{2,1,0:T(8,128)(2,1)} %get-tuple-element.51.tables_ref), custom_call_target="tpu_custom_call" | custom-call | flops 83886080 | bytes 12582912 | tf_op jit(solution)/shard_map/cond/branch_0_fun/pallas_call | solution.py:207
  30.2 21.4 %all-to-all-done.2.grad_ref = bf16[8,1,1120,128]{3,2,1,0:T(8,128)(2,1)} async-done(((bf16[8,1,1120,128]{3,2,1,0:T(8,128)(2,1)}), bf16[8,1,1120,128]{3,2,1,0:T(8,128)(2,1)}, u32[]{:S(2)}, u32[]{:S(2)}) %all-to-all-start.2) | async-done | bytes 2293792 | tf_op jit(solution)/shard_map/cond/branch_0_fun/all_to_all | solution.py:364
  51.6 5.4 %all-to-all-start.1 = ((bf16[8,2,1120,128]{3,2,1,0:T(8,128)(2,1)}), bf16[8,2,1120,128]{3,2,1,0:T(8,128)(2,1)}, u32[]{:S(2)}, u32[]{:S(2)}) async-start(bf16[8,2,1120,128]{3,2,1,0:T(8,128)(2,1)} %branch_0_fun.9), calls=%async_computation.1 | async-start | bytes 9175040 | tf_op jit(solution)/shard_map/cond/branch_0_fun/all_to_all | solution.py:364
  57.0 4.7 %branch_0_fun.7 = bf16[8,1,1120,128]{3,2,1,0:T(8,128)(2,1)} custom-call(s32[8,4,128]{2,1,0:T(4,128)S(1)} %get-tuple-element.49.starts_ref, s32[8,4,2176]{2,1,0:T(4,128)S(1)} %get-tuple-element.50.plan_ref, bf16[26,2048,128]{2,1,0:T(8,128)(2,1)} %get-tuple-element.51.tables_ref), custom_call_target="tpu_custom_call" | custom-call | flops 41943040 | bytes 6291456 | tf_op jit(solution)/shard_map/cond/branch_0_fun/pallas_call | solution.py:207
  61.7 0.0 copy-start.15
  61.7 0.0 copy-start.12
  61.7 48.4 %all-to-all-done.1.grad_ref = bf16[8,2,1120,128]{3,2,1,0:T(8,128)(2,1)} async-done(((bf16[8,2,1120,128]{3,2,1,0:T(8,128)(2,1)}), bf16[8,2,1120,128]{3,2,1,0:T(8,128)(2,1)}, u32[]{:S(2)}, u32[]{:S(2)}) %all-to-all-start.1) | async-done | bytes 4587552 | tf_op jit(solution)/shard_map/cond/branch_0_fun/all_to_all | solution.py:364
  110.1 5.2 %all-to-all-start = ((bf16[8,1,1120,128]{3,2,1,0:T(8,128)(2,1)}), bf16[8,1,1120,128]{3,2,1,0:T(8,128)(2,1)}, u32[]{:S(2)}, u32[]{:S(2)}) async-start(bf16[8,1,1120,128]{3,2,1,0:T(8,128)(2,1)} %branch_0_fun.7), calls=%async_computation | async-start | bytes 4587520 | tf_op jit(solution)/shard_map/cond/branch_0_fun/all_to_all | solution.py:364
  115.3 1.1 copy.38
  116.5 0.0 copy-done.15
  116.5 1.1 branch_0_fun.8
  117.6 0.0 copy-start.2
  117.6 0.6 copy-done.2
  118.2 0.0 copy-start.5
  118.2 0.6 copy-done.5
  118.8 0.0 copy-start.6
  118.8 0.6 copy-done.6
  119.4 0.0 copy-start.9
  119.4 0.6 copy-done.9
  120.0 0.0 copy-done.12
  120.0 18.9 %branch_0_fun.11 = (bf16[4,16384,128]{2,1,0:T(8,128)(2,1)}, f32[4,16384]{1,0:T(4,128)}) custom-call(f32[1]{0:T(128)} %bitcast.lr_ref, bf16[8,1,1120,128]{3,2,1,0:T(8,128)(2,1)} %all-to-all-done.2.grad_ref, bf16[4,16384,128]{2,1,0:T(8,128)(2,1)} %get-tuple-element.130.tables_ref, f32[4,16384]{1,0:T(4,128)S(1)} %copy-done.12, s32[1,8320]{1,0:T(1,128)} %copy-done.9), custom_call_target="tpu_custom_call" | custom-call | flops 838860800 | bytes 16777216 | tf_op jit(solution)/shard_map/cond/branch_0_fun/pallas_call | solution.py:320
  138.9 35.7 %branch_0_fun.12 = (bf16[4,16384,128]{2,1,0:T(8,128)(2,1)}, f32[4,16384]{1,0:T(4,128)}) custom-call(f32[1]{0:T(128)} %bitcast.lr_ref, bf16[8,2,1120,128]{3,2,1,0:T(8,128)(2,1)} %all-to-all-done.1.grad_ref, bf16[4,16384,128]{2,1,0:T(8,128)(2,1)} %get-tuple-element.130.tables_ref, f32[4,16384]{1,0:T(4,128)S(1)} %copy-done.12, ...), custom_call_target="tpu_custom_call", output_to_operand_aliasing={{0}: (6, {})} | custom-call | flops 1677721600 | bytes 33554432 | tf_op jit(solution)/shard_map/cond/branch_0_fun/pallas_call | solution.py:320
  174.6 0.0 all-to-all-done.grad_ref
  174.6 19.8 %branch_0_fun.13 = (bf16[4,16384,128]{2,1,0:T(8,128)(2,1)}, f32[4,16384]{1,0:T(4,128)}) custom-call(f32[1]{0:T(128)} %bitcast.lr_ref, bf16[8,1,1120,128]{3,2,1,0:T(8,128)(2,1)} %all-to-all-done.grad_ref, bf16[4,16384,128]{2,1,0:T(8,128)(2,1)} %get-tuple-element.130.tables_ref, f32[4,16384]{1,0:T(4,128)S(1)} %copy-done.12, ...), custom_call_target="tpu_custom_call", output_to_operand_aliasing={{0}: (5, {})} | custom-call | flops 838860800 | bytes 16777216 | tf_op jit(solution)/shard_map/cond/branch_0_fun/pallas_call | solution.py:320
Async XLA Ops:
  18.5 33.1 %all-to-all-start.2 = ((bf16[8,1,1120,128]{3,2,1,0:T(8,128)(2,1)}), bf16[8,1,1120,128]{3,2,1,0:T(8,128)(2,1)}, u32[]{:S(2)}, u32[]{:S(2)}) async-start(bf16[8,1,1120,128]{3,2,1,0:T(8,128)(2,1)} %branch_0_fun.10), calls=%async_computation.2 | async-start | bytes 4587520 | tf_op jit(solution)/shard_map/cond/branch_0_fun/all_to_all | solution.py:364
  51.6 58.5 %all-to-all-start.1 = ((bf16[8,2,1120,128]{3,2,1,0:T(8,128)(2,1)}), bf16[8,2,1120,128]{3,2,1,0:T(8,128)(2,1)}, u32[]{:S(2)}, u32[]{:S(2)}) async-start(bf16[8,2,1120,128]{3,2,1,0:T(8,128)(2,1)} %branch_0_fun.9), calls=%async_computation.1 | async-start | bytes 9175040 | tf_op jit(solution)/shard_map/cond/branch_0_fun/all_to_all | solution.py:364
  61.7 54.8 %copy-start.15 = (s32[4,16384]{1,0:T(4,128)S(1)}, s32[4,16384]{1,0:T(4,128)}, u32[]{:S(2)}) copy-start(s32[4,16384]{1,0:T(4,128)} %get-tuple-element.55.lengths_ref) | copy-start | bytes 786436 | tf_op jit(solution)/shard_map/cond
  61.7 58.3 %copy-start.12 = (f32[4,16384]{1,0:T(4,128)S(1)}, f32[4,16384]{1,0:T(4,128)}, u32[]{:S(2)}) copy-start(f32[4,16384]{1,0:T(4,128)} %get-tuple-element.133.accums_ref) | copy-start | bytes 786436 | tf_op jit(solution)/shard_map/cond
  110.1 64.5 %all-to-all-start = ((bf16[8,1,1120,128]{3,2,1,0:T(8,128)(2,1)}), bf16[8,1,1120,128]{3,2,1,0:T(8,128)(2,1)}, u32[]{:S(2)}, u32[]{:S(2)}) async-start(bf16[8,1,1120,128]{3,2,1,0:T(8,128)(2,1)} %branch_0_fun.7), calls=%async_computation | async-start | bytes 4587520 | tf_op jit(solution)/shard_map/cond/branch_0_fun/all_to_all | solution.py:364
  117.6 0.6 copy-start.2
  118.2 0.6 copy-start.5
  118.8 0.6 copy-start.6
  119.4 0.6 copy-start.9

commit v7 on v6

--- a/solution.py
+++ b/solution.py
@@ -11,7 +11,7 @@
 EPSILON = 1e-06
 TINY = 1e-36
 BANKS = 4
-UNROLL = 8
+UNROLL = 16
 BLOCK = 128
 CHUNK = 1024
 MAX_LANE = 64
@@ -98,10 +98,9 @@
     packed = jnp.where(spot < count, move & 0xFFFF, n_rows)
     most = jnp.max(count, axis=0, keepdims=True)
     for s in range(n_slots):
-        for j in range(n_dev // 2):
-            low, high = ((2 * j + h) * n_slots + s for h in range(2))
-            packed_refs[s][:, j * part:(j + 1) * part] = packed[low:low + 1, :] | (packed[high:high + 1, :] << 16)
-        packed_refs[s][:, n_dev // 2 * part:] = jnp.broadcast_to(most, (1, BLOCK))
+        for d in range(n_dev):
+            packed_refs[s][:, d * part:(d + 1) * part] = packed[d * n_slots + s:d * n_slots + s + 1, :]
+        packed_refs[s][:, n_dev * part:] = jnp.broadcast_to(most, (1, BLOCK))
 
 
 def pack_ids(ids, lengths, n_dev, n_rows):
@@ -110,7 +109,7 @@
     assert n_rows < 1 << 15 and part <= 1 << 15
     return pl.pallas_call(
         functools.partial(ids_kernel, n_dev, n_rows),
-        out_shape=(jax.ShapeDtypeStruct((1, batch // 2 + BLOCK), jnp.int32),) * n_slots,
+        out_shape=(jax.ShapeDtypeStruct((1, batch + BLOCK), jnp.int32),) * n_slots,
         in_specs=[pl.BlockSpec(memory_space=pltpu.VMEM)] * 2,
         out_specs=(pl.BlockSpec(memory_space=pltpu.VMEM),) * n_slots,
         scratch_shapes=[pltpu.VMEM((n_dev * n_slots, part), jnp.int32)] * 2,
@@ -225,23 +224,29 @@
     n = len(slots)
     ids_refs, carried_refs = refs[:n], refs[n:n + n_carried]
     out_tables_ref, out_accums_ref, *scratch = refs[n + n_carried:]
-    ids_s, banks, (stage, table_v, grad_v, sem, out_sem) = scratch[:n], scratch[n:n + BANKS], scratch[n + BANKS:]
+    banks, (stage, table_v, grad_v, done_v, sem, out_sem, ids_sem), scalars = scratch[:BANKS], scratch[BANKS:BANKS + 7], scratch[BANKS + 7:]
     _, segs, seg_rows, dim = grad_v.shape
+    part = (ids_refs[0].shape[1] - BLOCK) // segs
+    ids_s = [scalars[i * (segs + 1):(i + 1) * (segs + 1)] for i in range(n)]
     n_rows = tables_ref.shape[1]
-    id_stride = (ids_refs[0].shape[1] - BLOCK) // BANKS
     copies = [
         (
             pltpu.make_async_copy(grad_ref.at[:, i], grad_v.at[i], sem.at[i, 0]),
-            pltpu.make_async_copy(ids_refs[i], ids_s[i], sem.at[i, 1]),
+            [pltpu.make_async_copy(ids_refs[i].at[:, j * part:(j + 1) * part], ids_s[i][j], ids_sem.at[i, j]) for j in range(segs)]
+            + [pltpu.make_async_copy(ids_refs[i].at[:, segs * part:], ids_s[i][segs], ids_sem.at[i, segs])],
             pltpu.make_async_copy(tables_ref.at[slot], table_v.at[i], sem.at[i, 2]),
         )
         for i, slot in enumerate(slots)
     ]
-    for grad_copy, ids_copy, table_copy in copies:
-        ids_copy.start()
+    for grad_copy, ids_copies, table_copy in copies:
+        for copy in ids_copies:
+            copy.start()
         grad_copy.start()
         table_copy.start()
 
+    if n_carried:
+        done_copy = pltpu.make_async_copy(carried_refs[1], done_v, out_sem.at[n])
+        done_copy.start()
     zero = jnp.zeros((BLOCK, dim), jnp.float32)
 
     def clear(i, carry):
@@ -252,13 +257,13 @@
     lax.fori_loop(0, n_rows // BLOCK, clear, 0)
     for bank in banks:
         bank[pl.ds(n_rows, 8), :] = zero[:8]
-    out_accums_ref[...] = (carried_refs[1] if n_carried else accums_ref)[...]
     eye = lax.broadcasted_iota(jnp.int32, (BLOCK, dim), 0) == lax.broadcasted_iota(jnp.int32, (BLOCK, dim), 1)
     lr = lr_ref[0]
 
     for i, slot in enumerate(slots):
-        grad_copy, ids_copy, table_copy = copies[i]
-        ids_copy.wait()
+        grad_copy, ids_copies, table_copy = copies[i]
+        for copy in ids_copies:
+            copy.wait()
         grad_copy.wait()
 
         def widen(t, carry):
@@ -273,8 +278,7 @@
             base = t * UNROLL
             for u in range(UNROLL):
                 for j, bank in enumerate(banks):
-                    pair = ids_s[i][0, j * id_stride + u + base]
-                    first, second = pair & 0xFFFF, pair >> 16
+                    first, second = ids_s[i][2 * j][0, base + u], ids_s[i][2 * j + 1][0, base + u]
                     same = jnp.full((1, dim), first) == jnp.full((1, dim), second)
                     add_first = stage[2 * j, pl.ds(base + u, 1), :]
                     add_second = stage[2 * j + 1, pl.ds(base + u, 1), :]
@@ -285,8 +289,10 @@
                     bank[pl.ds(second, 1), :] = old_second + add_second
             return carry
 
-        lax.fori_loop(0, (ids_s[i][0, BANKS * id_stride] + UNROLL - 1) // UNROLL, add_rows, 0)
+        lax.fori_loop(0, (ids_s[i][segs][0, 0] + UNROLL - 1) // UNROLL, add_rows, 0)
         table_copy.wait()
+        if n_carried and i == 0:
+            done_copy.wait()
 
         def update(c, carry):
             for s in range(CHUNK // BLOCK):
@@ -300,22 +306,26 @@
                         bank[rows, :] = zero
                 old = jnp.where(eye, accums_ref[slot:slot + 1, rows], 0.0)
                 new = jnp.sum(grad * grad * (1.0 / dim) + old, axis=1, keepdims=True)
-                out_accums_ref[slot:slot + 1, rows] = jnp.sum(jnp.where(eye, new, 0.0), axis=0, keepdims=True)
+                done_v[slot:slot + 1, rows] = jnp.sum(jnp.where(eye, new, 0.0), axis=0, keepdims=True)
                 root = lax.rsqrt(jnp.maximum(new, TINY))
                 scale = lr * root / (1.0 + EPSILON * root)
                 table_v[i, rows, :] = (table_v[i, rows, :].astype(jnp.float32) - grad * scale).astype(jnp.bfloat16)
             done = pl.ds(pl.multiple_of(c * CHUNK, CHUNK), CHUNK)
             pltpu.make_async_copy(table_v.at[i, done], out_tables_ref.at[slot, done], out_sem.at[i]).start()
+            if i == n - 1:
+                pltpu.make_async_copy(done_v.at[:, done], out_accums_ref.at[:, done], out_sem.at[n]).start()
             return carry
 
         lax.fori_loop(0, n_rows // CHUNK, update, 0)
     for i, slot in enumerate(slots):
         pltpu.make_async_copy(table_v.at[i], out_tables_ref.at[slot], out_sem.at[i]).wait()
+    pltpu.make_async_copy(done_v, out_accums_ref, out_sem.at[n]).wait()
 
 
 def apply_slots(slots, ids, lr, grad, tables, accums, carried):
     _, n_rows, dim = tables.shape
     segs, n, seg_rows, _ = grad.shape
+    part = (ids[0].shape[1] - BLOCK) // segs
     assert segs == 2 * BANKS
     return pl.pallas_call(
         functools.partial(apply_kernel, slots, len(carried)),
@@ -324,18 +334,20 @@
         + [pl.BlockSpec(memory_space=pl.ANY)] * 2
         + [pl.BlockSpec(memory_space=pltpu.VMEM)]
         + [pl.BlockSpec(memory_space=pl.ANY)] * n
-        + [pl.BlockSpec(memory_space=pl.ANY), pl.BlockSpec(memory_space=pltpu.VMEM)][:len(carried)],
-        out_specs=(pl.BlockSpec(memory_space=pl.ANY), pl.BlockSpec(memory_space=pltpu.VMEM)),
-        input_output_aliases={4 + n: 0} if carried else {},
-        scratch_shapes=[pltpu.SMEM(ids[0].shape, jnp.int32)] * n
-        + [pltpu.VMEM((n_rows + 8, dim), jnp.float32)] * BANKS
+        + [pl.BlockSpec(memory_space=pl.ANY)] * len(carried),
+        out_specs=(pl.BlockSpec(memory_space=pl.ANY),) * 2,
+        input_output_aliases={4 + n: 0, 5 + n: 1} if carried else {},
+        scratch_shapes=[pltpu.VMEM((n_rows + 8, dim), jnp.float32)] * BANKS
         + [
             pltpu.VMEM((segs, seg_rows, dim), jnp.float32),
             pltpu.VMEM((n, n_rows, dim), tables.dtype),
             pltpu.VMEM((n, segs, seg_rows, dim), grad.dtype),
+            pltpu.VMEM(accums.shape, accums.dtype),
             pltpu.SemaphoreType.DMA((n, 3)),
-            pltpu.SemaphoreType.DMA((n,)),
-        ],
+            pltpu.SemaphoreType.DMA((n + 1,)),
+            pltpu.SemaphoreType.DMA((n, segs + 1)),
+        ]
+        + ([pltpu.SMEM((1, part), jnp.int32)] * segs + [pltpu.SMEM((1, BLOCK), jnp.int32)]) * n,
         compiler_params=pltpu.CompilerParams(vmem_limit_bytes=VMEM_LIMIT),
         cost_estimate=pl.CostEstimate(flops=n * n_rows * dim * 400, bytes_accessed=4 * n * n_rows * dim * 2, transcendentals=0),
     )(lr, grad, tables, accums, *(ids[k] for k in slots), *carried)

time: 197 us -> 190 us (0.964)
  Pallas kernels: 104 us -> 97 us
    pallas_call x3, Pallas kernels: 74.4 us -> 67.6 us  [apply_slots(): pl.pallas_call(functools.partial(apply_kernel, slots, len(carried)), out_...]
  transfers between devices with their start and end apart: 3 -> 3, of which waited for: 2 -> 2; matrix products, arithmetic and copies ran while one was open for 1% -> 1% of each run, Pallas kernels for 35% -> 33%
where the time goes in v7:
time: 190 us; the launch traced here: 188 us
  Pallas kernels  97 us (51%)
  waiting for transfers between devices  69.8 us (37%)
  starting transfers between devices  15.2 us (8%)
  local copies, waits for them, and re-layouts  3.63 us (2%)
  between operations  2.09 us (1%)
    all_to_all x3, waiting for transfers between devices, run(): got.append(lax.all_to_all(pack, 'mp', 0, 0, tiled=True))  69.8 us
    pallas_call x3, Pallas kernels, apply_slots(): pl.pallas_call(functools.partial(apply_kernel, slots, len(carried)), out_...  67.6 us
    pallas_call x3, Pallas kernels, pack_slots(): pl.pallas_call(functools.partial(pack_kernel, slots), out_shape=jax.Shape...  16.8 us
    all_to_all x3, starting transfers between devices, run(): got.append(lax.all_to_all(pack, 'mp', 0, 0, tiled=True))  15.2 us
    pallas_call x1, Pallas kernels, share_plan(): pl.pallas_call(functools.partial(share_kernel, n_dev), out_shape=(jax.Sha...  10.4 us
  transfers between devices with their start and end apart: 3, of which 2 were waited for; matrix products, arithmetic and copies ran while one was open for 1% of the time, Pallas kernels for 33%

profile of v7, /device:TPU:81, one launch (start us, length us, event | category | flops | bytes accessed | tf_op | source)
XLA Modules:
  0.0 188.1 jit_solution(11298683217027958109)
XLA Ops:
  0.6 1.2 shard_map.95.plan_ref
  1.8 10.4 %shard_map.96 = (s32[8,4,2176]{2,1,0:T(4,128)S(1)}, s32[8,4,128]{2,1,0:T(4,128)S(1)}, s32[1]{0:T(128)}) custom-call(s32[8,4,2176]{2,1,0:T(4,128)S(1)} %shard_map.95.plan_ref), custom_call_target="tpu_custom_call" | custom-call | flops 20000000 | bytes 2000000 | tf_op jit(solution)/shard_map/pallas_call | solution.py:153
  13.5 174.4 %conditional.1 = ((bf16[4,16384,128]{2,1,0:T(8,128)(2,1)}, f32[4,16384]{1,0:T(4,128)})) conditional(s32[]{:T(128)} %bitcast.6, (s32[8,4,128]{2,1,0:T(4,128)S(1)}, s32[8,4,2176]{2,1,0:T(4,128)S(1)}, bf16[26,2048,128]{2,1,0:T(8,128)(2,1)}, s32[4,16384,1]{1,2,0:T(1,128)}, s32[4,16384]{1,0:T(4,128)}, /*index=5*/f32[]{:T(128)}, ...), branch_computations={%region_0.0_spmd, %region_1.0_spmd, %region_2.0_spmd} | conditional | flops 3543215360 | bytes 149333408 | solution.py:387
  13.5 5.0 %branch_0_fun.10 = bf16[8,1,1120,128]{3,2,1,0:T(8,128)(2,1)} custom-call(s32[8,4,128]{2,1,0:T(4,128)S(1)} %get-tuple-element.49.starts_ref, s32[8,4,2176]{2,1,0:T(4,128)S(1)} %get-tuple-element.50.plan_ref, bf16[26,2048,128]{2,1,0:T(8,128)(2,1)} %get-tuple-element.51.tables_ref), custom_call_target="tpu_custom_call" | custom-call | flops 41943040 | bytes 6291456 | tf_op jit(solution)/shard_map/cond/branch_0_fun/pallas_call | solution.py:206
  18.5 4.6 %all-to-all-start.2 = ((bf16[8,1,1120,128]{3,2,1,0:T(8,128)(2,1)}), bf16[8,1,1120,128]{3,2,1,0:T(8,128)(2,1)}, u32[]{:S(2)}, u32[]{:S(2)}) async-start(bf16[8,1,1120,128]{3,2,1,0:T(8,128)(2,1)} %branch_0_fun.10), calls=%async_computation.2 | async-start | bytes 4587520 | tf_op jit(solution)/shard_map/cond/branch_0_fun/all_to_all | solution.py:376
  23.1 7.1 %branch_0_fun.9 = bf16[8,2,1120,128]{3,2,1,0:T(8,128)(2,1)} custom-call(s32[8,4,128]{2,1,0:T(4,128)S(1)} %get-tuple-element.49.starts_ref, s32[8,4,2176]{2,1,0:T(4,128)S(1)} %get-tuple-element.50.plan_ref, bf16[26,2048,128]{2,1,0:T(8,128)(2,1)} %get-tuple-element.51.tables_ref), custom_call_target="tpu_custom_call" | custom-call | flops 83886080 | bytes 12582912 | tf_op jit(solution)/shard_map/cond/branch_0_fun/pallas_call | solution.py:206
  30.2 21.4 %all-to-all-done.2.grad_ref = bf16[8,1,1120,128]{3,2,1,0:T(8,128)(2,1)} async-done(((bf16[8,1,1120,128]{3,2,1,0:T(8,128)(2,1)}), bf16[8,1,1120,128]{3,2,1,0:T(8,128)(2,1)}, u32[]{:S(2)}, u32[]{:S(2)}) %all-to-all-start.2) | async-done | bytes 2293792 | tf_op jit(solution)/shard_map/cond/branch_0_fun/all_to_all | solution.py:376
  51.6 5.4 %all-to-all-start.1 = ((bf16[8,2,1120,128]{3,2,1,0:T(8,128)(2,1)}), bf16[8,2,1120,128]{3,2,1,0:T(8,128)(2,1)}, u32[]{:S(2)}, u32[]{:S(2)}) async-start(bf16[8,2,1120,128]{3,2,1,0:T(8,128)(2,1)} %branch_0_fun.9), calls=%async_computation.1 | async-start | bytes 9175040 | tf_op jit(solution)/shard_map/cond/branch_0_fun/all_to_all | solution.py:376
  57.0 4.7 %branch_0_fun.7 = bf16[8,1,1120,128]{3,2,1,0:T(8,128)(2,1)} custom-call(s32[8,4,128]{2,1,0:T(4,128)S(1)} %get-tuple-element.49.starts_ref, s32[8,4,2176]{2,1,0:T(4,128)S(1)} %get-tuple-element.50.plan_ref, bf16[26,2048,128]{2,1,0:T(8,128)(2,1)} %get-tuple-element.51.tables_ref), custom_call_target="tpu_custom_call" | custom-call | flops 41943040 | bytes 6291456 | tf_op jit(solution)/shard_map/cond/branch_0_fun/pallas_call | solution.py:206
  61.7 0.0 copy-start.15
  61.7 0.0 copy-start.12
  61.7 48.4 %all-to-all-done.1.grad_ref = bf16[8,2,1120,128]{3,2,1,0:T(8,128)(2,1)} async-done(((bf16[8,2,1120,128]{3,2,1,0:T(8,128)(2,1)}), bf16[8,2,1120,128]{3,2,1,0:T(8,128)(2,1)}, u32[]{:S(2)}, u32[]{:S(2)}) %all-to-all-start.1) | async-done | bytes 4587552 | tf_op jit(solution)/shard_map/cond/branch_0_fun/all_to_all | solution.py:376
  110.1 5.2 %all-to-all-start = ((bf16[8,1,1120,128]{3,2,1,0:T(8,128)(2,1)}), bf16[8,1,1120,128]{3,2,1,0:T(8,128)(2,1)}, u32[]{:S(2)}, u32[]{:S(2)}) async-start(bf16[8,1,1120,128]{3,2,1,0:T(8,128)(2,1)} %branch_0_fun.7), calls=%async_computation | async-start | bytes 4587520 | tf_op jit(solution)/shard_map/cond/branch_0_fun/all_to_all | solution.py:376
  115.3 1.1 copy.44
  116.5 0.0 copy-done.15
  116.5 1.1 branch_0_fun.8
  117.6 0.0 copy-start
  117.6 0.6 copy-done
  118.2 0.0 copy-start.1
  118.2 0.6 copy-done.1
  118.8 0.0 copy-start.6
  118.8 0.6 copy-done.6
  119.5 0.0 copy-start.9
  119.5 0.6 copy-done.9
  120.1 0.0 copy-done.12
  120.1 17.5 %branch_0_fun.11 = (bf16[4,16384,128]{2,1,0:T(8,128)(2,1)}, f32[4,16384]{1,0:T(4,128)}) custom-call(f32[1]{0:T(128)} %bitcast.lr_ref, bf16[8,1,1120,128]{3,2,1,0:T(8,128)(2,1)} %all-to-all-done.2.grad_ref, bf16[4,16384,128]{2,1,0:T(8,128)(2,1)} %get-tuple-element.130.tables_ref, f32[4,16384]{1,0:T(4,128)S(1)} %copy-done.12, s32[1,16512]{1,0:T(1,128)} %copy-done.6), custom_call_target="tpu_custom_call" | custom-call | flops 838860800 | bytes 16777216 | tf_op jit(solution)/shard_map/cond/branch_0_fun/pallas_call | solution.py:330
  137.6 32.7 %branch_0_fun.12 = (bf16[4,16384,128]{2,1,0:T(8,128)(2,1)}, f32[4,16384]{1,0:T(4,128)}) custom-call(f32[1]{0:T(128)} %bitcast.lr_ref, bf16[8,2,1120,128]{3,2,1,0:T(8,128)(2,1)} %all-to-all-done.1.grad_ref, bf16[4,16384,128]{2,1,0:T(8,128)(2,1)} %get-tuple-element.130.tables_ref, ...), custom_call_target="tpu_custom_call", output_to_operand_aliasing={{0}: (6, {}), {1}: (7, {})} | custom-call | flops 1677721600 | bytes 33554432 | tf_op jit(solution)/shard_map/cond/branch_0_fun/pallas_call | solution.py:330
  170.2 0.0 all-to-all-done.grad_ref
  170.2 17.5 %branch_0_fun.13 = (bf16[4,16384,128]{2,1,0:T(8,128)(2,1)}, f32[4,16384]{1,0:T(4,128)}) custom-call(f32[1]{0:T(128)} %bitcast.lr_ref, bf16[8,1,1120,128]{3,2,1,0:T(8,128)(2,1)} %all-to-all-done.grad_ref, bf16[4,16384,128]{2,1,0:T(8,128)(2,1)} %get-tuple-element.130.tables_ref, ...), custom_call_target="tpu_custom_call", output_to_operand_aliasing={{0}: (5, {}), {1}: (6, {})} | custom-call | flops 838860800 | bytes 16777216 | tf_op jit(solution)/shard_map/cond/branch_0_fun/pallas_call | solution.py:330
Async XLA Ops:
  18.5 33.1 %all-to-all-start.2 = ((bf16[8,1,1120,128]{3,2,1,0:T(8,128)(2,1)}), bf16[8,1,1120,128]{3,2,1,0:T(8,128)(2,1)}, u32[]{:S(2)}, u32[]{:S(2)}) async-start(bf16[8,1,1120,128]{3,2,1,0:T(8,128)(2,1)} %branch_0_fun.10), calls=%async_computation.2 | async-start | bytes 4587520 | tf_op jit(solution)/shard_map/cond/branch_0_fun/all_to_all | solution.py:376
  51.6 58.5 %all-to-all-start.1 = ((bf16[8,2,1120,128]{3,2,1,0:T(8,128)(2,1)}), bf16[8,2,1120,128]{3,2,1,0:T(8,128)(2,1)}, u32[]{:S(2)}, u32[]{:S(2)}) async-start(bf16[8,2,1120,128]{3,2,1,0:T(8,128)(2,1)} %branch_0_fun.9), calls=%async_computation.1 | async-start | bytes 9175040 | tf_op jit(solution)/shard_map/cond/branch_0_fun/all_to_all | solution.py:376
  61.7 54.8 %copy-start.15 = (s32[4,16384]{1,0:T(4,128)S(1)}, s32[4,16384]{1,0:T(4,128)}, u32[]{:S(2)}) copy-start(s32[4,16384]{1,0:T(4,128)} %get-tuple-element.55.lengths_ref) | copy-start | bytes 786436 | tf_op jit(solution)/shard_map/cond
  61.7 58.3 %copy-start.12 = (f32[4,16384]{1,0:T(4,128)S(1)}, f32[4,16384]{1,0:T(4,128)}, u32[]{:S(2)}) copy-start(f32[4,16384]{1,0:T(4,128)} %get-tuple-element.133.accums_ref) | copy-start | bytes 786436 | tf_op jit(solution)/shard_map/cond
  110.1 60.1 %all-to-all-start = ((bf16[8,1,1120,128]{3,2,1,0:T(8,128)(2,1)}), bf16[8,1,1120,128]{3,2,1,0:T(8,128)(2,1)}, u32[]{:S(2)}, u32[]{:S(2)}) async-start(bf16[8,1,1120,128]{3,2,1,0:T(8,128)(2,1)} %branch_0_fun.7), calls=%async_computation | async-start | bytes 4587520 | tf_op jit(solution)/shard_map/cond/branch_0_fun/all_to_all | solution.py:376
  117.6 0.6 copy-start
  118.2 0.6 copy-start.1
  118.8 0.6 copy-start.6
  119.5 0.6 copy-start.9

commit v8 on v7

--- a/solution.py
+++ b/solution.py
@@ -71,7 +71,7 @@
     )(lengths)
 
 
-def ids_kernel(n_dev, n_rows, ids_ref, lengths_ref, *refs):
+def ids_kernel(n_dev, n_rows, hop_slots, me_ref, ids_ref, lengths_ref, *refs):
     *packed_refs, ids_v, len_v = refs
     n_slots, batch = ids_ref.shape
     part, rows = batch // n_dev, n_dev * n_slots
@@ -95,27 +95,28 @@
         move = jnp.where((come & bit) != 0, come, stay)
         step *= 2
     spot = lax.broadcasted_iota(jnp.int32, (rows, part), 1)
-    packed = jnp.where(spot < count, move & 0xFFFF, n_rows)
+    ids_v[...] = jnp.where(spot < count, move & 0xFFFF, n_rows)
     most = jnp.max(count, axis=0, keepdims=True)
     for s in range(n_slots):
         for d in range(n_dev):
-            packed_refs[s][:, d * part:(d + 1) * part] = packed[d * n_slots + s:d * n_slots + s + 1, :]
+            sender = (me_ref[0] + (n_dev - d)) % n_dev if s in hop_slots else d
+            packed_refs[s][:, d * part:(d + 1) * part] = ids_v[pl.ds(sender * n_slots + s, 1), :]
         packed_refs[s][:, n_dev * part:] = jnp.broadcast_to(most, (1, BLOCK))
 
 
-def pack_ids(ids, lengths, n_dev, n_rows):
+def pack_ids(me, ids, lengths, n_dev, n_rows, hop_slots):
     n_slots, batch = ids.shape
     part = batch // n_dev
     assert n_rows < 1 << 15 and part <= 1 << 15
     return pl.pallas_call(
-        functools.partial(ids_kernel, n_dev, n_rows),
+        functools.partial(ids_kernel, n_dev, n_rows, hop_slots),
         out_shape=(jax.ShapeDtypeStruct((1, batch + BLOCK), jnp.int32),) * n_slots,
-        in_specs=[pl.BlockSpec(memory_space=pltpu.VMEM)] * 2,
+        in_specs=[pl.BlockSpec(memory_space=pltpu.SMEM)] + [pl.BlockSpec(memory_space=pltpu.VMEM)] * 2,
         out_specs=(pl.BlockSpec(memory_space=pltpu.VMEM),) * n_slots,
         scratch_shapes=[pltpu.VMEM((n_dev * n_slots, part), jnp.int32)] * 2,
         compiler_params=pltpu.CompilerParams(vmem_limit_bytes=32000000),
         cost_estimate=pl.CostEstimate(flops=20000000, bytes_accessed=2000000, transcendentals=0),
-    )(ids, lengths)
+    )(me, ids, lengths)
 
 
 def share_kernel(n_dev, plan_ref, plans_ref, starts_ref, most_ref, send_sem, recv_sem, own_sem):
@@ -220,28 +221,88 @@
     )(starts, plan, by_table)
 
 
-def apply_kernel(slots, n_carried, lr_ref, grad_ref, tables_ref, accums_ref, *refs):
+def pack_hops_kernel(slot, me_ref, starts_ref, plan_ref, tables_ref, *refs):
+    n_dev, n_slots, _ = plan_ref.shape
+    n_tab, part, _ = tables_ref.shape
+    out_refs, (grad_v, stage, pack_v, in_sem, out_sem) = refs[:n_dev], refs[n_dev:]
+    cap = pack_v.shape[1]
+    slot_row = lax.broadcasted_iota(jnp.int32, (BLOCK, BLOCK), 0)
+    me = me_ref[0]
+
+    def fetch(o):
+        table = jnp.minimum((me + o) % n_dev * n_slots + slot, n_tab - 1)
+        return pltpu.make_async_copy(tables_ref.at[table], grad_v.at[o], in_sem.at[o])
+
+    for o in range(n_dev):
+        fetch(o).start()
+
+    def one(o, carry):
+        d = (me + o) % n_dev
+        fetch(o).wait()
+
+        @pl.when(d * n_slots + slot < n_tab)
+        def _():
+            for b in range(part // BLOCK):
+                place = plan_ref[d, slot:slot + 1, b * BLOCK:(b + 1) * BLOCK]
+                pick = jnp.where(slot_row == place, 1.0, 0.0).astype(jnp.bfloat16)
+                rows = jnp.dot(pick, grad_v[o, b * BLOCK:(b + 1) * BLOCK, :], preferred_element_type=jnp.float32)
+                stage[pl.ds(starts_ref[d, slot, b], BLOCK), :] = rows
+            pack_v[o] = stage[:cap, :].astype(jnp.bfloat16)
+
+        return carry
+
+    lax.fori_loop(0, n_dev, one, 0)
+    copies = [pltpu.make_async_copy(pack_v.at[o], out_refs[o], out_sem.at[o]) for o in range(n_dev)]
+    for copy in copies:
+        copy.start()
+    for copy in copies:
+        copy.wait()
+
+
+def pack_hops(slot, cap, me, starts, plan, by_table):
+    n_dev, _, _ = plan.shape
+    _, part, dim = by_table.shape
+    return pl.pallas_call(
+        functools.partial(pack_hops_kernel, slot),
+        out_shape=(jax.ShapeDtypeStruct((cap, dim), by_table.dtype),) * n_dev,
+        in_specs=[pl.BlockSpec(memory_space=pltpu.SMEM)] * 2 + [pl.BlockSpec(memory_space=pltpu.VMEM), pl.BlockSpec(memory_space=pl.ANY)],
+        out_specs=(pl.BlockSpec(memory_space=pl.ANY),) * n_dev,
+        scratch_shapes=[
+            pltpu.VMEM((n_dev, part, dim), by_table.dtype),
+            pltpu.VMEM((cap + BLOCK, dim), jnp.float32),
+            pltpu.VMEM((n_dev, cap, dim), by_table.dtype),
+            pltpu.SemaphoreType.DMA((n_dev,)),
+            pltpu.SemaphoreType.DMA((n_dev,)),
+        ],
+        compiler_params=pltpu.CompilerParams(vmem_limit_bytes=VMEM_LIMIT),
+        cost_estimate=pl.CostEstimate(flops=n_dev * part * dim * 20, bytes_accessed=n_dev * part * dim * 3, transcendentals=0),
+    )(me, starts, plan, by_table)
+
+
+def apply_kernel(slots, n_carried, n_grads, lr_ref, tables_ref, accums_ref, *refs):
     n = len(slots)
+    grad_refs, refs = refs[:n_grads], refs[n_grads:]
     ids_refs, carried_refs = refs[:n], refs[n:n + n_carried]
     out_tables_ref, out_accums_ref, *scratch = refs[n + n_carried:]
-    banks, (stage, table_v, grad_v, done_v, sem, out_sem, ids_sem), scalars = scratch[:BANKS], scratch[BANKS:BANKS + 7], scratch[BANKS + 7:]
+    banks, (stage, table_v, grad_v, done_v, sem, out_sem, ids_sem, grad_sem), scalars = scratch[:BANKS], scratch[BANKS:BANKS + 8], scratch[BANKS + 8:]
     _, segs, seg_rows, dim = grad_v.shape
     part = (ids_refs[0].shape[1] - BLOCK) // segs
     ids_s = [scalars[i * (segs + 1):(i + 1) * (segs + 1)] for i in range(n)]
     n_rows = tables_ref.shape[1]
     copies = [
         (
-            pltpu.make_async_copy(grad_ref.at[:, i], grad_v.at[i], sem.at[i, 0]),
+            [pltpu.make_async_copy(ref, grad_v.at[i, o], grad_sem.at[i, o]) for o, ref in enumerate(grad_refs)]
+            if n_grads > 1
+            else [pltpu.make_async_copy(grad_refs[0].at[:, i], grad_v.at[i], grad_sem.at[i, 0])],
             [pltpu.make_async_copy(ids_refs[i].at[:, j * part:(j + 1) * part], ids_s[i][j], ids_sem.at[i, j]) for j in range(segs)]
             + [pltpu.make_async_copy(ids_refs[i].at[:, segs * part:], ids_s[i][segs], ids_sem.at[i, segs])],
-            pltpu.make_async_copy(tables_ref.at[slot], table_v.at[i], sem.at[i, 2]),
+            pltpu.make_async_copy(tables_ref.at[slot], table_v.at[i], sem.at[i]),
         )
         for i, slot in enumerate(slots)
     ]
-    for grad_copy, ids_copies, table_copy in copies:
-        for copy in ids_copies:
+    for grad_copies, ids_copies, table_copy in copies:
+        for copy in ids_copies + grad_copies:
             copy.start()
-        grad_copy.start()
         table_copy.start()
 
     if n_carried:
@@ -261,10 +322,9 @@
     lr = lr_ref[0]
 
     for i, slot in enumerate(slots):
-        grad_copy, ids_copies, table_copy = copies[i]
-        for copy in ids_copies:
+        grad_copies, ids_copies, table_copy = copies[i]
+        for copy in ids_copies + grad_copies:
             copy.wait()
-        grad_copy.wait()
 
         def widen(t, carry):
             for j in range(segs):
@@ -322,35 +382,41 @@
     pltpu.make_async_copy(done_v, out_accums_ref, out_sem.at[n]).wait()
 
 
-def apply_slots(slots, ids, lr, grad, tables, accums, carried):
+def apply_slots(slots, ids, lr, grads, tables, accums, carried):
     _, n_rows, dim = tables.shape
-    segs, n, seg_rows, _ = grad.shape
+    n, segs = len(slots), (len(grads) if len(grads) > 1 else grads[0].shape[0])
+    seg_rows = grads[0].shape[-2]
     part = (ids[0].shape[1] - BLOCK) // segs
     assert segs == 2 * BANKS
     return pl.pallas_call(
-        functools.partial(apply_kernel, slots, len(carried)),
+        functools.partial(apply_kernel, slots, len(carried), len(grads)),
         out_shape=tuple(jax.ShapeDtypeStruct(x.shape, x.dtype) for x in (tables, accums)),
         in_specs=[pl.BlockSpec(memory_space=pltpu.SMEM)]
-        + [pl.BlockSpec(memory_space=pl.ANY)] * 2
-        + [pl.BlockSpec(memory_space=pltpu.VMEM)]
-        + [pl.BlockSpec(memory_space=pl.ANY)] * n
+        + [pl.BlockSpec(memory_space=pl.ANY), pl.BlockSpec(memory_space=pltpu.VMEM)]
+        + [pl.BlockSpec(memory_space=pl.ANY)] * (len(grads) + n)
         + [pl.BlockSpec(memory_space=pl.ANY)] * len(carried),
         out_specs=(pl.BlockSpec(memory_space=pl.ANY),) * 2,
-        input_output_aliases={4 + n: 0, 5 + n: 1} if carried else {},
+        input_output_aliases={3 + len(grads) + n + i: i for i in range(len(carried))},
         scratch_shapes=[pltpu.VMEM((n_rows + 8, dim), jnp.float32)] * BANKS
         + [
             pltpu.VMEM((segs, seg_rows, dim), jnp.float32),
             pltpu.VMEM((n, n_rows, dim), tables.dtype),
-            pltpu.VMEM((n, segs, seg_rows, dim), grad.dtype),
+            pltpu.VMEM((n, segs, seg_rows, dim), grads[0].dtype),
             pltpu.VMEM(accums.shape, accums.dtype),
-            pltpu.SemaphoreType.DMA((n, 3)),
+            pltpu.SemaphoreType.DMA((n,)),
             pltpu.SemaphoreType.DMA((n + 1,)),
             pltpu.SemaphoreType.DMA((n, segs + 1)),
+            pltpu.SemaphoreType.DMA((n, segs)),
         ]
         + ([pltpu.SMEM((1, part), jnp.int32)] * segs + [pltpu.SMEM((1, BLOCK), jnp.int32)]) * n,
         compiler_params=pltpu.CompilerParams(vmem_limit_bytes=VMEM_LIMIT),
         cost_estimate=pl.CostEstimate(flops=n * n_rows * dim * 400, bytes_accessed=4 * n * n_rows * dim * 2, transcendentals=0),
-    )(lr, grad, tables, accums, *(ids[k] for k in slots), *carried)
+    )(lr, tables, accums, *grads, *(ids[k] for k in slots), *carried)
+
+
+def routes(n_dev, n_slots, n_tab, slot, offset):
+    pairs = [(d, (d + offset) % n_dev) for d in range(n_dev)]
+    return [(src, dst) for src, dst in pairs if dst * n_slots + slot < n_tab]
 
 
 def solution(mesh):
@@ -361,6 +427,8 @@
         n_slots, n_rows, _ = tables.shape
         by_table = jnp.transpose(d_pool, (1, 0, 2))
         part = by_table.shape[1]
+        me = lax.axis_index('mp').reshape(1)
+        n_tab = by_table.shape[0]
         plan_out = make_plan(lengths, n_group)
         plan, starts, most = share_plan(plan_out)
         most = most[0]
@@ -369,21 +437,29 @@
 
         def exchange(level):
             def run(operands):
-                by_table, plan, starts, row_ids, lengths, lr, tables, accums = operands
-                got = []
-                for slots in CHUNKS(n_slots):
-                    pack = pack_slots(slots, caps[level], starts, plan, by_table)
-                    got.append(lax.all_to_all(pack, 'mp', 0, 0, tiled=True))
-                ids = pack_ids(row_ids[:, :, 0], lengths, n_group, n_rows)
+                me, by_table, plan, starts, row_ids, lengths, lr, tables, accums = operands
+                got = {}
+                chunks, hop_slots = CHUNKS(n_slots)
+                for c, slots in enumerate(chunks):
+                    if slots == hop_slots:
+                        pack = pack_hops(slots[0], caps[level], me, starts, plan, by_table)
+                    else:
+                        pack = pack_slots(slots, caps[level], starts, plan, by_table)
+                    if slots == hop_slots:
+                        hops = [lax.ppermute(pack[o], 'mp', routes(n_group, n_slots, n_tab, slots[0], o)) for o in range(1, n_group)]
+                        got[c] = [pack[0]] + hops
+                    else:
+                        got[c] = [lax.all_to_all(pack, 'mp', 0, 0, tiled=True)]
+                ids = pack_ids(me, row_ids[:, :, 0], lengths, n_group, n_rows, hop_slots)
                 carried = ()
-                for c, slots in enumerate(CHUNKS(n_slots)):
+                for c, slots in enumerate(chunks):
                     carried = apply_slots(slots, ids, lr, got[c], tables, accums, carried)
                 return tuple(carried)
 
             return run
 
         level = sum((most > cap).astype(jnp.int32) for cap in caps[:-1])
-        operands = (by_table, plan, starts, row_ids, lengths, lr, tables, row_accum)
+        operands = (me, by_table, plan, starts, row_ids, lengths, lr, tables, row_accum)
         return lax.switch(level, [exchange(i) for i in range(len(caps))], operands)
 
     return jax.shard_map(local_step, mesh=mesh, in_specs=(slot_spec, slot_spec, slot_spec, slot_spec, slot_spec, P()), out_specs=(slot_spec, slot_spec), check_vma=False)
@@ -394,4 +470,4 @@
 
 
 def CHUNKS(n_slots):
-    return (0,), tuple(range(1, n_slots - 1)), (n_slots - 1,)
+    return tuple((k,) for k in range(n_slots)), (n_slots - 2,)

time: 190 us -> 221 us (1.16)
  starting transfers between devices: 15.2 us -> 32.4 us
  waiting for transfers between devices: 69.8 us -> 79.1 us
  Pallas kernels: 97 us -> 103 us
    ppermute x0 -> x7, waiting for transfers between devices: none -> 31.8 us  [run(): lax.ppermute(pack[o], 'mp', routes(n_group, n_slots, n_tab, slots[0], o))]
    all_to_all x3, waiting for transfers between devices: 69.8 us -> 47.4 us  [run(): got[c] = [lax.all_to_all(pack, 'mp', 0, 0, tiled=True)]]
    ppermute x0 -> x7, starting transfers between devices: none -> 17.4 us  [run(): lax.ppermute(pack[o], 'mp', routes(n_group, n_slots, n_tab, slots[0], o))]
    pallas_call x4 -> x6, Pallas kernels: 68.7 us -> 76.6 us  [the longest x4 70.1 us: apply_slots(): pl.pallas_call(functools.partial(apply_kernel, slots, len(carried), len(g...]
  transfers between devices with their start and end apart: 3 -> 10, of which waited for: 2 -> 4; matrix products, arithmetic and copies ran while one was open for 1% -> 1% of each run, Pallas kernels for 33% -> 31%
where the time goes in v8:
time: 221 us; the launch traced here: 220 us
  Pallas kernels  103 us (47%)
  waiting for transfers between devices  79.1 us (36%)
  starting transfers between devices  32.4 us (15%)
  local copies, waits for them, and re-layouts  3.62 us (2%)
    pallas_call x4, Pallas kernels, apply_slots(): pl.pallas_call(functools.partial(apply_kernel, slots, len(carried), len(g...  70.1 us
    all_to_all x3, waiting for transfers between devices, run(): got[c] = [lax.all_to_all(pack, 'mp', 0, 0, tiled=True)]  47.4 us
    ppermute x7, waiting for transfers between devices, run(): lax.ppermute(pack[o], 'mp', routes(n_group, n_slots, n_tab, slots[0], o))  31.8 us
    ppermute x7, starting transfers between devices, run(): lax.ppermute(pack[o], 'mp', routes(n_group, n_slots, n_tab, slots[0], o))  17.4 us
    all_to_all x3, starting transfers between devices, run(): got[c] = [lax.all_to_all(pack, 'mp', 0, 0, tiled=True)]  15.1 us
    pallas_call x3, Pallas kernels, pack_slots(): pl.pallas_call(functools.partial(pack_kernel, slots), out_shape=jax.Shape...  14.7 us
    pallas_call x1, Pallas kernels, share_plan(): pl.pallas_call(functools.partial(share_kernel, n_dev), out_shape=(jax.Sha...  10.4 us
    pallas_call x1, Pallas kernels, pack_hops(): pl.pallas_call(functools.partial(pack_hops_kernel, slot), out_shape=(jax....  5.4 us
  transfers between devices with their start and end apart: 10, of which 4 were waited for; matrix products, arithmetic and copies ran while one was open for 1% of the time, Pallas kernels for 31%

profile of v8, /device:TPU:81, one launch (start us, length us, event | category | flops | bytes accessed | tf_op | source)
XLA Modules:
  0.0 220.4 jit_solution(12002810973471146435)
XLA Ops:
  0.6 1.2 shard_map.95.plan_ref
  1.8 10.4 %shard_map.96 = (s32[8,4,2176]{2,1,0:T(4,128)S(1)}, s32[8,4,128]{2,1,0:T(4,128)S(1)}, s32[1]{0:T(128)}) custom-call(s32[8,4,2176]{2,1,0:T(4,128)S(1)} %shard_map.95.plan_ref), custom_call_target="tpu_custom_call" | custom-call | flops 20000000 | bytes 2000000 | tf_op jit(solution)/shard_map/pallas_call | solution.py:154
  13.4 206.9 %conditional.1 = ((bf16[4,16384,128]{2,1,0:T(8,128)(2,1)}, f32[4,16384]{1,0:T(4,128)})) conditional(s32[]{:T(128)} %bitcast.9, (s32[8,4,128]{2,1,0:T(4,128)S(1)}, s32[8,4,2176]{2,1,0:T(4,128)S(1)}, bf16[26,2048,128]{2,1,0:T(8,128)(2,1)}, s32[4,16384,1]{1,2,0:T(1,128)}, s32[]{:T(128)}, /*index=5*/s32[4,16384]{1,0:T(4,128)}, ...), branch_computations={%region_0.0_spmd, %region_1.0_spmd, %region_2.0_spmd} | conditional | flops 3543215360 | bytes 154576608 | solution.py:463
  13.4 5.0 %branch_0_fun.13 = bf16[8,1,1120,128]{3,2,1,0:T(8,128)(2,1)} custom-call(s32[8,4,128]{2,1,0:T(4,128)S(1)} %get-tuple-element.57.starts_ref, s32[8,4,2176]{2,1,0:T(4,128)S(1)} %get-tuple-element.58.plan_ref, bf16[26,2048,128]{2,1,0:T(8,128)(2,1)} %get-tuple-element.59.tables_ref), custom_call_target="tpu_custom_call" | custom-call | flops 41943040 | bytes 6291456 | tf_op jit(solution)/shard_map/cond/branch_0_fun/pallas_call | solution.py:207
  18.4 4.6 %all-to-all-start.2 = ((bf16[8,1,1120,128]{3,2,1,0:T(8,128)(2,1)}), bf16[8,1,1120,128]{3,2,1,0:T(8,128)(2,1)}, u32[]{:S(2)}, u32[]{:S(2)}) async-start(bf16[8,1,1120,128]{3,2,1,0:T(8,128)(2,1)} %branch_0_fun.13), calls=%async_computation.2 | async-start | bytes 4587520 | tf_op jit(solution)/shard_map/cond/branch_0_fun/all_to_all | solution.py:452
  23.0 5.0 %branch_0_fun.12 = bf16[8,1,1120,128]{3,2,1,0:T(8,128)(2,1)} custom-call(s32[8,4,128]{2,1,0:T(4,128)S(1)} %get-tuple-element.57.starts_ref, s32[8,4,2176]{2,1,0:T(4,128)S(1)} %get-tuple-element.58.plan_ref, bf16[26,2048,128]{2,1,0:T(8,128)(2,1)} %get-tuple-element.59.tables_ref), custom_call_target="tpu_custom_call" | custom-call | flops 41943040 | bytes 6291456 | tf_op jit(solution)/shard_map/cond/branch_0_fun/pallas_call | solution.py:207
  28.0 23.5 %all-to-all-done.2.refs_0_ = bf16[8,1,1120,128]{3,2,1,0:T(8,128)(2,1)} async-done(((bf16[8,1,1120,128]{3,2,1,0:T(8,128)(2,1)}), bf16[8,1,1120,128]{3,2,1,0:T(8,128)(2,1)}, u32[]{:S(2)}, u32[]{:S(2)}) %all-to-all-start.2) | async-done | bytes 2293792 | tf_op jit(solution)/shard_map/cond/branch_0_fun/all_to_all | solution.py:452
  51.6 5.2 %all-to-all-start.1 = ((bf16[8,1,1120,128]{3,2,1,0:T(8,128)(2,1)}), bf16[8,1,1120,128]{3,2,1,0:T(8,128)(2,1)}, u32[]{:S(2)}, u32[]{:S(2)}) async-start(bf16[8,1,1120,128]{3,2,1,0:T(8,128)(2,1)} %branch_0_fun.12), calls=%async_computation.1 | async-start | bytes 4587520 | tf_op jit(solution)/shard_map/cond/branch_0_fun/all_to_all | solution.py:452
  56.8 4.7 %branch_0_fun.9 = bf16[8,1,1120,128]{3,2,1,0:T(8,128)(2,1)} custom-call(s32[8,4,128]{2,1,0:T(4,128)S(1)} %get-tuple-element.57.starts_ref, s32[8,4,2176]{2,1,0:T(4,128)S(1)} %get-tuple-element.58.plan_ref, bf16[26,2048,128]{2,1,0:T(8,128)(2,1)} %get-tuple-element.59.tables_ref), custom_call_target="tpu_custom_call" | custom-call | flops 41943040 | bytes 6291456 | tf_op jit(solution)/shard_map/cond/branch_0_fun/pallas_call | solution.py:207
  61.4 23.8 %all-to-all-done.1.refs_0_ = bf16[8,1,1120,128]{3,2,1,0:T(8,128)(2,1)} async-done(((bf16[8,1,1120,128]{3,2,1,0:T(8,128)(2,1)}), bf16[8,1,1120,128]{3,2,1,0:T(8,128)(2,1)}, u32[]{:S(2)}, u32[]{:S(2)}) %all-to-all-start.1) | async-done | bytes 2293792 | tf_op jit(solution)/shard_map/cond/branch_0_fun/all_to_all | solution.py:452
  85.3 5.2 %all-to-all-start = ((bf16[8,1,1120,128]{3,2,1,0:T(8,128)(2,1)}), bf16[8,1,1120,128]{3,2,1,0:T(8,128)(2,1)}, u32[]{:S(2)}, u32[]{:S(2)}) async-start(bf16[8,1,1120,128]{3,2,1,0:T(8,128)(2,1)} %branch_0_fun.9), calls=%async_computation | async-start | bytes 4587520 | tf_op jit(solution)/shard_map/cond/branch_0_fun/all_to_all | solution.py:452
  90.5 0.0 copy-start.15
  90.5 0.0 copy-start.12
  90.5 5.4 %branch_0_fun.11 = (bf16[1120,128]{1,0:T(8,128)(2,1)}, bf16[1120,128]{1,0:T(8,128)(2,1)}, bf16[1120,128]{1,0:T(8,128)(2,1)}, bf16[1120,128]{1,0:T(8,128)(2,1)}, ...) custom-call(s32[1]{0:T(128)} %bitcast.1.me_ref, ...), custom_call_target="tpu_custom_call" | custom-call | flops 41943040 | bytes 6291456 | tf_op jit(solution)/shard_map/cond/branch_0_fun/pallas_call | solution.py:265
  95.9 3.6 %collective-permute-start = (bf16[1120,128]{1,0:T(8,128)(2,1)}, bf16[1120,128]{1,0:T(8,128)(2,1)S(1)}, u32[]{:S(2)}, u32[]{:S(2)}) collective-permute-start(bf16[1120,128]{1,0:T(8,128)(2,1)} %get-tuple-element.65), channel_id=1, source_target_pairs={{0,1},{1,2},{2,3},{3,4},{4,5},{7,0},{8,9},{9,10},{10,11},{11,12},{... | collective-permute-start | bytes 860168 | tf_op jit(solution)/shard_map/cond/branch_0_fun/ppermute | solution.py:449
  99.5 3.5 %collective-permute-start.1 = (bf16[1120,128]{1,0:T(8,128)(2,1)}, bf16[1120,128]{1,0:T(8,128)(2,1)S(1)}, u32[]{:S(2)}, u32[]{:S(2)}) collective-permute-start(bf16[1120,128]{1,0:T(8,128)(2,1)} %get-tuple-element.66), channel_id=1, source_target_pairs={{0,2},{1,3},{2,4},{3,5},{6,0},{7,1},{8,10},{9,11},{10,12},{11,13},... | collective-permute-start | bytes 860168 | tf_op jit(solution)/shard_map/cond/branch_0_fun/ppermute | solution.py:449
  103.0 2.0 collective-permute-start.2
  105.0 3.8 %collective-permute-start.3 = (bf16[1120,128]{1,0:T(8,128)(2,1)}, bf16[1120,128]{1,0:T(8,128)(2,1)}, u32[]{:S(2)}, u32[]{:S(2)}) collective-permute-start(bf16[1120,128]{1,0:T(8,128)(2,1)} %get-tuple-element.68), channel_id=1, source_target_pairs={{0,4},{1,5},{4,0},{5,1},{6,2},{7,3},{8,12},{9,13},{12,8},{13,9},{1... | collective-permute-start | bytes 860168 | tf_op jit(solution)/shard_map/cond/branch_0_fun/ppermute | solution.py:449
  108.8 1.3 collective-permute-start.4
  110.1 11.7 %collective-permute-done.refs_1_ = bf16[1120,128]{1,0:T(8,128)(2,1)S(1)} collective-permute-done((bf16[1120,128]{1,0:T(8,128)(2,1)}, bf16[1120,128]{1,0:T(8,128)(2,1)S(1)}, u32[]{:S(2)}, u32[]{:S(2)}) %collective-permute-start) | collective-permute-done | bytes 286752 | tf_op jit(solution)/shard_map/cond/branch_0_fun/ppermute | solution.py:449
  121.7 0.0 copy-start.22
  121.7 1.3 collective-permute-start.5
  123.0 20.1 %collective-permute-done.1.refs_2_ = bf16[1120,128]{1,0:T(8,128)(2,1)S(1)} collective-permute-done((bf16[1120,128]{1,0:T(8,128)(2,1)}, bf16[1120,128]{1,0:T(8,128)(2,1)S(1)}, u32[]{:S(2)}, u32[]{:S(2)}) %collective-permute-start.1) | collective-permute-done | bytes 286752 | tf_op jit(solution)/shard_map/cond/branch_0_fun/ppermute | solution.py:449
  143.1 0.0 copy-start.23
  143.1 1.9 collective-permute-start.6
  145.1 0.0 copy-done.22
  145.1 0.0 copy-done.23
  145.1 1.1 copy.50
  146.2 0.0 copy-done.15
  146.2 1.1 branch_0_fun.10
  147.3 0.0 copy-start
  147.3 0.6 copy-done
  148.0 0.0 copy-start.3
  148.0 0.6 copy-done.3
  148.6 0.0 copy-start.6
  148.6 0.6 copy-done.6
  149.2 0.6 copy-done.9
  149.8 0.0 copy-done.12
  149.8 17.5 %branch_0_fun.14 = (bf16[4,16384,128]{2,1,0:T(8,128)(2,1)}, f32[4,16384]{1,0:T(4,128)}) custom-call(f32[1]{0:T(128)} %bitcast.lr_ref, bf16[4,16384,128]{2,1,0:T(8,128)(2,1)} %get-tuple-element.172.tables_ref, f32[4,16384]{1,0:T(4,128)S(1)} %copy-done.12, bf16[8,1,1120,128]{3,2,1,0:T(8,128)(2,1)} %all-to-all-done.2.refs_0_, s32[1,16512]{1,0:T(1,128)} %copy-done), custom_call_target="tpu_custom_call" | custom-call | flops 838860800 | bytes 16777216 | tf_op jit(solution)/shard_map/cond/branch_0_fun/pallas_call | solution.py:391
  167.4 17.5 %branch_0_fun.15 = (bf16[4,16384,128]{2,1,0:T(8,128)(2,1)}, f32[4,16384]{1,0:T(4,128)}) custom-call(f32[1]{0:T(128)} %bitcast.lr_ref, bf16[4,16384,128]{2,1,0:T(8,128)(2,1)} %get-tuple-element.172.tables_ref, f32[4,16384]{1,0:T(4,128)S(1)} %copy-done.12, ...), custom_call_target="tpu_custom_call", output_to_operand_aliasing={{0}: (5, {}), {1}: (6, {})} | custom-call | flops 838860800 | bytes 16777216 | tf_op jit(solution)/shard_map/cond/branch_0_fun/pallas_call | solution.py:391
  184.9 0.0 collective-permute-done.2.refs_3_
  184.9 0.0 collective-permute-done.3.refs_4_
  184.9 0.0 collective-permute-done.4.refs_5_
  184.9 0.0 collective-permute-done.5.refs_6_
  184.9 0.0 collective-permute-done.6.refs_7_
  185.0 17.5 %branch_0_fun.16 = (bf16[4,16384,128]{2,1,0:T(8,128)(2,1)}, f32[4,16384]{1,0:T(4,128)}) custom-call(f32[1]{0:T(128)} %bitcast.lr_ref, bf16[4,16384,128]{2,1,0:T(8,128)(2,1)} %get-tuple-element.172.tables_ref, f32[4,16384]{1,0:T(4,128)S(1)} %copy-done.12, ...), custom_call_target="tpu_custom_call", output_to_operand_aliasing={{0}: (12, {}), {1}: (13, {})} | custom-call | flops 838860800 | bytes 16777216 | tf_op jit(solution)/shard_map/cond/branch_0_fun/pallas_call | solution.py:391
  202.5 0.0 all-to-all-done.refs_0_
  202.5 17.5 %branch_0_fun.17 = (bf16[4,16384,128]{2,1,0:T(8,128)(2,1)}, f32[4,16384]{1,0:T(4,128)}) custom-call(f32[1]{0:T(128)} %bitcast.lr_ref, bf16[4,16384,128]{2,1,0:T(8,128)(2,1)} %get-tuple-element.172.tables_ref, f32[4,16384]{1,0:T(4,128)S(1)} %copy-done.12, ...), custom_call_target="tpu_custom_call", output_to_operand_aliasing={{0}: (5, {}), {1}: (6, {})} | custom-call | flops 838860800 | bytes 16777216 | tf_op jit(solution)/shard_map/cond/branch_0_fun/pallas_call | solution.py:391
  (1 shorter events, 0.0 us)
Async XLA Ops:
  18.4 33.1 %all-to-all-start.2 = ((bf16[8,1,1120,128]{3,2,1,0:T(8,128)(2,1)}), bf16[8,1,1120,128]{3,2,1,0:T(8,128)(2,1)}, u32[]{:S(2)}, u32[]{:S(2)}) async-start(bf16[8,1,1120,128]{3,2,1,0:T(8,128)(2,1)} %branch_0_fun.13), calls=%async_computation.2 | async-start | bytes 4587520 | tf_op jit(solution)/shard_map/cond/branch_0_fun/all_to_all | solution.py:452
  51.6 33.7 %all-to-all-start.1 = ((bf16[8,1,1120,128]{3,2,1,0:T(8,128)(2,1)}), bf16[8,1,1120,128]{3,2,1,0:T(8,128)(2,1)}, u32[]{:S(2)}, u32[]{:S(2)}) async-start(bf16[8,1,1120,128]{3,2,1,0:T(8,128)(2,1)} %branch_0_fun.12), calls=%async_computation.1 | async-start | bytes 4587520 | tf_op jit(solution)/shard_map/cond/branch_0_fun/all_to_all | solution.py:452
  85.3 117.2 %all-to-all-start = ((bf16[8,1,1120,128]{3,2,1,0:T(8,128)(2,1)}), bf16[8,1,1120,128]{3,2,1,0:T(8,128)(2,1)}, u32[]{:S(2)}, u32[]{:S(2)}) async-start(bf16[8,1,1120,128]{3,2,1,0:T(8,128)(2,1)} %branch_0_fun.9), calls=%async_computation | async-start | bytes 4587520 | tf_op jit(solution)/shard_map/cond/branch_0_fun/all_to_all | solution.py:452
  90.5 55.7 %copy-start.15 = (s32[4,16384]{1,0:T(4,128)S(1)}, s32[4,16384]{1,0:T(4,128)}, u32[]{:S(2)}) copy-start(s32[4,16384]{1,0:T(4,128)} %get-tuple-element.62.lengths_ref) | copy-start | bytes 786436 | tf_op jit(solution)/shard_map/cond
  90.5 59.3 %copy-start.12 = (f32[4,16384]{1,0:T(4,128)S(1)}, f32[4,16384]{1,0:T(4,128)}, u32[]{:S(2)}) copy-start(f32[4,16384]{1,0:T(4,128)} %get-tuple-element.175.accums_ref) | copy-start | bytes 786436 | tf_op jit(solution)/shard_map/cond
  95.9 25.8 %collective-permute-start = (bf16[1120,128]{1,0:T(8,128)(2,1)}, bf16[1120,128]{1,0:T(8,128)(2,1)S(1)}, u32[]{:S(2)}, u32[]{:S(2)}) collective-permute-start(bf16[1120,128]{1,0:T(8,128)(2,1)} %get-tuple-element.65), channel_id=1, source_target_pairs={{0,1},{1,2},{2,3},{3,4},{4,5},{7,0},{8,9},{9,10},{10,11},{11,12},{... | collective-permute-start | bytes 860168 | tf_op jit(solution)/shard_map/cond/branch_0_fun/ppermute | solution.py:449
  99.5 43.6 %collective-permute-start.1 = (bf16[1120,128]{1,0:T(8,128)(2,1)}, bf16[1120,128]{1,0:T(8,128)(2,1)S(1)}, u32[]{:S(2)}, u32[]{:S(2)}) collective-permute-start(bf16[1120,128]{1,0:T(8,128)(2,1)} %get-tuple-element.66), channel_id=1, source_target_pairs={{0,2},{1,3},{2,4},{3,5},{6,0},{7,1},{8,10},{9,11},{10,12},{11,13},... | collective-permute-start | bytes 860168 | tf_op jit(solution)/shard_map/cond/branch_0_fun/ppermute | solution.py:449
  103.0 81.9 %collective-permute-start.2 = (bf16[1120,128]{1,0:T(8,128)(2,1)}, bf16[1120,128]{1,0:T(8,128)(2,1)}, u32[]{:S(2)}, u32[]{:S(2)}) collective-permute-start(bf16[1120,128]{1,0:T(8,128)(2,1)} %get-tuple-element.67), channel_id=1, source_target_pairs={{0,3},{1,4},{2,5},{5,0},{6,1},{7,2},{8,11},{9,12},{10,13},{13,8},{... | collective-permute-start | bytes 860168 | tf_op jit(solution)/shard_map/cond/branch_0_fun/ppermute | solution.py:449
  105.0 80.0 %collective-permute-start.3 = (bf16[1120,128]{1,0:T(8,128)(2,1)}, bf16[1120,128]{1,0:T(8,128)(2,1)}, u32[]{:S(2)}, u32[]{:S(2)}) collective-permute-start(bf16[1120,128]{1,0:T(8,128)(2,1)} %get-tuple-element.68), channel_id=1, source_target_pairs={{0,4},{1,5},{4,0},{5,1},{6,2},{7,3},{8,12},{9,13},{12,8},{13,9},{1... | collective-permute-start | bytes 860168 | tf_op jit(solution)/shard_map/cond/branch_0_fun/ppermute | solution.py:449
  108.8 76.2 %collective-permute-start.4 = (bf16[1120,128]{1,0:T(8,128)(2,1)}, bf16[1120,128]{1,0:T(8,128)(2,1)}, u32[]{:S(2)}, u32[]{:S(2)}) collective-permute-start(bf16[1120,128]{1,0:T(8,128)(2,1)} %get-tuple-element.69), channel_id=1, source_target_pairs={{0,5},{3,0},{4,1},{5,2},{6,3},{7,4},{8,13},{11,8},{12,9},{13,10},{... | collective-permute-start | bytes 860168 | tf_op jit(solution)/shard_map/cond/branch_0_fun/ppermute | solution.py:449
  121.7 23.4 %copy-start.22 = (bf16[1120,128]{1,0:T(8,128)(2,1)}, bf16[1120,128]{1,0:T(8,128)(2,1)S(1)}, u32[]{:S(2)}) copy-start(bf16[1120,128]{1,0:T(8,128)(2,1)S(1)} %collective-permute-done.refs_1_) | copy-start | bytes 860164 | tf_op jit(solution)/shard_map/cond
  121.7 63.2 %collective-permute-start.5 = (bf16[1120,128]{1,0:T(8,128)(2,1)}, bf16[1120,128]{1,0:T(8,128)(2,1)}, u32[]{:S(2)}, u32[]{:S(2)}) collective-permute-start(bf16[1120,128]{1,0:T(8,128)(2,1)} %get-tuple-element.70), channel_id=1, source_target_pairs={{2,0},{3,1},{4,2},{5,3},{6,4},{7,5},{10,8},{11,9},{12,10},{13,11},... | collective-permute-start | bytes 860168 | tf_op jit(solution)/shard_map/cond/branch_0_fun/ppermute | solution.py:449
  143.1 2.0 copy-start.23
  143.1 41.8 %collective-permute-start.6 = (bf16[1120,128]{1,0:T(8,128)(2,1)}, bf16[1120,128]{1,0:T(8,128)(2,1)}, u32[]{:S(2)}, u32[]{:S(2)}) collective-permute-start(bf16[1120,128]{1,0:T(8,128)(2,1)} %get-tuple-element.71), channel_id=1, source_target_pairs={{1,0},{2,1},{3,2},{4,3},{5,4},{6,5},{9,8},{10,9},{11,10},{12,11},{... | collective-permute-start | bytes 860168 | tf_op jit(solution)/shard_map/cond/branch_0_fun/ppermute | solution.py:449
  147.3 0.6 copy-start
  148.0 0.6 copy-start.3
  148.6 0.6 copy-start.6
  149.2 0.6 copy-start.9

commit v9 on v8

--- a/solution.py
+++ b/solution.py
@@ -119,7 +119,7 @@
     )(me, ids, lengths)
 
 
-def share_kernel(n_dev, plan_ref, plans_ref, starts_ref, most_ref, send_sem, recv_sem, own_sem):
+def share_kernel(n_dev, caps, plan_ref, plans_ref, starts_ref, level_ref, send_sem, recv_sem, own_sem):
     pod, me = lax.axis_index('pod'), lax.axis_index('mp')
     barrier = pltpu.get_barrier_semaphore()
     for o in range(1, n_dev):
@@ -146,13 +146,14 @@
     part = plans_ref.shape[2] - BLOCK
     starts = plans_ref[:, :, part:]
     starts_ref[...] = starts
-    most_ref[0] = jnp.max(starts[:, :, MAX_LANE:MAX_LANE + 1])
-
-
-def share_plan(plan):
+    most = jnp.max(starts[:, :, MAX_LANE:MAX_LANE + 1])
+    level_ref[0] = sum((most > cap).astype(jnp.int32) for cap in caps[:-1])
+
+
+def share_plan(plan, caps):
     n_dev, n_slots, _ = plan.shape
     return pl.pallas_call(
-        functools.partial(share_kernel, n_dev),
+        functools.partial(share_kernel, n_dev, caps),
         out_shape=(
             jax.ShapeDtypeStruct(plan.shape, plan.dtype),
             jax.ShapeDtypeStruct((n_dev, n_slots, BLOCK), plan.dtype),
@@ -319,6 +320,9 @@
     for bank in banks:
         bank[pl.ds(n_rows, 8), :] = zero[:8]
     eye = lax.broadcasted_iota(jnp.int32, (BLOCK, dim), 0) == lax.broadcasted_iota(jnp.int32, (BLOCK, dim), 1)
+    lane = lax.broadcasted_iota(jnp.int32, (8, dim), 1)
+    lane_group = lane // 8
+    eye_line = lane % 8 == lax.broadcasted_iota(jnp.int32, (8, dim), 0)
     lr = lr_ref[0]
 
     for i, slot in enumerate(slots):
@@ -366,7 +370,10 @@
                         bank[rows, :] = zero
                 old = jnp.where(eye, accums_ref[slot:slot + 1, rows], 0.0)
                 new = jnp.sum(grad * grad * (1.0 / dim) + old, axis=1, keepdims=True)
-                done_v[slot:slot + 1, rows] = jnp.sum(jnp.where(eye, new, 0.0), axis=0, keepdims=True)
+                line = jnp.broadcast_to(new[:8], (8, dim))
+                for k in range(1, BLOCK // 8):
+                    line = jnp.where(lane_group == k, new[8 * k:8 * k + 8], line)
+                done_v[slot:slot + 1, rows] = jnp.sum(jnp.where(eye_line, line, 0.0), axis=0, keepdims=True)
                 root = lax.rsqrt(jnp.maximum(new, TINY))
                 scale = lr * root / (1.0 + EPSILON * root)
                 table_v[i, rows, :] = (table_v[i, rows, :].astype(jnp.float32) - grad * scale).astype(jnp.bfloat16)
@@ -430,10 +437,9 @@
         me = lax.axis_index('mp').reshape(1)
         n_tab = by_table.shape[0]
         plan_out = make_plan(lengths, n_group)
-        plan, starts, most = share_plan(plan_out)
-        most = most[0]
+        caps = CAPS(part)
+        plan, starts, level = share_plan(plan_out, caps)
         lr = learn_rate.reshape(1)
-        caps = CAPS(part)
 
         def exchange(level):
             def run(operands):
@@ -446,7 +452,9 @@
                     else:
                         pack = pack_slots(slots, caps[level], starts, plan, by_table)
                     if slots == hop_slots:
-                        hops = [lax.ppermute(pack[o], 'mp', routes(n_group, n_slots, n_tab, slots[0], o)) for o in range(1, n_group)]
+                        hops = []
+                        for o in range(1, n_group):
+                            hops.append(lax.ppermute(pack[o], 'mp', routes(n_group, n_slots, n_tab, slots[0], o)))
                         got[c] = [pack[0]] + hops
                     else:
                         got[c] = [lax.all_to_all(pack, 'mp', 0, 0, tiled=True)]
@@ -458,15 +466,14 @@
 
             return run
 
-        level = sum((most > cap).astype(jnp.int32) for cap in caps[:-1])
         operands = (me, by_table, plan, starts, row_ids, lengths, lr, tables, row_accum)
-        return lax.switch(level, [exchange(i) for i in range(len(caps))], operands)
+        return lax.switch(level[0], [exchange(i) for i in range(len(caps))], operands)
 
     return jax.shard_map(local_step, mesh=mesh, in_specs=(slot_spec, slot_spec, slot_spec, slot_spec, slot_spec, P()), out_specs=(slot_spec, slot_spec), check_vma=False)
 
 
 def CAPS(part):
-    return part * 35 // 64, part * 39 // 64, part
+    return part * 35 // 64, part * 37 // 64, part
 
 
 def CHUNKS(n_slots):

time: 221 us -> 220 us (level)
  no operation moved by 1% of the time
where the time goes in v9:
time: 220 us
  Pallas kernels  103 us (47%)
  waiting for transfers between devices  79.1 us (36%)
  starting transfers between devices  32.4 us (15%)
  local copies, waits for them, and re-layouts  3.62 us (2%)
    pallas_call x4, Pallas kernels, apply_slots(): pl.pallas_call(functools.partial(apply_kernel, slots, len(carried), len(g...  69.9 us
    all_to_all x3, waiting for transfers between devices, run(): got[c] = [lax.all_to_all(pack, 'mp', 0, 0, tiled=True)]  47.4 us
    ppermute x7, waiting for transfers between devices, run(): lax.ppermute(pack[o], 'mp', routes(n_group, n_slots, n_tab, slots[0], o))  31.8 us
    ppermute x7, starting transfers between devices, run(): lax.ppermute(pack[o], 'mp', routes(n_group, n_slots, n_tab, slots[0], o))  17.3 us
    all_to_all x3, starting transfers between devices, run(): got[c] = [lax.all_to_all(pack, 'mp', 0, 0, tiled=True)]  15.1 us
    pallas_call x3, Pallas kernels, pack_slots(): pl.pallas_call(functools.partial(pack_kernel, slots), out_shape=jax.Shape...  14.7 us
    pallas_call x1, Pallas kernels, share_plan(): pl.pallas_call(functools.partial(share_kernel, n_dev, caps), out_shape=(j...  10.4 us
    pallas_call x1, Pallas kernels, pack_hops(): pl.pallas_call(functools.partial(pack_hops_kernel, slot), out_shape=(jax....  5.4 us
  transfers between devices with their start and end apart: 10, of which 4 were waited for; matrix products, arithmetic and copies ran while one was open for 1% of the time, Pallas kernels for 31%

profile of v9, /device:TPU:81, one launch (start us, length us, event | category | flops | bytes accessed | tf_op | source)
XLA Modules:
  0.0 219.7 jit_solution(8271361362949976817)
XLA Ops:
  0.6 1.2 shard_map.95.plan_ref
  1.8 10.4 %shard_map.96 = (s32[8,4,2176]{2,1,0:T(4,128)S(1)}, s32[8,4,128]{2,1,0:T(4,128)S(1)}, s32[1]{0:T(128)}) custom-call(s32[8,4,2176]{2,1,0:T(4,128)S(1)} %shard_map.95.plan_ref), custom_call_target="tpu_custom_call" | custom-call | flops 20000000 | bytes 2000000 | tf_op jit(solution)/shard_map/pallas_call | solution.py:155
  12.8 206.7 %conditional.1 = ((bf16[4,16384,128]{2,1,0:T(8,128)(2,1)}, f32[4,16384]{1,0:T(4,128)})) conditional(s32[]{:T(128)} %bitcast.9, (s32[8,4,128]{2,1,0:T(4,128)S(1)}, s32[8,4,2176]{2,1,0:T(4,128)S(1)}, bf16[26,2048,128]{2,1,0:T(8,128)(2,1)}, s32[4,16384,1]{1,2,0:T(1,128)}, s32[]{:T(128)}, /*index=5*/s32[4,16384]{1,0:T(4,128)}, ...), branch_computations={%region_0.0_spmd, %region_1.0_spmd, %region_2.0_spmd} | conditional | flops 3543215360 | bytes 154576608 | solution.py:470
  12.8 5.0 %branch_0_fun.13 = bf16[8,1,1120,128]{3,2,1,0:T(8,128)(2,1)} custom-call(s32[8,4,128]{2,1,0:T(4,128)S(1)} %get-tuple-element.57.starts_ref, s32[8,4,2176]{2,1,0:T(4,128)S(1)} %get-tuple-element.58.plan_ref, bf16[26,2048,128]{2,1,0:T(8,128)(2,1)} %get-tuple-element.59.tables_ref), custom_call_target="tpu_custom_call" | custom-call | flops 41943040 | bytes 6291456 | tf_op jit(solution)/shard_map/cond/branch_0_fun/pallas_call | solution.py:208
  17.8 4.6 %all-to-all-start.2 = ((bf16[8,1,1120,128]{3,2,1,0:T(8,128)(2,1)}), bf16[8,1,1120,128]{3,2,1,0:T(8,128)(2,1)}, u32[]{:S(2)}, u32[]{:S(2)}) async-start(bf16[8,1,1120,128]{3,2,1,0:T(8,128)(2,1)} %branch_0_fun.13), calls=%async_computation.2 | async-start | bytes 4587520 | tf_op jit(solution)/shard_map/cond/branch_0_fun/all_to_all | solution.py:460
  22.5 5.0 %branch_0_fun.12 = bf16[8,1,1120,128]{3,2,1,0:T(8,128)(2,1)} custom-call(s32[8,4,128]{2,1,0:T(4,128)S(1)} %get-tuple-element.57.starts_ref, s32[8,4,2176]{2,1,0:T(4,128)S(1)} %get-tuple-element.58.plan_ref, bf16[26,2048,128]{2,1,0:T(8,128)(2,1)} %get-tuple-element.59.tables_ref), custom_call_target="tpu_custom_call" | custom-call | flops 41943040 | bytes 6291456 | tf_op jit(solution)/shard_map/cond/branch_0_fun/pallas_call | solution.py:208
  27.5 23.5 %all-to-all-done.2.refs_0_ = bf16[8,1,1120,128]{3,2,1,0:T(8,128)(2,1)} async-done(((bf16[8,1,1120,128]{3,2,1,0:T(8,128)(2,1)}), bf16[8,1,1120,128]{3,2,1,0:T(8,128)(2,1)}, u32[]{:S(2)}, u32[]{:S(2)}) %all-to-all-start.2) | async-done | bytes 2293792 | tf_op jit(solution)/shard_map/cond/branch_0_fun/all_to_all | solution.py:460
  51.0 5.2 %all-to-all-start.1 = ((bf16[8,1,1120,128]{3,2,1,0:T(8,128)(2,1)}), bf16[8,1,1120,128]{3,2,1,0:T(8,128)(2,1)}, u32[]{:S(2)}, u32[]{:S(2)}) async-start(bf16[8,1,1120,128]{3,2,1,0:T(8,128)(2,1)} %branch_0_fun.12), calls=%async_computation.1 | async-start | bytes 4587520 | tf_op jit(solution)/shard_map/cond/branch_0_fun/all_to_all | solution.py:460
  56.2 4.7 %branch_0_fun.9 = bf16[8,1,1120,128]{3,2,1,0:T(8,128)(2,1)} custom-call(s32[8,4,128]{2,1,0:T(4,128)S(1)} %get-tuple-element.57.starts_ref, s32[8,4,2176]{2,1,0:T(4,128)S(1)} %get-tuple-element.58.plan_ref, bf16[26,2048,128]{2,1,0:T(8,128)(2,1)} %get-tuple-element.59.tables_ref), custom_call_target="tpu_custom_call" | custom-call | flops 41943040 | bytes 6291456 | tf_op jit(solution)/shard_map/cond/branch_0_fun/pallas_call | solution.py:208
  60.9 23.8 %all-to-all-done.1.refs_0_ = bf16[8,1,1120,128]{3,2,1,0:T(8,128)(2,1)} async-done(((bf16[8,1,1120,128]{3,2,1,0:T(8,128)(2,1)}), bf16[8,1,1120,128]{3,2,1,0:T(8,128)(2,1)}, u32[]{:S(2)}, u32[]{:S(2)}) %all-to-all-start.1) | async-done | bytes 2293792 | tf_op jit(solution)/shard_map/cond/branch_0_fun/all_to_all | solution.py:460
  84.7 5.2 %all-to-all-start = ((bf16[8,1,1120,128]{3,2,1,0:T(8,128)(2,1)}), bf16[8,1,1120,128]{3,2,1,0:T(8,128)(2,1)}, u32[]{:S(2)}, u32[]{:S(2)}) async-start(bf16[8,1,1120,128]{3,2,1,0:T(8,128)(2,1)} %branch_0_fun.9), calls=%async_computation | async-start | bytes 4587520 | tf_op jit(solution)/shard_map/cond/branch_0_fun/all_to_all | solution.py:460
  89.9 0.0 copy-start.15
  89.9 0.0 copy-start.12
  89.9 5.4 %branch_0_fun.11 = (bf16[1120,128]{1,0:T(8,128)(2,1)}, bf16[1120,128]{1,0:T(8,128)(2,1)}, bf16[1120,128]{1,0:T(8,128)(2,1)}, bf16[1120,128]{1,0:T(8,128)(2,1)}, ...) custom-call(s32[1]{0:T(128)} %bitcast.1.me_ref, ...), custom_call_target="tpu_custom_call" | custom-call | flops 41943040 | bytes 6291456 | tf_op jit(solution)/shard_map/cond/branch_0_fun/pallas_call | solution.py:266
  95.3 3.6 %collective-permute-start = (bf16[1120,128]{1,0:T(8,128)(2,1)}, bf16[1120,128]{1,0:T(8,128)(2,1)S(1)}, u32[]{:S(2)}, u32[]{:S(2)}) collective-permute-start(bf16[1120,128]{1,0:T(8,128)(2,1)} %get-tuple-element.65), channel_id=1, source_target_pairs={{0,1},{1,2},{2,3},{3,4},{4,5},{7,0},{8,9},{9,10},{10,11},{11,12},{... | collective-permute-start | bytes 860168 | tf_op jit(solution)/shard_map/cond/branch_0_fun/ppermute | solution.py:457
  98.9 3.5 %collective-permute-start.1 = (bf16[1120,128]{1,0:T(8,128)(2,1)}, bf16[1120,128]{1,0:T(8,128)(2,1)S(1)}, u32[]{:S(2)}, u32[]{:S(2)}) collective-permute-start(bf16[1120,128]{1,0:T(8,128)(2,1)} %get-tuple-element.66), channel_id=1, source_target_pairs={{0,2},{1,3},{2,4},{3,5},{6,0},{7,1},{8,10},{9,11},{10,12},{11,13},... | collective-permute-start | bytes 860168 | tf_op jit(solution)/shard_map/cond/branch_0_fun/ppermute | solution.py:457
  102.4 2.0 collective-permute-start.2
  104.4 3.8 %collective-permute-start.3 = (bf16[1120,128]{1,0:T(8,128)(2,1)}, bf16[1120,128]{1,0:T(8,128)(2,1)}, u32[]{:S(2)}, u32[]{:S(2)}) collective-permute-start(bf16[1120,128]{1,0:T(8,128)(2,1)} %get-tuple-element.68), channel_id=1, source_target_pairs={{0,4},{1,5},{4,0},{5,1},{6,2},{7,3},{8,12},{9,13},{12,8},{13,9},{1... | collective-permute-start | bytes 860168 | tf_op jit(solution)/shard_map/cond/branch_0_fun/ppermute | solution.py:457
  108.2 1.3 collective-permute-start.4
  109.5 11.7 %collective-permute-done.refs_1_ = bf16[1120,128]{1,0:T(8,128)(2,1)S(1)} collective-permute-done((bf16[1120,128]{1,0:T(8,128)(2,1)}, bf16[1120,128]{1,0:T(8,128)(2,1)S(1)}, u32[]{:S(2)}, u32[]{:S(2)}) %collective-permute-start) | collective-permute-done | bytes 286752 | tf_op jit(solution)/shard_map/cond/branch_0_fun/ppermute | solution.py:457
  121.2 0.0 copy-start.22
  121.2 1.3 collective-permute-start.5
  122.5 20.1 %collective-permute-done.1.refs_2_ = bf16[1120,128]{1,0:T(8,128)(2,1)S(1)} collective-permute-done((bf16[1120,128]{1,0:T(8,128)(2,1)}, bf16[1120,128]{1,0:T(8,128)(2,1)S(1)}, u32[]{:S(2)}, u32[]{:S(2)}) %collective-permute-start.1) | collective-permute-done | bytes 286752 | tf_op jit(solution)/shard_map/cond/branch_0_fun/ppermute | solution.py:457
  142.6 0.0 copy-start.23
  142.6 1.9 collective-permute-start.6
  144.5 0.0 copy-done.22
  144.5 0.0 copy-done.23
  144.5 1.1 copy.50
  145.7 0.0 copy-done.15
  145.7 1.1 branch_0_fun.10
  146.8 0.0 copy-start
  146.8 0.6 copy-done
  147.4 0.0 copy-start.3
  147.4 0.6 copy-done.3
  148.0 0.0 copy-start.6
  148.0 0.6 copy-done.6
  148.6 0.6 copy-done.9
  149.3 0.0 copy-done.12
  149.3 17.5 %branch_0_fun.14 = (bf16[4,16384,128]{2,1,0:T(8,128)(2,1)}, f32[4,16384]{1,0:T(4,128)}) custom-call(f32[1]{0:T(128)} %bitcast.lr_ref, bf16[4,16384,128]{2,1,0:T(8,128)(2,1)} %get-tuple-element.172.tables_ref, f32[4,16384]{1,0:T(4,128)S(1)} %copy-done.12, bf16[8,1,1120,128]{3,2,1,0:T(8,128)(2,1)} %all-to-all-done.2.refs_0_, s32[1,16512]{1,0:T(1,128)} %copy-done), custom_call_target="tpu_custom_call" | custom-call | flops 838860800 | bytes 16777216 | tf_op jit(solution)/shard_map/cond/branch_0_fun/pallas_call | solution.py:398
  166.7 17.5 %branch_0_fun.15 = (bf16[4,16384,128]{2,1,0:T(8,128)(2,1)}, f32[4,16384]{1,0:T(4,128)}) custom-call(f32[1]{0:T(128)} %bitcast.lr_ref, bf16[4,16384,128]{2,1,0:T(8,128)(2,1)} %get-tuple-element.172.tables_ref, f32[4,16384]{1,0:T(4,128)S(1)} %copy-done.12, ...), custom_call_target="tpu_custom_call", output_to_operand_aliasing={{0}: (5, {}), {1}: (6, {})} | custom-call | flops 838860800 | bytes 16777216 | tf_op jit(solution)/shard_map/cond/branch_0_fun/pallas_call | solution.py:398
  184.2 0.0 collective-permute-done.2.refs_3_
  184.2 0.0 collective-permute-done.3.refs_4_
  184.2 0.0 collective-permute-done.4.refs_5_
  184.2 0.0 collective-permute-done.5.refs_6_
  184.3 0.0 collective-permute-done.6.refs_7_
  184.3 17.5 %branch_0_fun.16 = (bf16[4,16384,128]{2,1,0:T(8,128)(2,1)}, f32[4,16384]{1,0:T(4,128)}) custom-call(f32[1]{0:T(128)} %bitcast.lr_ref, bf16[4,16384,128]{2,1,0:T(8,128)(2,1)} %get-tuple-element.172.tables_ref, f32[4,16384]{1,0:T(4,128)S(1)} %copy-done.12, ...), custom_call_target="tpu_custom_call", output_to_operand_aliasing={{0}: (12, {}), {1}: (13, {})} | custom-call | flops 838860800 | bytes 16777216 | tf_op jit(solution)/shard_map/cond/branch_0_fun/pallas_call | solution.py:398
  201.8 0.0 all-to-all-done.refs_0_
  201.8 17.5 %branch_0_fun.17 = (bf16[4,16384,128]{2,1,0:T(8,128)(2,1)}, f32[4,16384]{1,0:T(4,128)}) custom-call(f32[1]{0:T(128)} %bitcast.lr_ref, bf16[4,16384,128]{2,1,0:T(8,128)(2,1)} %get-tuple-element.172.tables_ref, f32[4,16384]{1,0:T(4,128)S(1)} %copy-done.12, ...), custom_call_target="tpu_custom_call", output_to_operand_aliasing={{0}: (5, {}), {1}: (6, {})} | custom-call | flops 838860800 | bytes 16777216 | tf_op jit(solution)/shard_map/cond/branch_0_fun/pallas_call | solution.py:398
  (1 shorter events, 0.0 us)
Async XLA Ops:
  17.8 33.1 %all-to-all-start.2 = ((bf16[8,1,1120,128]{3,2,1,0:T(8,128)(2,1)}), bf16[8,1,1120,128]{3,2,1,0:T(8,128)(2,1)}, u32[]{:S(2)}, u32[]{:S(2)}) async-start(bf16[8,1,1120,128]{3,2,1,0:T(8,128)(2,1)} %branch_0_fun.13), calls=%async_computation.2 | async-start | bytes 4587520 | tf_op jit(solution)/shard_map/cond/branch_0_fun/all_to_all | solution.py:460
  51.0 33.7 %all-to-all-start.1 = ((bf16[8,1,1120,128]{3,2,1,0:T(8,128)(2,1)}), bf16[8,1,1120,128]{3,2,1,0:T(8,128)(2,1)}, u32[]{:S(2)}, u32[]{:S(2)}) async-start(bf16[8,1,1120,128]{3,2,1,0:T(8,128)(2,1)} %branch_0_fun.12), calls=%async_computation.1 | async-start | bytes 4587520 | tf_op jit(solution)/shard_map/cond/branch_0_fun/all_to_all | solution.py:460
  84.7 117.1 %all-to-all-start = ((bf16[8,1,1120,128]{3,2,1,0:T(8,128)(2,1)}), bf16[8,1,1120,128]{3,2,1,0:T(8,128)(2,1)}, u32[]{:S(2)}, u32[]{:S(2)}) async-start(bf16[8,1,1120,128]{3,2,1,0:T(8,128)(2,1)} %branch_0_fun.9), calls=%async_computation | async-start | bytes 4587520 | tf_op jit(solution)/shard_map/cond/branch_0_fun/all_to_all | solution.py:460
  89.9 55.7 %copy-start.15 = (s32[4,16384]{1,0:T(4,128)S(1)}, s32[4,16384]{1,0:T(4,128)}, u32[]{:S(2)}) copy-start(s32[4,16384]{1,0:T(4,128)} %get-tuple-element.62.lengths_ref) | copy-start | bytes 786436 | tf_op jit(solution)/shard_map/cond
  89.9 59.3 %copy-start.12 = (f32[4,16384]{1,0:T(4,128)S(1)}, f32[4,16384]{1,0:T(4,128)}, u32[]{:S(2)}) copy-start(f32[4,16384]{1,0:T(4,128)} %get-tuple-element.175.accums_ref) | copy-start | bytes 786436 | tf_op jit(solution)/shard_map/cond
  95.3 25.8 %collective-permute-start = (bf16[1120,128]{1,0:T(8,128)(2,1)}, bf16[1120,128]{1,0:T(8,128)(2,1)S(1)}, u32[]{:S(2)}, u32[]{:S(2)}) collective-permute-start(bf16[1120,128]{1,0:T(8,128)(2,1)} %get-tuple-element.65), channel_id=1, source_target_pairs={{0,1},{1,2},{2,3},{3,4},{4,5},{7,0},{8,9},{9,10},{10,11},{11,12},{... | collective-permute-start | bytes 860168 | tf_op jit(solution)/shard_map/cond/branch_0_fun/ppermute | solution.py:457
  98.9 43.6 %collective-permute-start.1 = (bf16[1120,128]{1,0:T(8,128)(2,1)}, bf16[1120,128]{1,0:T(8,128)(2,1)S(1)}, u32[]{:S(2)}, u32[]{:S(2)}) collective-permute-start(bf16[1120,128]{1,0:T(8,128)(2,1)} %get-tuple-element.66), channel_id=1, source_target_pairs={{0,2},{1,3},{2,4},{3,5},{6,0},{7,1},{8,10},{9,11},{10,12},{11,13},... | collective-permute-start | bytes 860168 | tf_op jit(solution)/shard_map/cond/branch_0_fun/ppermute | solution.py:457
  102.4 81.8 %collective-permute-start.2 = (bf16[1120,128]{1,0:T(8,128)(2,1)}, bf16[1120,128]{1,0:T(8,128)(2,1)}, u32[]{:S(2)}, u32[]{:S(2)}) collective-permute-start(bf16[1120,128]{1,0:T(8,128)(2,1)} %get-tuple-element.67), channel_id=1, source_target_pairs={{0,3},{1,4},{2,5},{5,0},{6,1},{7,2},{8,11},{9,12},{10,13},{13,8},{... | collective-permute-start | bytes 860168 | tf_op jit(solution)/shard_map/cond/branch_0_fun/ppermute | solution.py:457
  104.4 79.8 %collective-permute-start.3 = (bf16[1120,128]{1,0:T(8,128)(2,1)}, bf16[1120,128]{1,0:T(8,128)(2,1)}, u32[]{:S(2)}, u32[]{:S(2)}) collective-permute-start(bf16[1120,128]{1,0:T(8,128)(2,1)} %get-tuple-element.68), channel_id=1, source_target_pairs={{0,4},{1,5},{4,0},{5,1},{6,2},{7,3},{8,12},{9,13},{12,8},{13,9},{1... | collective-permute-start | bytes 860168 | tf_op jit(solution)/shard_map/cond/branch_0_fun/ppermute | solution.py:457
  108.2 76.1 %collective-permute-start.4 = (bf16[1120,128]{1,0:T(8,128)(2,1)}, bf16[1120,128]{1,0:T(8,128)(2,1)}, u32[]{:S(2)}, u32[]{:S(2)}) collective-permute-start(bf16[1120,128]{1,0:T(8,128)(2,1)} %get-tuple-element.69), channel_id=1, source_target_pairs={{0,5},{3,0},{4,1},{5,2},{6,3},{7,4},{8,13},{11,8},{12,9},{13,10},{... | collective-permute-start | bytes 860168 | tf_op jit(solution)/shard_map/cond/branch_0_fun/ppermute | solution.py:457
  121.2 23.4 %copy-start.22 = (bf16[1120,128]{1,0:T(8,128)(2,1)}, bf16[1120,128]{1,0:T(8,128)(2,1)S(1)}, u32[]{:S(2)}) copy-start(bf16[1120,128]{1,0:T(8,128)(2,1)S(1)} %collective-permute-done.refs_1_) | copy-start | bytes 860164 | tf_op jit(solution)/shard_map/cond
  121.2 63.1 %collective-permute-start.5 = (bf16[1120,128]{1,0:T(8,128)(2,1)}, bf16[1120,128]{1,0:T(8,128)(2,1)}, u32[]{:S(2)}, u32[]{:S(2)}) collective-permute-start(bf16[1120,128]{1,0:T(8,128)(2,1)} %get-tuple-element.70), channel_id=1, source_target_pairs={{2,0},{3,1},{4,2},{5,3},{6,4},{7,5},{10,8},{11,9},{12,10},{13,11},... | collective-permute-start | bytes 860168 | tf_op jit(solution)/shard_map/cond/branch_0_fun/ppermute | solution.py:457
  142.6 2.0 copy-start.23
  142.6 41.7 %collective-permute-start.6 = (bf16[1120,128]{1,0:T(8,128)(2,1)}, bf16[1120,128]{1,0:T(8,128)(2,1)}, u32[]{:S(2)}, u32[]{:S(2)}) collective-permute-start(bf16[1120,128]{1,0:T(8,128)(2,1)} %get-tuple-element.71), channel_id=1, source_target_pairs={{1,0},{2,1},{3,2},{4,3},{5,4},{6,5},{9,8},{10,9},{11,10},{12,11},{... | collective-permute-start | bytes 860168 | tf_op jit(solution)/shard_map/cond/branch_0_fun/ppermute | solution.py:457
  146.8 0.6 copy-start
  147.4 0.6 copy-start.3
  148.0 0.6 copy-start.6
  148.6 0.6 copy-start.9

commit v10 on v9

--- a/solution.py
+++ b/solution.py
@@ -14,6 +14,7 @@
 UNROLL = 16
 BLOCK = 128
 CHUNK = 1024
+CLEAR = 512
 MAX_LANE = 64
 VMEM_LIMIT = 66000000
 
@@ -35,40 +36,6 @@
 def prefix_matrix():
     below = lax.broadcasted_iota(jnp.int32, (BLOCK, BLOCK), 0) < lax.broadcasted_iota(jnp.int32, (BLOCK, BLOCK), 1)
     return jnp.where(below, 1.0, 0.0).astype(jnp.bfloat16)
-
-
-def plan_kernel(lengths_ref, plan_ref, len_v):
-    n_dev, n_slots, width = plan_ref.shape
-    part, rows = width - BLOCK, n_dev * n_slots
-    gather_parts(lengths_ref, len_v, n_dev)
-    prefix = prefix_matrix()
-    lane = lax.broadcasted_iota(jnp.int32, (rows, BLOCK), 1)
-    count = jnp.zeros((rows, 1), jnp.int32)
-    starts = jnp.zeros((rows, BLOCK), jnp.int32)
-    for b in range(part // BLOCK):
-        valid, local, more = block_prefix(len_v, b, prefix)
-        place = jnp.where(valid, local, -1)
-        for d in range(n_dev):
-            plan_ref[d, :, b * BLOCK:(b + 1) * BLOCK] = place[d * n_slots:(d + 1) * n_slots, :]
-        starts = jnp.where(lane == b, count, starts)
-        count = count + more
-    starts = jnp.where(lane == MAX_LANE, jnp.max(count, axis=0, keepdims=True), starts)
-    for d in range(n_dev):
-        plan_ref[d, :, part:] = starts[d * n_slots:(d + 1) * n_slots, :]
-
-
-def make_plan(lengths, n_dev):
-    n_slots, batch = lengths.shape
-    part = batch // n_dev
-    return pl.pallas_call(
-        plan_kernel,
-        out_shape=jax.ShapeDtypeStruct((n_dev, n_slots, part + BLOCK), jnp.int32),
-        in_specs=[pl.BlockSpec(memory_space=pltpu.VMEM)],
-        out_specs=pl.BlockSpec(memory_space=pltpu.VMEM),
-        scratch_shapes=[pltpu.VMEM((n_dev * n_slots, part), jnp.int32)],
-        compiler_params=pltpu.CompilerParams(vmem_limit_bytes=16000000),
-        cost_estimate=pl.CostEstimate(flops=10000000, bytes_accessed=1000000, transcendentals=0),
-    )(lengths)
 
 
 def ids_kernel(n_dev, n_rows, hop_slots, me_ref, ids_ref, lengths_ref, *refs):
@@ -119,11 +86,32 @@
     )(me, ids, lengths)
 
 
-def share_kernel(n_dev, caps, plan_ref, plans_ref, starts_ref, level_ref, send_sem, recv_sem, own_sem):
+def write_plan(lengths_ref, plan_ref, len_v):
+    n_dev, n_slots, width = plan_ref.shape
+    part, rows = width - BLOCK, n_dev * n_slots
+    gather_parts(lengths_ref, len_v, n_dev)
+    prefix = prefix_matrix()
+    lane = lax.broadcasted_iota(jnp.int32, (rows, BLOCK), 1)
+    count = jnp.zeros((rows, 1), jnp.int32)
+    starts = jnp.zeros((rows, BLOCK), jnp.int32)
+    for b in range(part // BLOCK):
+        valid, local, more = block_prefix(len_v, b, prefix)
+        place = jnp.where(valid, local, -1)
+        for d in range(n_dev):
+            plan_ref[d, :, b * BLOCK:(b + 1) * BLOCK] = place[d * n_slots:(d + 1) * n_slots, :]
+        starts = jnp.where(lane == b, count, starts)
+        count = count + more
+    starts = jnp.where(lane == MAX_LANE, jnp.max(count, axis=0, keepdims=True), starts)
+    for d in range(n_dev):
+        plan_ref[d, :, part:] = starts[d * n_slots:(d + 1) * n_slots, :]
+
+
+def plan_kernel(n_dev, caps, lengths_ref, plans_ref, starts_ref, level_ref, plan_ref, len_v, send_sem, recv_sem, own_sem):
     pod, me = lax.axis_index('pod'), lax.axis_index('mp')
     barrier = pltpu.get_barrier_semaphore()
     for o in range(1, n_dev):
         pl.semaphore_signal(barrier, inc=1, device_id=(pod, (me + o) % n_dev), device_id_type=pl.DeviceIdType.MESH)
+    write_plan(lengths_ref, plan_ref, len_v)
     pl.semaphore_wait(barrier, n_dev - 1)
     copies = [
         pltpu.make_async_remote_copy(
@@ -150,21 +138,29 @@
     level_ref[0] = sum((most > cap).astype(jnp.int32) for cap in caps[:-1])
 
 
-def share_plan(plan, caps):
-    n_dev, n_slots, _ = plan.shape
+def make_plan(lengths, n_dev, caps):
+    n_slots, batch = lengths.shape
+    part = batch // n_dev
+    plan_shape = (n_dev, n_slots, part + BLOCK)
     return pl.pallas_call(
-        functools.partial(share_kernel, n_dev, caps),
+        functools.partial(plan_kernel, n_dev, caps),
         out_shape=(
-            jax.ShapeDtypeStruct(plan.shape, plan.dtype),
-            jax.ShapeDtypeStruct((n_dev, n_slots, BLOCK), plan.dtype),
-            jax.ShapeDtypeStruct((1,), plan.dtype),
+            jax.ShapeDtypeStruct(plan_shape, jnp.int32),
+            jax.ShapeDtypeStruct((n_dev, n_slots, BLOCK), jnp.int32),
+            jax.ShapeDtypeStruct((1,), jnp.int32),
         ),
         in_specs=[pl.BlockSpec(memory_space=pltpu.VMEM)],
         out_specs=(pl.BlockSpec(memory_space=pltpu.VMEM), pl.BlockSpec(memory_space=pltpu.VMEM), pl.BlockSpec(memory_space=pltpu.SMEM)),
-        scratch_shapes=[pltpu.SemaphoreType.DMA((n_dev,)), pltpu.SemaphoreType.DMA((n_dev,)), pltpu.SemaphoreType.DMA],
+        scratch_shapes=[
+            pltpu.VMEM(plan_shape, jnp.int32),
+            pltpu.VMEM((n_dev * n_slots, part), jnp.int32),
+            pltpu.SemaphoreType.DMA((n_dev,)),
+            pltpu.SemaphoreType.DMA((n_dev,)),
+            pltpu.SemaphoreType.DMA,
+        ],
         compiler_params=pltpu.CompilerParams(collective_id=0, has_side_effects=True, vmem_limit_bytes=16000000),
         cost_estimate=pl.CostEstimate(flops=20000000, bytes_accessed=2000000, transcendentals=0),
-    )(plan)
+    )(lengths)
 
 
 def pack_kernel(slots, starts_ref, plan_ref, tables_ref, out_ref, grad_v, stage, pack_v, in_sem, out_sem):
@@ -313,10 +309,11 @@
 
     def clear(i, carry):
         for bank in banks:
-            bank[pl.ds(pl.multiple_of(i * BLOCK, BLOCK), BLOCK), :] = zero
+            for s in range(CLEAR // BLOCK):
+                bank[pl.ds(pl.multiple_of(i * CLEAR, CLEAR) + s * BLOCK, BLOCK), :] = zero
         return carry
 
-    lax.fori_loop(0, n_rows // BLOCK, clear, 0)
+    lax.fori_loop(0, n_rows // CLEAR, clear, 0)
     for bank in banks:
         bank[pl.ds(n_rows, 8), :] = zero[:8]
     eye = lax.broadcasted_iota(jnp.int32, (BLOCK, dim), 0) == lax.broadcasted_iota(jnp.int32, (BLOCK, dim), 1)
@@ -436,9 +433,8 @@
         part = by_table.shape[1]
         me = lax.axis_index('mp').reshape(1)
         n_tab = by_table.shape[0]
-        plan_out = make_plan(lengths, n_group)
         caps = CAPS(part)
-        plan, starts, level = share_plan(plan_out, caps)
+        plan, starts, level = make_plan(lengths, n_group, caps)
         lr = learn_rate.reshape(1)
 
         def exchange(level):

time: 220 us -> 219 us (level)
    pallas_call x2 -> x1, Pallas kernels: 11.6 us -> 11.2 us  [make_plan(): pl.pallas_call(functools.partial(plan_kernel, n_dev, caps), out_shape=(ja...]
where the time goes in v10:
time: 219 us
  Pallas kernels  102 us (47%)
  waiting for transfers between devices  79.1 us (36%)
  starting transfers between devices  32.4 us (15%)
  local copies, waits for them, and re-layouts  3.62 us (2%)
    pallas_call x4, Pallas kernels, apply_slots(): pl.pallas_call(functools.partial(apply_kernel, slots, len(carried), len(g...  69.3 us
    all_to_all x3, waiting for transfers between devices, run(): got[c] = [lax.all_to_all(pack, 'mp', 0, 0, tiled=True)]  47.4 us
    ppermute x7, waiting for transfers between devices, run(): lax.ppermute(pack[o], 'mp', routes(n_group, n_slots, n_tab, slots[0], o))  31.8 us
    ppermute x7, starting transfers between devices, run(): lax.ppermute(pack[o], 'mp', routes(n_group, n_slots, n_tab, slots[0], o))  17.3 us
    all_to_all x3, starting transfers between devices, run(): got[c] = [lax.all_to_all(pack, 'mp', 0, 0, tiled=True)]  15.1 us
    pallas_call x3, Pallas kernels, pack_slots(): pl.pallas_call(functools.partial(pack_kernel, slots), out_shape=jax.Shape...  14.7 us
    pallas_call x1, Pallas kernels, make_plan(): pl.pallas_call(functools.partial(plan_kernel, n_dev, caps), out_shape=(ja...  11.2 us
    pallas_call x1, Pallas kernels, pack_hops(): pl.pallas_call(functools.partial(pack_hops_kernel, slot), out_shape=(jax....  5.4 us
  transfers between devices with their start and end apart: 10, of which 4 were waited for; matrix products, arithmetic and copies ran while one was open for 1% of the time, Pallas kernels for 31%

profile of v10, /device:TPU:81, one launch (start us, length us, event | category | flops | bytes accessed | tf_op | source)
XLA Modules:
  0.0 218.6 jit_solution(3710437615489940221)
XLA Ops:
  0.6 11.2 %shard_map.95 = (s32[8,4,2176]{2,1,0:T(4,128)S(1)}, s32[8,4,128]{2,1,0:T(4,128)S(1)}, s32[1]{0:T(128)}) custom-call(s32[4,16384]{1,0:T(4,128)} %lengths_ref.1), custom_call_target="tpu_custom_call" | custom-call | flops 20000000 | bytes 2000000 | tf_op jit(solution)/shard_map/pallas_call | solution.py:145
  12.4 206.1 %conditional.1 = ((bf16[4,16384,128]{2,1,0:T(8,128)(2,1)}, f32[4,16384]{1,0:T(4,128)})) conditional(s32[]{:T(128)} %bitcast.9, (s32[8,4,128]{2,1,0:T(4,128)S(1)}, s32[8,4,2176]{2,1,0:T(4,128)S(1)}, bf16[26,2048,128]{2,1,0:T(8,128)(2,1)}, s32[4,16384,1]{1,2,0:T(1,128)}, s32[]{:T(128)}, /*index=5*/s32[4,16384]{1,0:T(4,128)}, ...), branch_computations={%region_0.0_spmd, %region_1.0_spmd, %region_2.0_spmd} | conditional | flops 3543215360 | bytes 154576608 | solution.py:466
  12.4 5.0 %branch_0_fun.13 = bf16[8,1,1120,128]{3,2,1,0:T(8,128)(2,1)} custom-call(s32[8,4,128]{2,1,0:T(4,128)S(1)} %get-tuple-element.57.starts_ref, s32[8,4,2176]{2,1,0:T(4,128)S(1)} %get-tuple-element.58.plan_ref, bf16[26,2048,128]{2,1,0:T(8,128)(2,1)} %get-tuple-element.59.tables_ref), custom_call_target="tpu_custom_call" | custom-call | flops 41943040 | bytes 6291456 | tf_op jit(solution)/shard_map/cond/branch_0_fun/pallas_call | solution.py:204
  17.4 4.6 %all-to-all-start.2 = ((bf16[8,1,1120,128]{3,2,1,0:T(8,128)(2,1)}), bf16[8,1,1120,128]{3,2,1,0:T(8,128)(2,1)}, u32[]{:S(2)}, u32[]{:S(2)}) async-start(bf16[8,1,1120,128]{3,2,1,0:T(8,128)(2,1)} %branch_0_fun.13), calls=%async_computation.2 | async-start | bytes 4587520 | tf_op jit(solution)/shard_map/cond/branch_0_fun/all_to_all | solution.py:456
  22.0 5.0 %branch_0_fun.12 = bf16[8,1,1120,128]{3,2,1,0:T(8,128)(2,1)} custom-call(s32[8,4,128]{2,1,0:T(4,128)S(1)} %get-tuple-element.57.starts_ref, s32[8,4,2176]{2,1,0:T(4,128)S(1)} %get-tuple-element.58.plan_ref, bf16[26,2048,128]{2,1,0:T(8,128)(2,1)} %get-tuple-element.59.tables_ref), custom_call_target="tpu_custom_call" | custom-call | flops 41943040 | bytes 6291456 | tf_op jit(solution)/shard_map/cond/branch_0_fun/pallas_call | solution.py:204
  27.0 23.5 %all-to-all-done.2.refs_0_ = bf16[8,1,1120,128]{3,2,1,0:T(8,128)(2,1)} async-done(((bf16[8,1,1120,128]{3,2,1,0:T(8,128)(2,1)}), bf16[8,1,1120,128]{3,2,1,0:T(8,128)(2,1)}, u32[]{:S(2)}, u32[]{:S(2)}) %all-to-all-start.2) | async-done | bytes 2293792 | tf_op jit(solution)/shard_map/cond/branch_0_fun/all_to_all | solution.py:456
  50.5 5.2 %all-to-all-start.1 = ((bf16[8,1,1120,128]{3,2,1,0:T(8,128)(2,1)}), bf16[8,1,1120,128]{3,2,1,0:T(8,128)(2,1)}, u32[]{:S(2)}, u32[]{:S(2)}) async-start(bf16[8,1,1120,128]{3,2,1,0:T(8,128)(2,1)} %branch_0_fun.12), calls=%async_computation.1 | async-start | bytes 4587520 | tf_op jit(solution)/shard_map/cond/branch_0_fun/all_to_all | solution.py:456
  55.8 4.7 %branch_0_fun.9 = bf16[8,1,1120,128]{3,2,1,0:T(8,128)(2,1)} custom-call(s32[8,4,128]{2,1,0:T(4,128)S(1)} %get-tuple-element.57.starts_ref, s32[8,4,2176]{2,1,0:T(4,128)S(1)} %get-tuple-element.58.plan_ref, bf16[26,2048,128]{2,1,0:T(8,128)(2,1)} %get-tuple-element.59.tables_ref), custom_call_target="tpu_custom_call" | custom-call | flops 41943040 | bytes 6291456 | tf_op jit(solution)/shard_map/cond/branch_0_fun/pallas_call | solution.py:204
  60.4 23.8 %all-to-all-done.1.refs_0_ = bf16[8,1,1120,128]{3,2,1,0:T(8,128)(2,1)} async-done(((bf16[8,1,1120,128]{3,2,1,0:T(8,128)(2,1)}), bf16[8,1,1120,128]{3,2,1,0:T(8,128)(2,1)}, u32[]{:S(2)}, u32[]{:S(2)}) %all-to-all-start.1) | async-done | bytes 2293792 | tf_op jit(solution)/shard_map/cond/branch_0_fun/all_to_all | solution.py:456
  84.3 5.2 %all-to-all-start = ((bf16[8,1,1120,128]{3,2,1,0:T(8,128)(2,1)}), bf16[8,1,1120,128]{3,2,1,0:T(8,128)(2,1)}, u32[]{:S(2)}, u32[]{:S(2)}) async-start(bf16[8,1,1120,128]{3,2,1,0:T(8,128)(2,1)} %branch_0_fun.9), calls=%async_computation | async-start | bytes 4587520 | tf_op jit(solution)/shard_map/cond/branch_0_fun/all_to_all | solution.py:456
  89.5 0.0 copy-start.15
  89.5 0.0 copy-start.12
  89.5 5.4 %branch_0_fun.11 = (bf16[1120,128]{1,0:T(8,128)(2,1)}, bf16[1120,128]{1,0:T(8,128)(2,1)}, bf16[1120,128]{1,0:T(8,128)(2,1)}, bf16[1120,128]{1,0:T(8,128)(2,1)}, ...) custom-call(s32[1]{0:T(128)} %bitcast.1.me_ref, ...), custom_call_target="tpu_custom_call" | custom-call | flops 41943040 | bytes 6291456 | tf_op jit(solution)/shard_map/cond/branch_0_fun/pallas_call | solution.py:262
  94.9 3.6 %collective-permute-start = (bf16[1120,128]{1,0:T(8,128)(2,1)}, bf16[1120,128]{1,0:T(8,128)(2,1)S(1)}, u32[]{:S(2)}, u32[]{:S(2)}) collective-permute-start(bf16[1120,128]{1,0:T(8,128)(2,1)} %get-tuple-element.65), channel_id=1, source_target_pairs={{0,1},{1,2},{2,3},{3,4},{4,5},{7,0},{8,9},{9,10},{10,11},{11,12},{... | collective-permute-start | bytes 860168 | tf_op jit(solution)/shard_map/cond/branch_0_fun/ppermute | solution.py:453
  98.5 3.5 %collective-permute-start.1 = (bf16[1120,128]{1,0:T(8,128)(2,1)}, bf16[1120,128]{1,0:T(8,128)(2,1)S(1)}, u32[]{:S(2)}, u32[]{:S(2)}) collective-permute-start(bf16[1120,128]{1,0:T(8,128)(2,1)} %get-tuple-element.66), channel_id=1, source_target_pairs={{0,2},{1,3},{2,4},{3,5},{6,0},{7,1},{8,10},{9,11},{10,12},{11,13},... | collective-permute-start | bytes 860168 | tf_op jit(solution)/shard_map/cond/branch_0_fun/ppermute | solution.py:453
  102.0 2.0 collective-permute-start.2
  104.0 3.8 %collective-permute-start.3 = (bf16[1120,128]{1,0:T(8,128)(2,1)}, bf16[1120,128]{1,0:T(8,128)(2,1)}, u32[]{:S(2)}, u32[]{:S(2)}) collective-permute-start(bf16[1120,128]{1,0:T(8,128)(2,1)} %get-tuple-element.68), channel_id=1, source_target_pairs={{0,4},{1,5},{4,0},{5,1},{6,2},{7,3},{8,12},{9,13},{12,8},{13,9},{1... | collective-permute-start | bytes 860168 | tf_op jit(solution)/shard_map/cond/branch_0_fun/ppermute | solution.py:453
  107.7 1.3 collective-permute-start.4
  109.1 11.7 %collective-permute-done.refs_1_ = bf16[1120,128]{1,0:T(8,128)(2,1)S(1)} collective-permute-done((bf16[1120,128]{1,0:T(8,128)(2,1)}, bf16[1120,128]{1,0:T(8,128)(2,1)S(1)}, u32[]{:S(2)}, u32[]{:S(2)}) %collective-permute-start) | collective-permute-done | bytes 286752 | tf_op jit(solution)/shard_map/cond/branch_0_fun/ppermute | solution.py:453
  120.7 0.0 copy-start.22
  120.7 1.3 collective-permute-start.5
  122.0 20.1 %collective-permute-done.1.refs_2_ = bf16[1120,128]{1,0:T(8,128)(2,1)S(1)} collective-permute-done((bf16[1120,128]{1,0:T(8,128)(2,1)}, bf16[1120,128]{1,0:T(8,128)(2,1)S(1)}, u32[]{:S(2)}, u32[]{:S(2)}) %collective-permute-start.1) | collective-permute-done | bytes 286752 | tf_op jit(solution)/shard_map/cond/branch_0_fun/ppermute | solution.py:453
  142.1 0.0 copy-start.23
  142.1 1.9 collective-permute-start.6
  144.1 0.0 copy-done.22
  144.1 0.0 copy-done.23
  144.1 1.1 copy.50
  145.2 0.0 copy-done.15
  145.2 1.1 branch_0_fun.10
  146.3 0.0 copy-start
  146.3 0.6 copy-done
  147.0 0.0 copy-start.3
  147.0 0.6 copy-done.3
  147.6 0.0 copy-start.6
  147.6 0.6 copy-done.6
  148.2 0.0 copy-start.9
  148.2 0.6 copy-done.9
  148.8 0.0 copy-done.12
  148.8 17.3 %branch_0_fun.14 = (bf16[4,16384,128]{2,1,0:T(8,128)(2,1)}, f32[4,16384]{1,0:T(4,128)}) custom-call(f32[1]{0:T(128)} %bitcast.lr_ref, bf16[4,16384,128]{2,1,0:T(8,128)(2,1)} %get-tuple-element.172.tables_ref, f32[4,16384]{1,0:T(4,128)S(1)} %copy-done.12, bf16[8,1,1120,128]{3,2,1,0:T(8,128)(2,1)} %all-to-all-done.2.refs_0_, s32[1,16512]{1,0:T(1,128)} %copy-done), custom_call_target="tpu_custom_call" | custom-call | flops 838860800 | bytes 16777216 | tf_op jit(solution)/shard_map/cond/branch_0_fun/pallas_call | solution.py:395
  166.2 17.3 %branch_0_fun.15 = (bf16[4,16384,128]{2,1,0:T(8,128)(2,1)}, f32[4,16384]{1,0:T(4,128)}) custom-call(f32[1]{0:T(128)} %bitcast.lr_ref, bf16[4,16384,128]{2,1,0:T(8,128)(2,1)} %get-tuple-element.172.tables_ref, f32[4,16384]{1,0:T(4,128)S(1)} %copy-done.12, ...), custom_call_target="tpu_custom_call", output_to_operand_aliasing={{0}: (5, {}), {1}: (6, {})} | custom-call | flops 838860800 | bytes 16777216 | tf_op jit(solution)/shard_map/cond/branch_0_fun/pallas_call | solution.py:395
  183.5 0.0 collective-permute-done.2.refs_3_
  183.5 0.0 collective-permute-done.3.refs_4_
  183.5 0.0 collective-permute-done.4.refs_5_
  183.5 0.0 collective-permute-done.5.refs_6_
  183.5 0.0 collective-permute-done.6.refs_7_
  183.5 17.3 %branch_0_fun.16 = (bf16[4,16384,128]{2,1,0:T(8,128)(2,1)}, f32[4,16384]{1,0:T(4,128)}) custom-call(f32[1]{0:T(128)} %bitcast.lr_ref, bf16[4,16384,128]{2,1,0:T(8,128)(2,1)} %get-tuple-element.172.tables_ref, f32[4,16384]{1,0:T(4,128)S(1)} %copy-done.12, ...), custom_call_target="tpu_custom_call", output_to_operand_aliasing={{0}: (12, {}), {1}: (13, {})} | custom-call | flops 838860800 | bytes 16777216 | tf_op jit(solution)/shard_map/cond/branch_0_fun/pallas_call | solution.py:395
  200.9 0.0 all-to-all-done.refs_0_
  200.9 17.3 %branch_0_fun.17 = (bf16[4,16384,128]{2,1,0:T(8,128)(2,1)}, f32[4,16384]{1,0:T(4,128)}) custom-call(f32[1]{0:T(128)} %bitcast.lr_ref, bf16[4,16384,128]{2,1,0:T(8,128)(2,1)} %get-tuple-element.172.tables_ref, f32[4,16384]{1,0:T(4,128)S(1)} %copy-done.12, ...), custom_call_target="tpu_custom_call", output_to_operand_aliasing={{0}: (5, {}), {1}: (6, {})} | custom-call | flops 838860800 | bytes 16777216 | tf_op jit(solution)/shard_map/cond/branch_0_fun/pallas_call | solution.py:395
Async XLA Ops:
  17.4 33.1 %all-to-all-start.2 = ((bf16[8,1,1120,128]{3,2,1,0:T(8,128)(2,1)}), bf16[8,1,1120,128]{3,2,1,0:T(8,128)(2,1)}, u32[]{:S(2)}, u32[]{:S(2)}) async-start(bf16[8,1,1120,128]{3,2,1,0:T(8,128)(2,1)} %branch_0_fun.13), calls=%async_computation.2 | async-start | bytes 4587520 | tf_op jit(solution)/shard_map/cond/branch_0_fun/all_to_all | solution.py:456
  50.5 33.7 %all-to-all-start.1 = ((bf16[8,1,1120,128]{3,2,1,0:T(8,128)(2,1)}), bf16[8,1,1120,128]{3,2,1,0:T(8,128)(2,1)}, u32[]{:S(2)}, u32[]{:S(2)}) async-start(bf16[8,1,1120,128]{3,2,1,0:T(8,128)(2,1)} %branch_0_fun.12), calls=%async_computation.1 | async-start | bytes 4587520 | tf_op jit(solution)/shard_map/cond/branch_0_fun/all_to_all | solution.py:456
  84.3 116.6 %all-to-all-start = ((bf16[8,1,1120,128]{3,2,1,0:T(8,128)(2,1)}), bf16[8,1,1120,128]{3,2,1,0:T(8,128)(2,1)}, u32[]{:S(2)}, u32[]{:S(2)}) async-start(bf16[8,1,1120,128]{3,2,1,0:T(8,128)(2,1)} %branch_0_fun.9), calls=%async_computation | async-start | bytes 4587520 | tf_op jit(solution)/shard_map/cond/branch_0_fun/all_to_all | solution.py:456
  89.5 55.7 %copy-start.15 = (s32[4,16384]{1,0:T(4,128)S(1)}, s32[4,16384]{1,0:T(4,128)}, u32[]{:S(2)}) copy-start(s32[4,16384]{1,0:T(4,128)} %get-tuple-element.62.lengths_ref) | copy-start | bytes 786436 | tf_op jit(solution)/shard_map/cond
  89.5 59.3 %copy-start.12 = (f32[4,16384]{1,0:T(4,128)S(1)}, f32[4,16384]{1,0:T(4,128)}, u32[]{:S(2)}) copy-start(f32[4,16384]{1,0:T(4,128)} %get-tuple-element.175.accums_ref) | copy-start | bytes 786436 | tf_op jit(solution)/shard_map/cond
  94.9 25.8 %collective-permute-start = (bf16[1120,128]{1,0:T(8,128)(2,1)}, bf16[1120,128]{1,0:T(8,128)(2,1)S(1)}, u32[]{:S(2)}, u32[]{:S(2)}) collective-permute-start(bf16[1120,128]{1,0:T(8,128)(2,1)} %get-tuple-element.65), channel_id=1, source_target_pairs={{0,1},{1,2},{2,3},{3,4},{4,5},{7,0},{8,9},{9,10},{10,11},{11,12},{... | collective-permute-start | bytes 860168 | tf_op jit(solution)/shard_map/cond/branch_0_fun/ppermute | solution.py:453
  98.5 43.6 %collective-permute-start.1 = (bf16[1120,128]{1,0:T(8,128)(2,1)}, bf16[1120,128]{1,0:T(8,128)(2,1)S(1)}, u32[]{:S(2)}, u32[]{:S(2)}) collective-permute-start(bf16[1120,128]{1,0:T(8,128)(2,1)} %get-tuple-element.66), channel_id=1, source_target_pairs={{0,2},{1,3},{2,4},{3,5},{6,0},{7,1},{8,10},{9,11},{10,12},{11,13},... | collective-permute-start | bytes 860168 | tf_op jit(solution)/shard_map/cond/branch_0_fun/ppermute | solution.py:453
  102.0 81.5 %collective-permute-start.2 = (bf16[1120,128]{1,0:T(8,128)(2,1)}, bf16[1120,128]{1,0:T(8,128)(2,1)}, u32[]{:S(2)}, u32[]{:S(2)}) collective-permute-start(bf16[1120,128]{1,0:T(8,128)(2,1)} %get-tuple-element.67), channel_id=1, source_target_pairs={{0,3},{1,4},{2,5},{5,0},{6,1},{7,2},{8,11},{9,12},{10,13},{13,8},{... | collective-permute-start | bytes 860168 | tf_op jit(solution)/shard_map/cond/branch_0_fun/ppermute | solution.py:453
  104.0 79.6 %collective-permute-start.3 = (bf16[1120,128]{1,0:T(8,128)(2,1)}, bf16[1120,128]{1,0:T(8,128)(2,1)}, u32[]{:S(2)}, u32[]{:S(2)}) collective-permute-start(bf16[1120,128]{1,0:T(8,128)(2,1)} %get-tuple-element.68), channel_id=1, source_target_pairs={{0,4},{1,5},{4,0},{5,1},{6,2},{7,3},{8,12},{9,13},{12,8},{13,9},{1... | collective-permute-start | bytes 860168 | tf_op jit(solution)/shard_map/cond/branch_0_fun/ppermute | solution.py:453
  107.7 75.8 %collective-permute-start.4 = (bf16[1120,128]{1,0:T(8,128)(2,1)}, bf16[1120,128]{1,0:T(8,128)(2,1)}, u32[]{:S(2)}, u32[]{:S(2)}) collective-permute-start(bf16[1120,128]{1,0:T(8,128)(2,1)} %get-tuple-element.69), channel_id=1, source_target_pairs={{0,5},{3,0},{4,1},{5,2},{6,3},{7,4},{8,13},{11,8},{12,9},{13,10},{... | collective-permute-start | bytes 860168 | tf_op jit(solution)/shard_map/cond/branch_0_fun/ppermute | solution.py:453
  120.7 23.4 %copy-start.22 = (bf16[1120,128]{1,0:T(8,128)(2,1)}, bf16[1120,128]{1,0:T(8,128)(2,1)S(1)}, u32[]{:S(2)}) copy-start(bf16[1120,128]{1,0:T(8,128)(2,1)S(1)} %collective-permute-done.refs_1_) | copy-start | bytes 860164 | tf_op jit(solution)/shard_map/cond
  120.7 62.8 %collective-permute-start.5 = (bf16[1120,128]{1,0:T(8,128)(2,1)}, bf16[1120,128]{1,0:T(8,128)(2,1)}, u32[]{:S(2)}, u32[]{:S(2)}) collective-permute-start(bf16[1120,128]{1,0:T(8,128)(2,1)} %get-tuple-element.70), channel_id=1, source_target_pairs={{2,0},{3,1},{4,2},{5,3},{6,4},{7,5},{10,8},{11,9},{12,10},{13,11},... | collective-permute-start | bytes 860168 | tf_op jit(solution)/shard_map/cond/branch_0_fun/ppermute | solution.py:453
  142.1 2.0 copy-start.23
  142.1 41.4 %collective-permute-start.6 = (bf16[1120,128]{1,0:T(8,128)(2,1)}, bf16[1120,128]{1,0:T(8,128)(2,1)}, u32[]{:S(2)}, u32[]{:S(2)}) collective-permute-start(bf16[1120,128]{1,0:T(8,128)(2,1)} %get-tuple-element.71), channel_id=1, source_target_pairs={{1,0},{2,1},{3,2},{4,3},{5,4},{6,5},{9,8},{10,9},{11,10},{12,11},{... | collective-permute-start | bytes 860168 | tf_op jit(solution)/shard_map/cond/branch_0_fun/ppermute | solution.py:453
  146.3 0.6 copy-start
  147.0 0.6 copy-start.3
  147.6 0.6 copy-start.6
  148.2 0.6 copy-start.9

commit v11 on v10

--- a/solution.py
+++ b/solution.py
@@ -16,7 +16,7 @@
 CHUNK = 1024
 CLEAR = 512
 MAX_LANE = 64
-VMEM_LIMIT = 66000000
+VMEM_LIMIT = 67000000
 
 
 def gather_parts(src_ref, dst, n_dev):
@@ -39,8 +39,8 @@
 
 
 def ids_kernel(n_dev, n_rows, hop_slots, me_ref, ids_ref, lengths_ref, *refs):
-    *packed_refs, ids_v, len_v = refs
     n_slots, batch = ids_ref.shape
+    out_refs, packed_refs, (ids_v, len_v, sem) = refs[:n_slots], refs[n_slots:2 * n_slots], refs[2 * n_slots:]
     part, rows = batch // n_dev, n_dev * n_slots
     gather_parts(ids_ref, ids_v, n_dev)
     gather_parts(lengths_ref, len_v, n_dev)
@@ -63,12 +63,16 @@
         step *= 2
     spot = lax.broadcasted_iota(jnp.int32, (rows, part), 1)
     ids_v[...] = jnp.where(spot < count, move & 0xFFFF, n_rows)
-    most = jnp.max(count, axis=0, keepdims=True)
+    slot_of = lax.broadcasted_iota(jnp.int32, (rows, 1), 0) % n_slots
     for s in range(n_slots):
+        most = jnp.max(jnp.where(slot_of == s, count, 0), axis=0, keepdims=True)
         for d in range(n_dev):
             sender = (me_ref[0] + (n_dev - d)) % n_dev if s in hop_slots else d
             packed_refs[s][:, d * part:(d + 1) * part] = ids_v[pl.ds(sender * n_slots + s, 1), :]
         packed_refs[s][:, n_dev * part:] = jnp.broadcast_to(most, (1, BLOCK))
+        pltpu.make_async_copy(packed_refs[s], out_refs[s], sem.at[s]).start()
+    for s in range(n_slots):
+        pltpu.make_async_copy(packed_refs[s], out_refs[s], sem.at[s]).wait()
 
 
 def pack_ids(me, ids, lengths, n_dev, n_rows, hop_slots):
@@ -79,9 +83,11 @@
         functools.partial(ids_kernel, n_dev, n_rows, hop_slots),
         out_shape=(jax.ShapeDtypeStruct((1, batch + BLOCK), jnp.int32),) * n_slots,
         in_specs=[pl.BlockSpec(memory_space=pltpu.SMEM)] + [pl.BlockSpec(memory_space=pltpu.VMEM)] * 2,
-        out_specs=(pl.BlockSpec(memory_space=pltpu.VMEM),) * n_slots,
-        scratch_shapes=[pltpu.VMEM((n_dev * n_slots, part), jnp.int32)] * 2,
-        compiler_params=pltpu.CompilerParams(vmem_limit_bytes=32000000),
+        out_specs=(pl.BlockSpec(memory_space=pl.ANY),) * n_slots,
+        scratch_shapes=[pltpu.VMEM((1, batch + BLOCK), jnp.int32)] * n_slots
+        + [pltpu.VMEM((n_dev * n_slots, part), jnp.int32)] * 2
+        + [pltpu.SemaphoreType.DMA((n_slots,))],
+        compiler_params=pltpu.CompilerParams(vmem_limit_bytes=VMEM_LIMIT),
         cost_estimate=pl.CostEstimate(flops=20000000, bytes_accessed=2000000, transcendentals=0),
     )(me, ids, lengths)
 
@@ -281,7 +287,7 @@
     grad_refs, refs = refs[:n_grads], refs[n_grads:]
     ids_refs, carried_refs = refs[:n], refs[n:n + n_carried]
     out_tables_ref, out_accums_ref, *scratch = refs[n + n_carried:]
-    banks, (stage, table_v, grad_v, done_v, sem, out_sem, ids_sem, grad_sem), scalars = scratch[:BANKS], scratch[BANKS:BANKS + 8], scratch[BANKS + 8:]
+    banks, (stage, table_v, grad_v, accum_v, done_v, sem, out_sem, ids_sem, grad_sem), scalars = scratch[:BANKS], scratch[BANKS:BANKS + 9], scratch[BANKS + 9:]
     _, segs, seg_rows, dim = grad_v.shape
     part = (ids_refs[0].shape[1] - BLOCK) // segs
     ids_s = [scalars[i * (segs + 1):(i + 1) * (segs + 1)] for i in range(n)]
@@ -302,6 +308,8 @@
             copy.start()
         table_copy.start()
 
+    accum_copy = pltpu.make_async_copy(accums_ref, accum_v, out_sem.at[n + 1])
+    accum_copy.start()
     if n_carried:
         done_copy = pltpu.make_async_copy(carried_refs[1], done_v, out_sem.at[n])
         done_copy.start()
@@ -352,6 +360,8 @@
 
         lax.fori_loop(0, (ids_s[i][segs][0, 0] + UNROLL - 1) // UNROLL, add_rows, 0)
         table_copy.wait()
+        if i == 0:
+            accum_copy.wait()
         if n_carried and i == 0:
             done_copy.wait()
 
@@ -365,7 +375,7 @@
                 if i + 1 < n:
                     for bank in banks:
                         bank[rows, :] = zero
-                old = jnp.where(eye, accums_ref[slot:slot + 1, rows], 0.0)
+                old = jnp.where(eye, accum_v[slot:slot + 1, rows], 0.0)
                 new = jnp.sum(grad * grad * (1.0 / dim) + old, axis=1, keepdims=True)
                 line = jnp.broadcast_to(new[:8], (8, dim))
                 for k in range(1, BLOCK // 8):
@@ -396,8 +406,9 @@
         functools.partial(apply_kernel, slots, len(carried), len(grads)),
         out_shape=tuple(jax.ShapeDtypeStruct(x.shape, x.dtype) for x in (tables, accums)),
         in_specs=[pl.BlockSpec(memory_space=pltpu.SMEM)]
-        + [pl.BlockSpec(memory_space=pl.ANY), pl.BlockSpec(memory_space=pltpu.VMEM)]
-        + [pl.BlockSpec(memory_space=pl.ANY)] * (len(grads) + n)
+        + [pl.BlockSpec(memory_space=pl.ANY)] * 2
+        + [pl.BlockSpec(memory_space=pl.ANY)] * len(grads)
+        + [pl.BlockSpec(memory_space=pl.ANY)] * n
         + [pl.BlockSpec(memory_space=pl.ANY)] * len(carried),
         out_specs=(pl.BlockSpec(memory_space=pl.ANY),) * 2,
         input_output_aliases={3 + len(grads) + n + i: i for i in range(len(carried))},
@@ -407,8 +418,9 @@
             pltpu.VMEM((n, n_rows, dim), tables.dtype),
             pltpu.VMEM((n, segs, seg_rows, dim), grads[0].dtype),
             pltpu.VMEM(accums.shape, accums.dtype),
+            pltpu.VMEM(accums.shape, accums.dtype),
             pltpu.SemaphoreType.DMA((n,)),
-            pltpu.SemaphoreType.DMA((n + 1,)),
+            pltpu.SemaphoreType.DMA((n + 2,)),
             pltpu.SemaphoreType.DMA((n, segs + 1)),
             pltpu.SemaphoreType.DMA((n, segs)),
         ]

time: 219 us -> 219 us (level)
    cond x16 -> x0, local copies, waits for them, and re-layouts: 2.5 us -> none
  transfers between devices with their start and end apart: 10 -> 10, of which waited for: 4 -> 4; matrix products, arithmetic and copies ran while one was open for 1% -> 1% of each run, Pallas kernels for 31% -> 32%
where the time goes in v11:
time: 219 us; the launch traced here: 218 us
  Pallas kernels  103 us (47%)
  waiting for transfers between devices  78.7 us (36%)
  starting transfers between devices  32.4 us (15%)
    pallas_call x4, Pallas kernels, apply_slots(): pl.pallas_call(functools.partial(apply_kernel, slots, len(carried), len(g...  68.6 us
    all_to_all x3, waiting for transfers between devices, run(): got[c] = [lax.all_to_all(pack, 'mp', 0, 0, tiled=True)]  47 us
    ppermute x7, waiting for transfers between devices, run(): lax.ppermute(pack[o], 'mp', routes(n_group, n_slots, n_tab, slots[0], o))  31.7 us
    ppermute x7, starting transfers between devices, run(): lax.ppermute(pack[o], 'mp', routes(n_group, n_slots, n_tab, slots[0], o))  17.3 us
    pallas_call x3, Pallas kernels, pack_slots(): pl.pallas_call(functools.partial(pack_kernel, slots), out_shape=jax.Shape...  15.1 us
    all_to_all x3, starting transfers between devices, run(): got[c] = [lax.all_to_all(pack, 'mp', 0, 0, tiled=True)]  15 us
    pallas_call x1, Pallas kernels, make_plan(): pl.pallas_call(functools.partial(plan_kernel, n_dev, caps), out_shape=(ja...  11.2 us
    pallas_call x1, Pallas kernels, pack_hops(): pl.pallas_call(functools.partial(pack_hops_kernel, slot), out_shape=(jax....  5.58 us
  transfers between devices with their start and end apart: 10, of which 4 were waited for; matrix products, arithmetic and copies ran while one was open for 1% of the time, Pallas kernels for 32%

profile of v11, /device:TPU:81, one launch (start us, length us, event | category | flops | bytes accessed | tf_op | source)
XLA Modules:
  0.0 218.1 jit_solution(1064743283869341921)
XLA Ops:
  0.6 11.2 %shard_map.95 = (s32[8,4,2176]{2,1,0:T(4,128)}, s32[8,4,128]{2,1,0:T(4,128)S(1)}, s32[1]{0:T(128)}) custom-call(s32[4,16384]{1,0:T(4,128)} %lengths_ref.1), custom_call_target="tpu_custom_call" | custom-call | flops 20000000 | bytes 2000000 | tf_op jit(solution)/shard_map/pallas_call | solution.py:151
  12.4 205.5 %conditional.1 = ((bf16[4,16384,128]{2,1,0:T(8,128)(2,1)}, f32[4,16384]{1,0:T(4,128)})) conditional(s32[]{:T(128)} %bitcast.9, (s32[8,4,128]{2,1,0:T(4,128)S(1)}, s32[8,4,2176]{2,1,0:T(4,128)}, bf16[26,2048,128]{2,1,0:T(8,128)(2,1)}, s32[4,16384,1]{1,2,0:T(1,128)}, s32[]{:T(128)}, /*index=5*/s32[4,16384]{1,0:T(4,128)}, f32[]{:T(128)}, ...), branch_computations={%region_0.0_spmd, %region_1.0_spmd, %region_2.0_spmd} | conditional | flops 3543215360 | bytes 147228160 | solution.py:478
  12.4 5.1 %branch_0_fun.13 = bf16[8,1,1120,128]{3,2,1,0:T(8,128)(2,1)} custom-call(s32[8,4,128]{2,1,0:T(4,128)S(1)} %get-tuple-element.57.starts_ref, s32[8,4,2176]{2,1,0:T(4,128)} %get-tuple-element.58.plan_ref, bf16[26,2048,128]{2,1,0:T(8,128)(2,1)} %get-tuple-element.59.tables_ref), custom_call_target="tpu_custom_call" | custom-call | flops 41943040 | bytes 6291456 | tf_op jit(solution)/shard_map/cond/branch_0_fun/pallas_call | solution.py:210
  17.6 4.6 %all-to-all-start.2 = ((bf16[8,1,1120,128]{3,2,1,0:T(8,128)(2,1)}), bf16[8,1,1120,128]{3,2,1,0:T(8,128)(2,1)}, u32[]{:S(2)}, u32[]{:S(2)}) async-start(bf16[8,1,1120,128]{3,2,1,0:T(8,128)(2,1)} %branch_0_fun.13), calls=%async_computation.2 | async-start | bytes 4587520 | tf_op jit(solution)/shard_map/cond/branch_0_fun/all_to_all | solution.py:468
  22.2 5.2 %branch_0_fun.12 = bf16[8,1,1120,128]{3,2,1,0:T(8,128)(2,1)} custom-call(s32[8,4,128]{2,1,0:T(4,128)S(1)} %get-tuple-element.57.starts_ref, s32[8,4,2176]{2,1,0:T(4,128)} %get-tuple-element.58.plan_ref, bf16[26,2048,128]{2,1,0:T(8,128)(2,1)} %get-tuple-element.59.tables_ref), custom_call_target="tpu_custom_call" | custom-call | flops 41943040 | bytes 6291456 | tf_op jit(solution)/shard_map/cond/branch_0_fun/pallas_call | solution.py:210
  27.3 23.3 %all-to-all-done.2.refs_0_ = bf16[8,1,1120,128]{3,2,1,0:T(8,128)(2,1)} async-done(((bf16[8,1,1120,128]{3,2,1,0:T(8,128)(2,1)}), bf16[8,1,1120,128]{3,2,1,0:T(8,128)(2,1)}, u32[]{:S(2)}, u32[]{:S(2)}) %all-to-all-start.2) | async-done | bytes 2293792 | tf_op jit(solution)/shard_map/cond/branch_0_fun/all_to_all | solution.py:468
  50.7 5.2 %all-to-all-start.1 = ((bf16[8,1,1120,128]{3,2,1,0:T(8,128)(2,1)}), bf16[8,1,1120,128]{3,2,1,0:T(8,128)(2,1)}, u32[]{:S(2)}, u32[]{:S(2)}) async-start(bf16[8,1,1120,128]{3,2,1,0:T(8,128)(2,1)} %branch_0_fun.12), calls=%async_computation.1 | async-start | bytes 4587520 | tf_op jit(solution)/shard_map/cond/branch_0_fun/all_to_all | solution.py:468
  55.9 4.8 %branch_0_fun.9 = bf16[8,1,1120,128]{3,2,1,0:T(8,128)(2,1)} custom-call(s32[8,4,128]{2,1,0:T(4,128)S(1)} %get-tuple-element.57.starts_ref, s32[8,4,2176]{2,1,0:T(4,128)} %get-tuple-element.58.plan_ref, bf16[26,2048,128]{2,1,0:T(8,128)(2,1)} %get-tuple-element.59.tables_ref), custom_call_target="tpu_custom_call" | custom-call | flops 41943040 | bytes 6291456 | tf_op jit(solution)/shard_map/cond/branch_0_fun/pallas_call | solution.py:210
  60.7 23.7 %all-to-all-done.1.refs_0_ = bf16[8,1,1120,128]{3,2,1,0:T(8,128)(2,1)} async-done(((bf16[8,1,1120,128]{3,2,1,0:T(8,128)(2,1)}), bf16[8,1,1120,128]{3,2,1,0:T(8,128)(2,1)}, u32[]{:S(2)}, u32[]{:S(2)}) %all-to-all-start.1) | async-done | bytes 2293792 | tf_op jit(solution)/shard_map/cond/branch_0_fun/all_to_all | solution.py:468
  84.4 5.2 %all-to-all-start = ((bf16[8,1,1120,128]{3,2,1,0:T(8,128)(2,1)}), bf16[8,1,1120,128]{3,2,1,0:T(8,128)(2,1)}, u32[]{:S(2)}, u32[]{:S(2)}) async-start(bf16[8,1,1120,128]{3,2,1,0:T(8,128)(2,1)} %branch_0_fun.9), calls=%async_computation | async-start | bytes 4587520 | tf_op jit(solution)/shard_map/cond/branch_0_fun/all_to_all | solution.py:468
  89.6 5.6 %branch_0_fun.11 = (bf16[1120,128]{1,0:T(8,128)(2,1)}, bf16[1120,128]{1,0:T(8,128)(2,1)}, bf16[1120,128]{1,0:T(8,128)(2,1)}, bf16[1120,128]{1,0:T(8,128)(2,1)}, ...) custom-call(s32[1]{0:T(128)} %bitcast.1.me_ref, ...), custom_call_target="tpu_custom_call" | custom-call | flops 41943040 | bytes 6291456 | tf_op jit(solution)/shard_map/cond/branch_0_fun/pallas_call | solution.py:268
  95.2 3.6 %collective-permute-start = (bf16[1120,128]{1,0:T(8,128)(2,1)}, bf16[1120,128]{1,0:T(8,128)(2,1)}, u32[]{:S(2)}, u32[]{:S(2)}) collective-permute-start(bf16[1120,128]{1,0:T(8,128)(2,1)} %get-tuple-element.65), channel_id=1, source_target_pairs={{0,1},{1,2},{2,3},{3,4},{4,5},{7,0},{8,9},{9,10},{10,11},{11,12},{... | collective-permute-start | bytes 860168 | tf_op jit(solution)/shard_map/cond/branch_0_fun/ppermute | solution.py:465
  98.8 3.5 %collective-permute-start.1 = (bf16[1120,128]{1,0:T(8,128)(2,1)}, bf16[1120,128]{1,0:T(8,128)(2,1)}, u32[]{:S(2)}, u32[]{:S(2)}) collective-permute-start(bf16[1120,128]{1,0:T(8,128)(2,1)} %get-tuple-element.66), channel_id=1, source_target_pairs={{0,2},{1,3},{2,4},{3,5},{6,0},{7,1},{8,10},{9,11},{10,12},{11,13},... | collective-permute-start | bytes 860168 | tf_op jit(solution)/shard_map/cond/branch_0_fun/ppermute | solution.py:465
  102.3 2.0 collective-permute-start.2
  104.3 3.8 %collective-permute-start.3 = (bf16[1120,128]{1,0:T(8,128)(2,1)}, bf16[1120,128]{1,0:T(8,128)(2,1)}, u32[]{:S(2)}, u32[]{:S(2)}) collective-permute-start(bf16[1120,128]{1,0:T(8,128)(2,1)} %get-tuple-element.68), channel_id=1, source_target_pairs={{0,4},{1,5},{4,0},{5,1},{6,2},{7,3},{8,12},{9,13},{12,8},{13,9},{1... | collective-permute-start | bytes 860168 | tf_op jit(solution)/shard_map/cond/branch_0_fun/ppermute | solution.py:465
  108.1 1.3 collective-permute-start.4
  109.4 11.5 %collective-permute-done.refs_1_ = bf16[1120,128]{1,0:T(8,128)(2,1)} collective-permute-done((bf16[1120,128]{1,0:T(8,128)(2,1)}, bf16[1120,128]{1,0:T(8,128)(2,1)}, u32[]{:S(2)}, u32[]{:S(2)}) %collective-permute-start) | collective-permute-done | bytes 286752 | tf_op jit(solution)/shard_map/cond/branch_0_fun/ppermute | solution.py:465
  120.9 1.3 collective-permute-start.5
  122.2 20.2 %collective-permute-done.1.refs_2_ = bf16[1120,128]{1,0:T(8,128)(2,1)} collective-permute-done((bf16[1120,128]{1,0:T(8,128)(2,1)}, bf16[1120,128]{1,0:T(8,128)(2,1)}, u32[]{:S(2)}, u32[]{:S(2)}) %collective-permute-start.1) | collective-permute-done | bytes 286752 | tf_op jit(solution)/shard_map/cond/branch_0_fun/ppermute | solution.py:465
  142.4 1.9 collective-permute-start.6
  144.3 1.8 copy.50
  146.2 2.8 %branch_0_fun.10 = (s32[1,16512]{1,0:T(1,128)}, s32[1,16512]{1,0:T(1,128)}, s32[1,16512]{1,0:T(1,128)}, s32[1,16512]{1,0:T(1,128)}) custom-call(s32[1]{0:T(128)} %bitcast.1.me_ref, s32[4,16384]{1,0:T(4,128)} %bitcast.20, s32[4,16384]{1,0:T(4,128)} %get-tuple-element.62.lengths_ref), custom_call_target="tpu_custom_call" | custom-call | flops 20000000 | bytes 2000000 | tf_op jit(solution)/shard_map/cond/branch_0_fun/pallas_call | solution.py:82
  149.0 17.0 %branch_0_fun.14 = (bf16[4,16384,128]{2,1,0:T(8,128)(2,1)}, f32[4,16384]{1,0:T(4,128)}) custom-call(f32[1]{0:T(128)} %bitcast.lr_ref, bf16[4,16384,128]{2,1,0:T(8,128)(2,1)} %get-tuple-element.172.tables_ref, f32[4,16384]{1,0:T(4,128)} %get-tuple-element.175.accums_ref, bf16[8,1,1120,128]{3,2,1,0:T(8,128)(2,1)} %all-to-all-done.2.refs_0_, ...), custom_call_target="tpu_custom_call" | custom-call | flops 838860800 | bytes 16777216 | tf_op jit(solution)/shard_map/cond/branch_0_fun/pallas_call | solution.py:405
  165.9 17.2 %branch_0_fun.15 = (bf16[4,16384,128]{2,1,0:T(8,128)(2,1)}, f32[4,16384]{1,0:T(4,128)}) custom-call(f32[1]{0:T(128)} %bitcast.lr_ref, bf16[4,16384,128]{2,1,0:T(8,128)(2,1)} %get-tuple-element.172.tables_ref, f32[4,16384]{1,0:T(4,128)} %get-tuple-element.175.accums_ref, ...), custom_call_target="tpu_custom_call", output_to_operand_aliasing={{0}: (5, {}), {1}: (6, {})} | custom-call | flops 838860800 | bytes 16777216 | tf_op jit(solution)/shard_map/cond/branch_0_fun/pallas_call | solution.py:405
  183.2 0.0 collective-permute-done.2.refs_3_
  183.2 0.0 collective-permute-done.3.refs_4_
  183.2 0.0 collective-permute-done.4.refs_5_
  183.2 0.0 collective-permute-done.5.refs_6_
  183.2 0.0 collective-permute-done.6.refs_7_
  183.2 17.1 %branch_0_fun.16 = (bf16[4,16384,128]{2,1,0:T(8,128)(2,1)}, f32[4,16384]{1,0:T(4,128)}) custom-call(f32[1]{0:T(128)} %bitcast.lr_ref, bf16[4,16384,128]{2,1,0:T(8,128)(2,1)} %get-tuple-element.172.tables_ref, f32[4,16384]{1,0:T(4,128)} %get-tuple-element.175.accums_ref, ...), custom_call_target="tpu_custom_call", output_to_operand_aliasing={{0}: (12, {}), {1}: (13, {})} | custom-call | flops 838860800 | bytes 16777216 | tf_op jit(solution)/shard_map/cond/branch_0_fun/pallas_call | solution.py:405
  200.3 0.0 all-to-all-done.refs_0_
  200.3 17.3 %branch_0_fun.17 = (bf16[4,16384,128]{2,1,0:T(8,128)(2,1)}, f32[4,16384]{1,0:T(4,128)}) custom-call(f32[1]{0:T(128)} %bitcast.lr_ref, bf16[4,16384,128]{2,1,0:T(8,128)(2,1)} %get-tuple-element.172.tables_ref, f32[4,16384]{1,0:T(4,128)} %get-tuple-element.175.accums_ref, ...), custom_call_target="tpu_custom_call", output_to_operand_aliasing={{0}: (5, {}), {1}: (6, {})} | custom-call | flops 838860800 | bytes 16777216 | tf_op jit(solution)/shard_map/cond/branch_0_fun/pallas_call | solution.py:405
Async XLA Ops:
  17.6 33.1 %all-to-all-start.2 = ((bf16[8,1,1120,128]{3,2,1,0:T(8,128)(2,1)}), bf16[8,1,1120,128]{3,2,1,0:T(8,128)(2,1)}, u32[]{:S(2)}, u32[]{:S(2)}) async-start(bf16[8,1,1120,128]{3,2,1,0:T(8,128)(2,1)} %branch_0_fun.13), calls=%async_computation.2 | async-start | bytes 4587520 | tf_op jit(solution)/shard_map/cond/branch_0_fun/all_to_all | solution.py:468
  50.7 33.7 %all-to-all-start.1 = ((bf16[8,1,1120,128]{3,2,1,0:T(8,128)(2,1)}), bf16[8,1,1120,128]{3,2,1,0:T(8,128)(2,1)}, u32[]{:S(2)}, u32[]{:S(2)}) async-start(bf16[8,1,1120,128]{3,2,1,0:T(8,128)(2,1)} %branch_0_fun.12), calls=%async_computation.1 | async-start | bytes 4587520 | tf_op jit(solution)/shard_map/cond/branch_0_fun/all_to_all | solution.py:468
  84.4 115.9 %all-to-all-start = ((bf16[8,1,1120,128]{3,2,1,0:T(8,128)(2,1)}), bf16[8,1,1120,128]{3,2,1,0:T(8,128)(2,1)}, u32[]{:S(2)}, u32[]{:S(2)}) async-start(bf16[8,1,1120,128]{3,2,1,0:T(8,128)(2,1)} %branch_0_fun.9), calls=%async_computation | async-start | bytes 4587520 | tf_op jit(solution)/shard_map/cond/branch_0_fun/all_to_all | solution.py:468
  95.2 25.7 %collective-permute-start = (bf16[1120,128]{1,0:T(8,128)(2,1)}, bf16[1120,128]{1,0:T(8,128)(2,1)}, u32[]{:S(2)}, u32[]{:S(2)}) collective-permute-start(bf16[1120,128]{1,0:T(8,128)(2,1)} %get-tuple-element.65), channel_id=1, source_target_pairs={{0,1},{1,2},{2,3},{3,4},{4,5},{7,0},{8,9},{9,10},{10,11},{11,12},{... | collective-permute-start | bytes 860168 | tf_op jit(solution)/shard_map/cond/branch_0_fun/ppermute | solution.py:465
  98.8 43.5 %collective-permute-start.1 = (bf16[1120,128]{1,0:T(8,128)(2,1)}, bf16[1120,128]{1,0:T(8,128)(2,1)}, u32[]{:S(2)}, u32[]{:S(2)}) collective-permute-start(bf16[1120,128]{1,0:T(8,128)(2,1)} %get-tuple-element.66), channel_id=1, source_target_pairs={{0,2},{1,3},{2,4},{3,5},{6,0},{7,1},{8,10},{9,11},{10,12},{11,13},... | collective-permute-start | bytes 860168 | tf_op jit(solution)/shard_map/cond/branch_0_fun/ppermute | solution.py:465
  102.3 80.9 %collective-permute-start.2 = (bf16[1120,128]{1,0:T(8,128)(2,1)}, bf16[1120,128]{1,0:T(8,128)(2,1)}, u32[]{:S(2)}, u32[]{:S(2)}) collective-permute-start(bf16[1120,128]{1,0:T(8,128)(2,1)} %get-tuple-element.67), channel_id=1, source_target_pairs={{0,3},{1,4},{2,5},{5,0},{6,1},{7,2},{8,11},{9,12},{10,13},{13,8},{... | collective-permute-start | bytes 860168 | tf_op jit(solution)/shard_map/cond/branch_0_fun/ppermute | solution.py:465
  104.3 78.9 %collective-permute-start.3 = (bf16[1120,128]{1,0:T(8,128)(2,1)}, bf16[1120,128]{1,0:T(8,128)(2,1)}, u32[]{:S(2)}, u32[]{:S(2)}) collective-permute-start(bf16[1120,128]{1,0:T(8,128)(2,1)} %get-tuple-element.68), channel_id=1, source_target_pairs={{0,4},{1,5},{4,0},{5,1},{6,2},{7,3},{8,12},{9,13},{12,8},{13,9},{1... | collective-permute-start | bytes 860168 | tf_op jit(solution)/shard_map/cond/branch_0_fun/ppermute | solution.py:465
  108.1 75.1 %collective-permute-start.4 = (bf16[1120,128]{1,0:T(8,128)(2,1)}, bf16[1120,128]{1,0:T(8,128)(2,1)}, u32[]{:S(2)}, u32[]{:S(2)}) collective-permute-start(bf16[1120,128]{1,0:T(8,128)(2,1)} %get-tuple-element.69), channel_id=1, source_target_pairs={{0,5},{3,0},{4,1},{5,2},{6,3},{7,4},{8,13},{11,8},{12,9},{13,10},{... | collective-permute-start | bytes 860168 | tf_op jit(solution)/shard_map/cond/branch_0_fun/ppermute | solution.py:465
  120.9 62.3 %collective-permute-start.5 = (bf16[1120,128]{1,0:T(8,128)(2,1)}, bf16[1120,128]{1,0:T(8,128)(2,1)}, u32[]{:S(2)}, u32[]{:S(2)}) collective-permute-start(bf16[1120,128]{1,0:T(8,128)(2,1)} %get-tuple-element.70), channel_id=1, source_target_pairs={{2,0},{3,1},{4,2},{5,3},{6,4},{7,5},{10,8},{11,9},{12,10},{13,11},... | collective-permute-start | bytes 860168 | tf_op jit(solution)/shard_map/cond/branch_0_fun/ppermute | solution.py:465
  142.4 40.8 %collective-permute-start.6 = (bf16[1120,128]{1,0:T(8,128)(2,1)}, bf16[1120,128]{1,0:T(8,128)(2,1)}, u32[]{:S(2)}, u32[]{:S(2)}) collective-permute-start(bf16[1120,128]{1,0:T(8,128)(2,1)} %get-tuple-element.71), channel_id=1, source_target_pairs={{1,0},{2,1},{3,2},{4,3},{5,4},{6,5},{9,8},{10,9},{11,10},{12,11},{... | collective-permute-start | bytes 860168 | tf_op jit(solution)/shard_map/cond/branch_0_fun/ppermute | solution.py:465

commit v12 on v10

--- a/solution.py
+++ b/solution.py
@@ -17,6 +17,7 @@
 CLEAR = 512
 MAX_LANE = 64
 VMEM_LIMIT = 66000000
+APPLY_VMEM = 66600000
 
 
 def gather_parts(src_ref, dst, n_dev):
@@ -63,8 +64,9 @@
         step *= 2
     spot = lax.broadcasted_iota(jnp.int32, (rows, part), 1)
     ids_v[...] = jnp.where(spot < count, move & 0xFFFF, n_rows)
-    most = jnp.max(count, axis=0, keepdims=True)
+    slot_of = lax.broadcasted_iota(jnp.int32, (rows, 1), 0) % n_slots
     for s in range(n_slots):
+        most = jnp.max(jnp.where(slot_of == s, count, 0), axis=0, keepdims=True)
         for d in range(n_dev):
             sender = (me_ref[0] + (n_dev - d)) % n_dev if s in hop_slots else d
             packed_refs[s][:, d * part:(d + 1) * part] = ids_v[pl.ds(sender * n_slots + s, 1), :]
@@ -413,7 +415,7 @@
             pltpu.SemaphoreType.DMA((n, segs)),
         ]
         + ([pltpu.SMEM((1, part), jnp.int32)] * segs + [pltpu.SMEM((1, BLOCK), jnp.int32)]) * n,
-        compiler_params=pltpu.CompilerParams(vmem_limit_bytes=VMEM_LIMIT),
+        compiler_params=pltpu.CompilerParams(vmem_limit_bytes=APPLY_VMEM),
         cost_estimate=pl.CostEstimate(flops=n * n_rows * dim * 400, bytes_accessed=4 * n * n_rows * dim * 2, transcendentals=0),
     )(lr, tables, accums, *grads, *(ids[k] for k in slots), *carried)
 

time: 219 us -> 218 us (level)
  no operation moved by 1% of the time
where the time goes in v12:
time: 218 us
  Pallas kernels  101 us (46%)
  waiting for transfers between devices  79.1 us (36%)
  starting transfers between devices  32.4 us (15%)
  local copies, waits for them, and re-layouts  3.62 us (2%)
    pallas_call x4, Pallas kernels, apply_slots(): pl.pallas_call(functools.partial(apply_kernel, slots, len(carried), len(g...  68.5 us
    all_to_all x3, waiting for transfers between devices, run(): got[c] = [lax.all_to_all(pack, 'mp', 0, 0, tiled=True)]  47.4 us
    ppermute x7, waiting for transfers between devices, run(): lax.ppermute(pack[o], 'mp', routes(n_group, n_slots, n_tab, slots[0], o))  31.8 us
    ppermute x7, starting transfers between devices, run(): lax.ppermute(pack[o], 'mp', routes(n_group, n_slots, n_tab, slots[0], o))  17.3 us
    all_to_all x3, starting transfers between devices, run(): got[c] = [lax.all_to_all(pack, 'mp', 0, 0, tiled=True)]  15.1 us
    pallas_call x3, Pallas kernels, pack_slots(): pl.pallas_call(functools.partial(pack_kernel, slots), out_shape=jax.Shape...  14.7 us
    pallas_call x1, Pallas kernels, make_plan(): pl.pallas_call(functools.partial(plan_kernel, n_dev, caps), out_shape=(ja...  11.2 us
    pallas_call x1, Pallas kernels, pack_hops(): pl.pallas_call(functools.partial(pack_hops_kernel, slot), out_shape=(jax....  5.4 us
  transfers between devices with their start and end apart: 10, of which 4 were waited for; matrix products, arithmetic and copies ran while one was open for 1% of the time, Pallas kernels for 31%

profile of v12, /device:TPU:81, one launch (start us, length us, event | category | flops | bytes accessed | tf_op | source)
XLA Modules:
  0.0 217.8 jit_solution(11930103259011273098)
XLA Ops:
  0.6 11.2 %shard_map.95 = (s32[8,4,2176]{2,1,0:T(4,128)S(1)}, s32[8,4,128]{2,1,0:T(4,128)S(1)}, s32[1]{0:T(128)}) custom-call(s32[4,16384]{1,0:T(4,128)} %lengths_ref.1), custom_call_target="tpu_custom_call" | custom-call | flops 20000000 | bytes 2000000 | tf_op jit(solution)/shard_map/pallas_call | solution.py:147
  12.4 205.2 %conditional.1 = ((bf16[4,16384,128]{2,1,0:T(8,128)(2,1)}, f32[4,16384]{1,0:T(4,128)})) conditional(s32[]{:T(128)} %bitcast.9, (s32[8,4,128]{2,1,0:T(4,128)S(1)}, s32[8,4,2176]{2,1,0:T(4,128)S(1)}, bf16[26,2048,128]{2,1,0:T(8,128)(2,1)}, s32[4,16384,1]{1,2,0:T(1,128)}, s32[]{:T(128)}, /*index=5*/s32[4,16384]{1,0:T(4,128)}, ...), branch_computations={%region_0.0_spmd, %region_1.0_spmd, %region_2.0_spmd} | conditional | flops 3543215360 | bytes 154576608 | solution.py:468
  12.4 5.0 %branch_0_fun.13 = bf16[8,1,1120,128]{3,2,1,0:T(8,128)(2,1)} custom-call(s32[8,4,128]{2,1,0:T(4,128)S(1)} %get-tuple-element.57.starts_ref, s32[8,4,2176]{2,1,0:T(4,128)S(1)} %get-tuple-element.58.plan_ref, bf16[26,2048,128]{2,1,0:T(8,128)(2,1)} %get-tuple-element.59.tables_ref), custom_call_target="tpu_custom_call" | custom-call | flops 41943040 | bytes 6291456 | tf_op jit(solution)/shard_map/cond/branch_0_fun/pallas_call | solution.py:206
  17.4 4.6 %all-to-all-start.2 = ((bf16[8,1,1120,128]{3,2,1,0:T(8,128)(2,1)}), bf16[8,1,1120,128]{3,2,1,0:T(8,128)(2,1)}, u32[]{:S(2)}, u32[]{:S(2)}) async-start(bf16[8,1,1120,128]{3,2,1,0:T(8,128)(2,1)} %branch_0_fun.13), calls=%async_computation.2 | async-start | bytes 4587520 | tf_op jit(solution)/shard_map/cond/branch_0_fun/all_to_all | solution.py:458
  22.0 5.0 %branch_0_fun.12 = bf16[8,1,1120,128]{3,2,1,0:T(8,128)(2,1)} custom-call(s32[8,4,128]{2,1,0:T(4,128)S(1)} %get-tuple-element.57.starts_ref, s32[8,4,2176]{2,1,0:T(4,128)S(1)} %get-tuple-element.58.plan_ref, bf16[26,2048,128]{2,1,0:T(8,128)(2,1)} %get-tuple-element.59.tables_ref), custom_call_target="tpu_custom_call" | custom-call | flops 41943040 | bytes 6291456 | tf_op jit(solution)/shard_map/cond/branch_0_fun/pallas_call | solution.py:206
  27.0 23.5 %all-to-all-done.2.refs_0_ = bf16[8,1,1120,128]{3,2,1,0:T(8,128)(2,1)} async-done(((bf16[8,1,1120,128]{3,2,1,0:T(8,128)(2,1)}), bf16[8,1,1120,128]{3,2,1,0:T(8,128)(2,1)}, u32[]{:S(2)}, u32[]{:S(2)}) %all-to-all-start.2) | async-done | bytes 2293792 | tf_op jit(solution)/shard_map/cond/branch_0_fun/all_to_all | solution.py:458
  50.5 5.2 %all-to-all-start.1 = ((bf16[8,1,1120,128]{3,2,1,0:T(8,128)(2,1)}), bf16[8,1,1120,128]{3,2,1,0:T(8,128)(2,1)}, u32[]{:S(2)}, u32[]{:S(2)}) async-start(bf16[8,1,1120,128]{3,2,1,0:T(8,128)(2,1)} %branch_0_fun.12), calls=%async_computation.1 | async-start | bytes 4587520 | tf_op jit(solution)/shard_map/cond/branch_0_fun/all_to_all | solution.py:458
  55.8 4.7 %branch_0_fun.9 = bf16[8,1,1120,128]{3,2,1,0:T(8,128)(2,1)} custom-call(s32[8,4,128]{2,1,0:T(4,128)S(1)} %get-tuple-element.57.starts_ref, s32[8,4,2176]{2,1,0:T(4,128)S(1)} %get-tuple-element.58.plan_ref, bf16[26,2048,128]{2,1,0:T(8,128)(2,1)} %get-tuple-element.59.tables_ref), custom_call_target="tpu_custom_call" | custom-call | flops 41943040 | bytes 6291456 | tf_op jit(solution)/shard_map/cond/branch_0_fun/pallas_call | solution.py:206
  60.4 23.8 %all-to-all-done.1.refs_0_ = bf16[8,1,1120,128]{3,2,1,0:T(8,128)(2,1)} async-done(((bf16[8,1,1120,128]{3,2,1,0:T(8,128)(2,1)}), bf16[8,1,1120,128]{3,2,1,0:T(8,128)(2,1)}, u32[]{:S(2)}, u32[]{:S(2)}) %all-to-all-start.1) | async-done | bytes 2293792 | tf_op jit(solution)/shard_map/cond/branch_0_fun/all_to_all | solution.py:458
  84.3 5.2 %all-to-all-start = ((bf16[8,1,1120,128]{3,2,1,0:T(8,128)(2,1)}), bf16[8,1,1120,128]{3,2,1,0:T(8,128)(2,1)}, u32[]{:S(2)}, u32[]{:S(2)}) async-start(bf16[8,1,1120,128]{3,2,1,0:T(8,128)(2,1)} %branch_0_fun.9), calls=%async_computation | async-start | bytes 4587520 | tf_op jit(solution)/shard_map/cond/branch_0_fun/all_to_all | solution.py:458
  89.5 0.0 copy-start.15
  89.5 0.0 copy-start.12
  89.5 5.4 %branch_0_fun.11 = (bf16[1120,128]{1,0:T(8,128)(2,1)}, bf16[1120,128]{1,0:T(8,128)(2,1)}, bf16[1120,128]{1,0:T(8,128)(2,1)}, bf16[1120,128]{1,0:T(8,128)(2,1)}, ...) custom-call(s32[1]{0:T(128)} %bitcast.1.me_ref, ...), custom_call_target="tpu_custom_call" | custom-call | flops 41943040 | bytes 6291456 | tf_op jit(solution)/shard_map/cond/branch_0_fun/pallas_call | solution.py:264
  94.9 3.6 %collective-permute-start = (bf16[1120,128]{1,0:T(8,128)(2,1)}, bf16[1120,128]{1,0:T(8,128)(2,1)S(1)}, u32[]{:S(2)}, u32[]{:S(2)}) collective-permute-start(bf16[1120,128]{1,0:T(8,128)(2,1)} %get-tuple-element.65), channel_id=1, source_target_pairs={{0,1},{1,2},{2,3},{3,4},{4,5},{7,0},{8,9},{9,10},{10,11},{11,12},{... | collective-permute-start | bytes 860168 | tf_op jit(solution)/shard_map/cond/branch_0_fun/ppermute | solution.py:455
  98.5 3.5 %collective-permute-start.1 = (bf16[1120,128]{1,0:T(8,128)(2,1)}, bf16[1120,128]{1,0:T(8,128)(2,1)S(1)}, u32[]{:S(2)}, u32[]{:S(2)}) collective-permute-start(bf16[1120,128]{1,0:T(8,128)(2,1)} %get-tuple-element.66), channel_id=1, source_target_pairs={{0,2},{1,3},{2,4},{3,5},{6,0},{7,1},{8,10},{9,11},{10,12},{11,13},... | collective-permute-start | bytes 860168 | tf_op jit(solution)/shard_map/cond/branch_0_fun/ppermute | solution.py:455
  102.0 2.0 collective-permute-start.2
  104.0 3.8 %collective-permute-start.3 = (bf16[1120,128]{1,0:T(8,128)(2,1)}, bf16[1120,128]{1,0:T(8,128)(2,1)}, u32[]{:S(2)}, u32[]{:S(2)}) collective-permute-start(bf16[1120,128]{1,0:T(8,128)(2,1)} %get-tuple-element.68), channel_id=1, source_target_pairs={{0,4},{1,5},{4,0},{5,1},{6,2},{7,3},{8,12},{9,13},{12,8},{13,9},{1... | collective-permute-start | bytes 860168 | tf_op jit(solution)/shard_map/cond/branch_0_fun/ppermute | solution.py:455
  107.7 1.3 collective-permute-start.4
  109.1 11.7 %collective-permute-done.refs_1_ = bf16[1120,128]{1,0:T(8,128)(2,1)S(1)} collective-permute-done((bf16[1120,128]{1,0:T(8,128)(2,1)}, bf16[1120,128]{1,0:T(8,128)(2,1)S(1)}, u32[]{:S(2)}, u32[]{:S(2)}) %collective-permute-start) | collective-permute-done | bytes 286752 | tf_op jit(solution)/shard_map/cond/branch_0_fun/ppermute | solution.py:455
  120.7 0.0 copy-start.22
  120.7 1.3 collective-permute-start.5
  122.0 20.1 %collective-permute-done.1.refs_2_ = bf16[1120,128]{1,0:T(8,128)(2,1)S(1)} collective-permute-done((bf16[1120,128]{1,0:T(8,128)(2,1)}, bf16[1120,128]{1,0:T(8,128)(2,1)S(1)}, u32[]{:S(2)}, u32[]{:S(2)}) %collective-permute-start.1) | collective-permute-done | bytes 286752 | tf_op jit(solution)/shard_map/cond/branch_0_fun/ppermute | solution.py:455
  142.1 0.0 copy-start.23
  142.1 1.9 collective-permute-start.6
  144.1 0.0 copy-done.22
  144.1 0.0 copy-done.23
  144.1 1.1 copy.50
  145.2 0.0 copy-done.15
  145.2 1.1 branch_0_fun.10
  146.3 0.0 copy-start
  146.3 0.6 copy-done
  147.0 0.0 copy-start.3
  147.0 0.6 copy-done.3
  147.6 0.0 copy-start.6
  147.6 0.6 copy-done.6
  148.2 0.0 copy-start.9
  148.2 0.6 copy-done.9
  148.8 0.0 copy-done.12
  148.8 16.9 %branch_0_fun.14 = (bf16[4,16384,128]{2,1,0:T(8,128)(2,1)}, f32[4,16384]{1,0:T(4,128)}) custom-call(f32[1]{0:T(128)} %bitcast.lr_ref, bf16[4,16384,128]{2,1,0:T(8,128)(2,1)} %get-tuple-element.172.tables_ref, f32[4,16384]{1,0:T(4,128)S(1)} %copy-done.12, bf16[8,1,1120,128]{3,2,1,0:T(8,128)(2,1)} %all-to-all-done.2.refs_0_, s32[1,16512]{1,0:T(1,128)} %copy-done), custom_call_target="tpu_custom_call" | custom-call | flops 838860800 | bytes 16777216 | tf_op jit(solution)/shard_map/cond/branch_0_fun/pallas_call | solution.py:397
  165.8 17.2 %branch_0_fun.15 = (bf16[4,16384,128]{2,1,0:T(8,128)(2,1)}, f32[4,16384]{1,0:T(4,128)}) custom-call(f32[1]{0:T(128)} %bitcast.lr_ref, bf16[4,16384,128]{2,1,0:T(8,128)(2,1)} %get-tuple-element.172.tables_ref, f32[4,16384]{1,0:T(4,128)S(1)} %copy-done.12, ...), custom_call_target="tpu_custom_call", output_to_operand_aliasing={{0}: (5, {}), {1}: (6, {})} | custom-call | flops 838860800 | bytes 16777216 | tf_op jit(solution)/shard_map/cond/branch_0_fun/pallas_call | solution.py:397
  183.0 0.0 collective-permute-done.2.refs_3_
  183.0 0.0 collective-permute-done.3.refs_4_
  183.0 0.0 collective-permute-done.4.refs_5_
  183.0 0.0 collective-permute-done.5.refs_6_
  183.0 0.0 collective-permute-done.6.refs_7_
  183.0 17.1 %branch_0_fun.16 = (bf16[4,16384,128]{2,1,0:T(8,128)(2,1)}, f32[4,16384]{1,0:T(4,128)}) custom-call(f32[1]{0:T(128)} %bitcast.lr_ref, bf16[4,16384,128]{2,1,0:T(8,128)(2,1)} %get-tuple-element.172.tables_ref, f32[4,16384]{1,0:T(4,128)S(1)} %copy-done.12, ...), custom_call_target="tpu_custom_call", output_to_operand_aliasing={{0}: (12, {}), {1}: (13, {})} | custom-call | flops 838860800 | bytes 16777216 | tf_op jit(solution)/shard_map/cond/branch_0_fun/pallas_call | solution.py:397
  200.1 0.0 all-to-all-done.refs_0_
  200.1 17.3 %branch_0_fun.17 = (bf16[4,16384,128]{2,1,0:T(8,128)(2,1)}, f32[4,16384]{1,0:T(4,128)}) custom-call(f32[1]{0:T(128)} %bitcast.lr_ref, bf16[4,16384,128]{2,1,0:T(8,128)(2,1)} %get-tuple-element.172.tables_ref, f32[4,16384]{1,0:T(4,128)S(1)} %copy-done.12, ...), custom_call_target="tpu_custom_call", output_to_operand_aliasing={{0}: (5, {}), {1}: (6, {})} | custom-call | flops 838860800 | bytes 16777216 | tf_op jit(solution)/shard_map/cond/branch_0_fun/pallas_call | solution.py:397
Async XLA Ops:
  17.4 33.1 %all-to-all-start.2 = ((bf16[8,1,1120,128]{3,2,1,0:T(8,128)(2,1)}), bf16[8,1,1120,128]{3,2,1,0:T(8,128)(2,1)}, u32[]{:S(2)}, u32[]{:S(2)}) async-start(bf16[8,1,1120,128]{3,2,1,0:T(8,128)(2,1)} %branch_0_fun.13), calls=%async_computation.2 | async-start | bytes 4587520 | tf_op jit(solution)/shard_map/cond/branch_0_fun/all_to_all | solution.py:458
  50.5 33.7 %all-to-all-start.1 = ((bf16[8,1,1120,128]{3,2,1,0:T(8,128)(2,1)}), bf16[8,1,1120,128]{3,2,1,0:T(8,128)(2,1)}, u32[]{:S(2)}, u32[]{:S(2)}) async-start(bf16[8,1,1120,128]{3,2,1,0:T(8,128)(2,1)} %branch_0_fun.12), calls=%async_computation.1 | async-start | bytes 4587520 | tf_op jit(solution)/shard_map/cond/branch_0_fun/all_to_all | solution.py:458
  84.3 115.8 %all-to-all-start = ((bf16[8,1,1120,128]{3,2,1,0:T(8,128)(2,1)}), bf16[8,1,1120,128]{3,2,1,0:T(8,128)(2,1)}, u32[]{:S(2)}, u32[]{:S(2)}) async-start(bf16[8,1,1120,128]{3,2,1,0:T(8,128)(2,1)} %branch_0_fun.9), calls=%async_computation | async-start | bytes 4587520 | tf_op jit(solution)/shard_map/cond/branch_0_fun/all_to_all | solution.py:458
  89.5 55.7 %copy-start.15 = (s32[4,16384]{1,0:T(4,128)S(1)}, s32[4,16384]{1,0:T(4,128)}, u32[]{:S(2)}) copy-start(s32[4,16384]{1,0:T(4,128)} %get-tuple-element.62.lengths_ref) | copy-start | bytes 786436 | tf_op jit(solution)/shard_map/cond
  89.5 59.3 %copy-start.12 = (f32[4,16384]{1,0:T(4,128)S(1)}, f32[4,16384]{1,0:T(4,128)}, u32[]{:S(2)}) copy-start(f32[4,16384]{1,0:T(4,128)} %get-tuple-element.175.accums_ref) | copy-start | bytes 786436 | tf_op jit(solution)/shard_map/cond
  94.9 25.8 %collective-permute-start = (bf16[1120,128]{1,0:T(8,128)(2,1)}, bf16[1120,128]{1,0:T(8,128)(2,1)S(1)}, u32[]{:S(2)}, u32[]{:S(2)}) collective-permute-start(bf16[1120,128]{1,0:T(8,128)(2,1)} %get-tuple-element.65), channel_id=1, source_target_pairs={{0,1},{1,2},{2,3},{3,4},{4,5},{7,0},{8,9},{9,10},{10,11},{11,12},{... | collective-permute-start | bytes 860168 | tf_op jit(solution)/shard_map/cond/branch_0_fun/ppermute | solution.py:455
  98.5 43.6 %collective-permute-start.1 = (bf16[1120,128]{1,0:T(8,128)(2,1)}, bf16[1120,128]{1,0:T(8,128)(2,1)S(1)}, u32[]{:S(2)}, u32[]{:S(2)}) collective-permute-start(bf16[1120,128]{1,0:T(8,128)(2,1)} %get-tuple-element.66), channel_id=1, source_target_pairs={{0,2},{1,3},{2,4},{3,5},{6,0},{7,1},{8,10},{9,11},{10,12},{11,13},... | collective-permute-start | bytes 860168 | tf_op jit(solution)/shard_map/cond/branch_0_fun/ppermute | solution.py:455
  102.0 81.0 %collective-permute-start.2 = (bf16[1120,128]{1,0:T(8,128)(2,1)}, bf16[1120,128]{1,0:T(8,128)(2,1)}, u32[]{:S(2)}, u32[]{:S(2)}) collective-permute-start(bf16[1120,128]{1,0:T(8,128)(2,1)} %get-tuple-element.67), channel_id=1, source_target_pairs={{0,3},{1,4},{2,5},{5,0},{6,1},{7,2},{8,11},{9,12},{10,13},{13,8},{... | collective-permute-start | bytes 860168 | tf_op jit(solution)/shard_map/cond/branch_0_fun/ppermute | solution.py:455
  104.0 79.0 %collective-permute-start.3 = (bf16[1120,128]{1,0:T(8,128)(2,1)}, bf16[1120,128]{1,0:T(8,128)(2,1)}, u32[]{:S(2)}, u32[]{:S(2)}) collective-permute-start(bf16[1120,128]{1,0:T(8,128)(2,1)} %get-tuple-element.68), channel_id=1, source_target_pairs={{0,4},{1,5},{4,0},{5,1},{6,2},{7,3},{8,12},{9,13},{12,8},{13,9},{1... | collective-permute-start | bytes 860168 | tf_op jit(solution)/shard_map/cond/branch_0_fun/ppermute | solution.py:455
  107.7 75.2 %collective-permute-start.4 = (bf16[1120,128]{1,0:T(8,128)(2,1)}, bf16[1120,128]{1,0:T(8,128)(2,1)}, u32[]{:S(2)}, u32[]{:S(2)}) collective-permute-start(bf16[1120,128]{1,0:T(8,128)(2,1)} %get-tuple-element.69), channel_id=1, source_target_pairs={{0,5},{3,0},{4,1},{5,2},{6,3},{7,4},{8,13},{11,8},{12,9},{13,10},{... | collective-permute-start | bytes 860168 | tf_op jit(solution)/shard_map/cond/branch_0_fun/ppermute | solution.py:455
  120.7 23.4 %copy-start.22 = (bf16[1120,128]{1,0:T(8,128)(2,1)}, bf16[1120,128]{1,0:T(8,128)(2,1)S(1)}, u32[]{:S(2)}) copy-start(bf16[1120,128]{1,0:T(8,128)(2,1)S(1)} %collective-permute-done.refs_1_) | copy-start | bytes 860164 | tf_op jit(solution)/shard_map/cond
  120.7 62.2 %collective-permute-start.5 = (bf16[1120,128]{1,0:T(8,128)(2,1)}, bf16[1120,128]{1,0:T(8,128)(2,1)}, u32[]{:S(2)}, u32[]{:S(2)}) collective-permute-start(bf16[1120,128]{1,0:T(8,128)(2,1)} %get-tuple-element.70), channel_id=1, source_target_pairs={{2,0},{3,1},{4,2},{5,3},{6,4},{7,5},{10,8},{11,9},{12,10},{13,11},... | collective-permute-start | bytes 860168 | tf_op jit(solution)/shard_map/cond/branch_0_fun/ppermute | solution.py:455
  142.1 2.0 copy-start.23
  142.1 40.9 %collective-permute-start.6 = (bf16[1120,128]{1,0:T(8,128)(2,1)}, bf16[1120,128]{1,0:T(8,128)(2,1)}, u32[]{:S(2)}, u32[]{:S(2)}) collective-permute-start(bf16[1120,128]{1,0:T(8,128)(2,1)} %get-tuple-element.71), channel_id=1, source_target_pairs={{1,0},{2,1},{3,2},{4,3},{5,4},{6,5},{9,8},{10,9},{11,10},{12,11},{... | collective-permute-start | bytes 860168 | tf_op jit(solution)/shard_map/cond/branch_0_fun/ppermute | solution.py:455
  146.3 0.6 copy-start
  147.0 0.6 copy-start.3
  147.6 0.6 copy-start.6
  148.2 0.6 copy-start.9
